TPU v7x, 128 devices: a whole 4x4x4 slice. The times are simulated.
128 devices in a mesh: rows: 16 (over z_hi, x, core), cols: 8 (over y, z_lo).
Axes of the slice: x: 4, y: 4, z: 4 (z_hi: 2, z_lo: 2; z = z_hi * 2 + z_lo), core: 2. Of those that a mesh axis runs over, the one named last changes fastest.
Arguments:
- block_values: bfloat16 [65536, 128], P(('rows', 'cols')), may hold values from -6 to 6
- block_length: int32 [65536], P(('rows', 'cols')), may hold values from 1 to 128
- block_owner: int32 [65536], P(('rows', 'cols')), may hold values from 0 to 16383, as said below
- block_second: int32 [65536], P(('rows', 'cols')), may hold values from 0 to 16383, as said below
- block_third: int32 [65536, 128], P(('rows', 'cols')), may hold values from 0 to 32767
- live_blocks: int32 [128], P(('rows', 'cols')), may hold values from 1 to 512, as said below
- second_factor: bfloat16 [16384, 256], P('cols', 'rows')
- third_factor: bfloat16 [32768, 256], P('cols', 'rows'), may hold values from -6 to 6
Outputs:
- first_factor: float32 [16384, 256], P('cols', 'rows')
Inputs may be any that keep to these rules, and one draw needn't show every extreme that they name: `block_owner`: slot b lies on device d = b // 512 with index r along rows; its row lies in r * 16384 // 16 up to (r + 1) * 16384 // 16 - 1, the device's mode-1 slab. `block_second`: slot b lies on device d = b // 512 with index c along cols; its row lies in c * 16384 // 8 up to (c + 1) * 16384 // 8 - 1. `live_blocks`: some device uses all 512 slots in every draw.
All inputs are finite; a program needn't handle non-finite values.
Results may differ from a plain program's by a relative error of at most 0.0003.
Values may be sent and summed in bfloat16 or wider, within the bound.
No kernel may reach another device: no remote copies, remote signals or barrier semaphores. Data moves between devices by JAX's collectives and lax.ppermute only.
A program may use at most 128 MiB of HBM per device.

v0:
```python
import jax
import jax.numpy as jnp
from jax import lax
from jax.sharding import PartitionSpec as P

I_DEV = 128


def joined_along(blocks, dim):
    shape = list(blocks.shape[1:])
    shape[dim] *= blocks.shape[0]
    return jnp.moveaxis(blocks, 0, dim).reshape(shape)


def from_everyone(value, axis):
    size = lax.axis_size(axis)
    return lax.all_to_all(
        jnp.broadcast_to(value[None], (size, *value.shape)), axis, 0, 0, tiled=True
    )


def collect(value, axis, dim):
    return joined_along(from_everyone(value, axis), dim)


def gram_product(left, right):
    contract = (((0,), (0,)), ((), ()))
    return lax.dot_general(left, right, contract, preferred_element_type=jnp.float32)


def block_fold(values, third, table):
    group = values.shape[0]
    width = values.shape[1]
    picked = table[third.reshape(group * width)]
    scaled = values.reshape(group * width, 1).astype(jnp.float32) * picked.astype(jnp.float32)
    return jnp.sum(scaled.reshape(group, width, picked.shape[1]), axis=1)


def per_device(
    block_values,
    block_length,
    block_owner,
    block_second,
    block_third,
    live_blocks,
    second_factor,
    third_factor,
):
    n_rows = lax.axis_size("rows")
    n_cols = lax.axis_size("cols")
    row_at = lax.axis_index("rows")
    col_at = lax.axis_index("cols")
    contract = (((0,), (0,)), ((), ()))
    width = block_values.shape[1]
    lane = jnp.arange(width, dtype=jnp.int32)
    slab = I_DEV * n_cols
    owned = jnp.arange(slab, dtype=jnp.int32)
    second_range = lax.all_gather(second_factor, "rows", axis=1, tiled=True)
    third_part = collect(third_factor, "cols", 0)
    third_whole = lax.all_gather(third_part, "rows", axis=1, tiled=True)
    range_rows = second_range.shape[0]
    local_gram = gram_product(second_range, second_range)
    gram_second = lax.psum(local_gram, "cols") / (range_rows * n_cols)
    gram_third = gram_product(third_whole, third_whole) / third_whole.shape[0]
    gram = gram_second * gram_third
    nblk = block_values.shape[0]
    group = min(nblk, 128)
    count = live_blocks[0]

    def accumulate(step, total):
        start = step * group
        values = lax.dynamic_slice_in_dim(block_values, start, group, 0)
        lengths = lax.dynamic_slice_in_dim(block_length, start, group, 0)
        third = lax.dynamic_slice_in_dim(block_third, start, group, 0)
        second = lax.dynamic_slice_in_dim(block_second, start, group, 0)
        owner = lax.dynamic_slice_in_dim(block_owner, start, group, 0)
        slot = start + jnp.arange(group, dtype=jnp.int32)
        live = (lane[None, :] < lengths[:, None]) & (slot < count)[:, None]
        values = jnp.where(live, values, jnp.zeros((), jnp.bfloat16))
        fold = block_fold(values, third, third_whole)
        contrib = second_range[second - col_at * range_rows].astype(jnp.float32) * fold
        onehot = ((owner - row_at * slab)[:, None] == owned[None, :]).astype(jnp.float32)
        return total + lax.dot_general(
            onehot,
            contrib,
            contract,
            precision=lax.Precision.HIGHEST,
            preferred_element_type=jnp.float32,
        )

    start_total = jnp.zeros((slab, gram.shape[0]), jnp.float32)
    partial_rows = lax.fori_loop(0, nblk // group, accumulate, start_total)
    mine = lax.psum_scatter(partial_rows, "cols", scatter_dimension=0, tiled=True)
    factor = jnp.linalg.cholesky(gram)
    solved = jax.scipy.linalg.cho_solve((factor, True), mine.T).T
    moved = lax.all_to_all(
        lax.all_to_all(solved, "rows", split_axis=1, concat_axis=0, tiled=True),
        "cols",
        split_axis=0,
        concat_axis=0,
        tiled=True,
    )
    share = n_rows // n_cols
    owned_rows = mine.shape[0]
    reordered = moved.reshape(n_cols, share, owned_rows, moved.shape[1]).transpose(1, 0, 2, 3)
    return reordered.reshape(n_rows * owned_rows, moved.shape[1])


def solution(mesh):
    return jax.shard_map(
        per_device,
        mesh=mesh,
        in_specs=(
            P(("rows", "cols"), None),
            P(("rows", "cols")),
            P(("rows", "cols")),
            P(("rows", "cols")),
            P(("rows", "cols"), None),
            P(("rows", "cols")),
            P("cols", "rows"),
            P("cols", "rows"),
        ),
        out_specs=P("cols", "rows"),
        check_vma=False,
    )
```

profile of v0, /device:TPU:0, one launch (start us, length us, event | category | flops | bytes accessed | tf_op | source)
XLA Modules:
  0.0 622.8 jit_solution(15795296984549790997)
XLA Ops:
  7.3 1.0 broadcast_in_dim.48
  8.3 21.1 %all_to_all.30 = bf16[8,4096,16]{1,2,0:T(8,128)(2,1)S(1)} all-to-all(bf16[8,4096,16]{1,2,0:T(8,128)(2,1)S(1)} %broadcast_in_dim.48), channel_id=1, replica_groups=mesh['rows'=16,'cols'=8] {'cols'}, dimensions={0} | all-to-all | bytes 2097152 | tf_op jit(solution)/shard_map/all_to_all | solution.py:17
  29.4 1.1 copy.51
  30.6 28.7 %all-gather.3.cloned.1.call-done = bf16[2048,256]{0,1:T(8,128)(2,1)} async-done(((bf16[2048,16]{0,1:T(8,128)(2,1)}), bf16[2048,256]{0,1:T(8,128)(2,1)}) %all-gather.3.cloned.1.call-update) | async-done | bytes 1048592 | tf_op jit(solution)/shard_map/all_gather | solution.py:58
  59.3 2.8 fusion.24
  62.1 1.5 copy.43
  63.6 106.5 %all-gather.5.cloned.1.call-done = bf16[32768,256]{0,1:T(8,128)(2,1)} async-done(((bf16[32768,16]{0,1:T(8,128)(2,1)}), bf16[32768,256]{0,1:T(8,128)(2,1)}) %all-gather.5.cloned.1.call-update) | async-done | bytes 16777232 | tf_op jit(solution)/shard_map/all_gather | solution.py:60
  170.2 22.4 %copy.44 = bf16[32768,256]{1,0:T(8,128)(2,1)} copy(bf16[32768,256]{0,1:T(8,128)(2,1)} %all-gather.5.cloned.1.call-done) | data formatting | bytes 33554432
  192.6 321.0 %while.18 = (s32[]{:T(128)}, f32[1024,256]{1,0:T(8,128)S(1)}, s32[512]{0:T(512)}, s32[]{:T(128)}, s32[512]{0:T(512)}, /*index=5*/s32[]{:T(128)}, bf16[2048,256]{...) while((s32[]{:T(128)}, f32[1024,256]{1,0:T(8,128)S(1)}, ...), condition=%wide.region_7.8_spmd.clone, body=%wide.region_5.7_spmd.clone.sunk | while | flops 416057216 | bytes 28354028 | solution.py:92
  194.0 0.9 fusion.42
  194.8 0.9 constant_dynamic-slice_fusion.5
  195.8 68.7 %gather_fusion = bf16[16384,256]{1,0:T(8,128)(2,1)} fusion(bf16[32768,256]{1,0:T(8,128)(2,1)} %get-tuple-element.593, s32[16384]{0:T(1024)S(1)} %broadcast_clamp_fusion.2), kind=kCustom, calls=%fused_computation.1.clone.clone.1 | custom fusion | bytes 16842752 | tf_op jit(solution)/shard_map/while/body/eval_jaxpr/gather | solution.py:34
  264.5 5.5 fusion.43
  269.9 0.8 compare_select_fusion.4
  270.7 0.8 gather_fusion.1
  271.6 1.2 convolution_add_fusion.2
  274.2 0.9 fusion.42
  275.1 0.9 constant_dynamic-slice_fusion.5
  276.0 68.7 %gather_fusion = bf16[16384,256]{1,0:T(8,128)(2,1)} fusion(bf16[32768,256]{1,0:T(8,128)(2,1)} %get-tuple-element.593, s32[16384]{0:T(1024)S(1)} %broadcast_clamp_fusion.2), kind=kCustom, calls=%fused_computation.1.clone.clone.1 | custom fusion | bytes 16842752 | tf_op jit(solution)/shard_map/while/body/eval_jaxpr/gather | solution.py:34
  344.7 5.5 fusion.43
  350.1 0.8 compare_select_fusion.4
  350.9 0.8 gather_fusion.1
  351.8 1.2 convolution_add_fusion.2
  354.4 0.9 fusion.42
  355.3 0.9 constant_dynamic-slice_fusion.5
  356.2 68.7 %gather_fusion = bf16[16384,256]{1,0:T(8,128)(2,1)} fusion(bf16[32768,256]{1,0:T(8,128)(2,1)} %get-tuple-element.593, s32[16384]{0:T(1024)S(1)} %broadcast_clamp_fusion.2), kind=kCustom, calls=%fused_computation.1.clone.clone.1 | custom fusion | bytes 16842752 | tf_op jit(solution)/shard_map/while/body/eval_jaxpr/gather | solution.py:34
  424.9 5.5 fusion.43
  431.1 0.8 gather_fusion.1
  432.0 1.2 convolution_add_fusion.2
  434.6 0.9 fusion.42
  435.5 0.9 constant_dynamic-slice_fusion.5
  436.4 68.7 %gather_fusion = bf16[16384,256]{1,0:T(8,128)(2,1)} fusion(bf16[32768,256]{1,0:T(8,128)(2,1)} %get-tuple-element.593, s32[16384]{0:T(1024)S(1)} %broadcast_clamp_fusion.2), kind=kCustom, calls=%fused_computation.1.clone.clone.1 | custom fusion | bytes 16842752 | tf_op jit(solution)/shard_map/while/body/eval_jaxpr/gather | solution.py:34
  505.1 5.5 fusion.43
  511.4 0.8 gather_fusion.1
  512.2 1.2 convolution_add_fusion.2
  513.6 1.3 copy.45
  515.0 15.2 %fusion.11 = f32[256,256]{0,1:T(8,128)S(1)} fusion(bf16[32768,256]{0,1:T(8,128)(2,1)} %all-gather.5.cloned.1.call-done, f32[256,256]{0,1:T(8,128)} %all-reduce.3.cloned.1.call-done), kind=kOutput, calls=%fused_computation.25 | convolution fusion | flops 4295163904 | bytes 17301504 | tf_op jit(solution)/shard_map/dot_general | solution.py:28
  530.3 11.7 %cholesky.50 = f32[128,128]{1,0:T(8,128)S(1)} custom-call(f32[128,128]{1,0:T(8,128)S(1)} %cholesky.118), custom_call_target="Cholesky" | custom-call | tf_op jit(solution)/shard_map/jit(cholesky)/cholesky | solution.py:94
  542.1 9.8 %custom-call.18 = f32[1,128,128]{1,2,0:T(8,128)S(1)} custom-call(f32[1,128,128]{2,1,0:T(8,128)S(1)} %get-tuple-element.439), custom_call_target="InvertDiagBlocksLowerTriangular" | custom-call | tf_op jit(solution)/shard_map/jit(cholesky)/cholesky | solution.py:94
  552.4 11.9 %cholesky.105 = f32[128,128]{1,0:T(8,128)S(1)} custom-call(f32[128,128]{1,0:T(8,128)S(1)} %convolution_subtract_fusion.2), custom_call_target="Cholesky" | custom-call | tf_op jit(solution)/shard_map/jit(cholesky)/cholesky | solution.py:94
  566.5 4.1 while.17
  567.1 1.3 bitcast_dynamic-update-slice_fusion.2
  569.2 1.3 bitcast_dynamic-update-slice_fusion.2
  570.5 19.7 %custom-call.19 = f32[2,128,128]{1,2,0:T(8,128)S(1)} custom-call(f32[2,128,128]{2,1,0:T(8,128)S(1)} %get-tuple-element.332), custom_call_target="InvertDiagBlocksLowerTriangular" | custom-call | tf_op jit(solution)/shard_map/jit(_cho_solve)/triangular_solve | solution.py:95
  590.2 1.1 fusion.13
  591.4 1.0 convolution_subtract_fusion.1
  593.5 10.6 %all_to_all.31 = f32[128,16,16]{0,2,1:T(8,128)S(1)} all-to-all(f32[128,16,16]{0,2,1:T(8,128)S(1)} %bitcast.75), channel_id=1, replica_groups=mesh['rows'=16,'cols'=8] {'rows'}, dimensions={1} | all-to-all | bytes 262144 | tf_op jit(solution)/shard_map/all_to_all | solution.py:97
  604.2 11.2 %all_to_all.32 = f32[8,256,16]{1,2,0:T(8,128)S(1)} all-to-all(f32[8,256,16]{1,2,0:T(8,128)S(1)} %copy.47), channel_id=1, replica_groups=mesh['rows'=16,'cols'=8] {'cols'}, dimensions={0} | all-to-all | bytes 262144 | tf_op jit(solution)/shard_map/all_to_all | solution.py:96
  (61 shorter events, 13.3 us)
Async XLA Ops:
  6.5 52.8 %all-gather.3.cloned.1.call-start = ((), (), s32[]{:S(2)}) async-start(), calls=%async_computation.4 | async-start | bytes 1114112 | tf_op jit(solution)/shard_map/all_gather | solution.py:58
  7.3 162.9 %all-gather.5.cloned.1.call-start = ((), (), s32[]{:S(2)}) async-start(), calls=%async_computation.6 | async-start | bytes 17825792 | tf_op jit(solution)/shard_map/all_gather | solution.py:60
  30.5 484.4 %all-reduce.3.cloned.1.call-start = ((), (), s32[]{:S(2)}) async-start(), calls=%async_computation.5 | async-start | bytes 524288 | tf_op jit(solution)/shard_map/psum | solution.py:63
  62.1 528.1 %reduce-scatter.2.cloned.1.call-start = ((), (), s32[]{:S(2)}) async-start(), calls=%async_computation.7 | async-start | bytes 1179648 | tf_op jit(solution)/shard_map/reduce_scatter | solution.py:93
Sparse Core Ops, SparseCore 0:
  9.8 49.4 all-gather.2
  61.7 108.3 all-gather.4
  172.6 71.8 all-reduce.2
  515.1 37.6 reduce-scatter.1
where the time goes:
time: 625 us; the launch traced here: 623 us
  local copies, waits for them, and re-layouts  317 us (51%)
  waiting for transfers between devices  136 us (22%)
  other arithmetic  85.4 us (14%)
  blocking collectives  42.9 us (7%)
  matrix products  26.3 us (4%)
  between operations  14.6 us (2%)
    gather x4, local copies, waits for them, and re-layouts, block_fold(): picked = table[third.reshape(group * width)]  275 us
    all_gather x1, waiting for transfers between devices, per_device(): third_whole = lax.all_gather(third_part, 'rows', axis=1, tiled=True)  107 us
    another operation x6, other arithmetic, per_device(): factor = jnp.linalg.cholesky(gram)  34.2 us
    all_gather x1, waiting for transfers between devices, per_device(): second_range = lax.all_gather(second_factor, 'rows', axis=1, tiled=True)  28.7 us
    unnamed x3, local copies, waits for them, and re-layouts  24.6 us
    reduce_sum x4, other arithmetic, block_fold(): return jnp.sum(scaled.reshape(group, width, picked.shape[1]), axis=1)  21.8 us
    all_to_all x1, blocking collectives, from_everyone(): lax.all_to_all(jnp.broadcast_to(value[None], (size, *value.shape)), axis,...  21.1 us
    another operation x4, other arithmetic, per_device(): solved = jax.scipy.linalg.cho_solve((factor, True), mine.T).T  19.7 us
  transfers between devices with their start and end apart: 4, of which 2 were waited for; matrix products, arithmetic and copies ran while one was open for 68% of the time, Pallas kernels for 0%

commit v1 on v0

v1 whole, which is shorter than its diff:
```python
import functools

import jax
import jax.numpy as jnp
from jax import lax
from jax.experimental import pallas as pl
from jax.experimental.pallas import tpu as pltpu
from jax.sharding import PartitionSpec as P

BF = jnp.bfloat16
F32 = jnp.float32
NT = (((1,), (1,)), ((), ()))
NN = (((1,), (0,)), ((), ()))

LO = 256
HI = 128
NB = 16
PITCH = 24
STEP = 4


def dot(a, b, dims):
    return lax.dot_general(a, b, dims, preferred_element_type=F32)


def halves(x):
    head = x.astype(BF)
    return head, (x - head.astype(F32)).astype(BF)


def build_kernel(hi_ref, lo_ref, v_ref, head_ref, rest_ref, left, right):
    base = lax.broadcasted_iota(jnp.int32, (16, 128), 0)
    iota = [(base + 16 * j).astype(F32).astype(BF) for j in range(LO // 16)]
    one = jnp.ones((16, 128), BF)
    zero = jnp.zeros((16, 128), BF)
    for b in range(NB):
        hi, lo, v = (
            jnp.broadcast_to(ref[b : b + 1, :], (16, 128)).astype(BF)
            for ref in (hi_ref, lo_ref, v_ref)
        )
        a = jnp.concatenate([jnp.where(hi == iota[j], v, zero) for j in range(HI // 16)], 0)
        c = jnp.concatenate([jnp.where(lo == iota[j], one, zero) for j in range(LO // 16)], 0)
        s = dot(a, c, NT)
        left[pl.ds(b, HI, stride=PITCH), :] = s[:, :128]
        right[pl.ds(b, HI, stride=PITCH), :] = s[:, 128:]

    def split(i, carry):
        for u in range(4):
            h = i * 4 + u
            at = pl.multiple_of(h * PITCH, 8)
            x = jnp.concatenate([left[pl.ds(at, NB), :], right[pl.ds(at, NB), :]], 1)
            head_ref[h], rest_ref[h] = halves(x)
        return carry

    lax.fori_loop(0, HI // 4, split, 0)


def build(hi, lo, v):
    n = hi.shape[0]
    spec = pl.BlockSpec((NB, 128), lambda i: (i, 0))
    out = pl.BlockSpec((HI, NB, LO), lambda i: (0, i, 0))
    shape = jax.ShapeDtypeStruct((HI, n, LO), BF)
    return pl.pallas_call(
        build_kernel,
        grid=(n // NB,),
        in_specs=[spec] * 3,
        out_specs=[out, out],
        out_shape=[shape, shape],
        scratch_shapes=[pltpu.VMEM((HI * PITCH, 128), F32)] * 2,
        cost_estimate=pl.CostEstimate(
            flops=40_000_000_000, bytes_accessed=n * HI * LO * 4, transcendentals=0
        ),
    )(hi, lo, v)


def product_kernel(head_ref, rest_ref, t_ref, second_ref, owner_ref, part_ref, gram_ref, acc):
    step = pl.program_id(0)
    t = t_ref[...].reshape(256, STEP * LO)
    head = jnp.concatenate([head_ref[i] for i in range(STEP)], 1)
    rest = jnp.concatenate([rest_ref[i] for i in range(STEP)], 1)
    fold = dot(head, t, NT) + dot(rest, t, NT)
    gram = dot(t, t, NT)

    @pl.when(step == 0)
    def _():
        acc[...] = fold
        gram_ref[...] = gram

    @pl.when(step > 0)
    def _():
        acc[...] += fold
        gram_ref[...] += gram

    @pl.when(step == pl.num_programs(0) - 1)
    def _():
        head, rest = halves(second_ref[...].astype(F32) * acc[...])
        n = owner_ref.shape[1]
        slot = lax.broadcasted_iota(jnp.int32, (part_ref.shape[0], n), 0)
        hot = (slot == owner_ref[...]).astype(F32).astype(BF)
        part_ref[...] = dot(hot, head, NN) + dot(hot, rest, NN)


def product(head, rest, table, second, owner, slab):
    n = head.shape[1]
    s_spec = pl.BlockSpec((STEP, n, LO), lambda i: (i, 0, 0))
    per = table.shape[3] // (STEP * LO)
    return pl.pallas_call(
        product_kernel,
        grid=(HI // STEP,),
        in_specs=[
            s_spec,
            s_spec,
            pl.BlockSpec((16, 1, 16, STEP * LO), lambda i: (0, i // per, 0, i % per)),
            pl.BlockSpec((n, 256), lambda i: (0, 0)),
            pl.BlockSpec((1, n), lambda i: (0, 0)),
        ],
        out_specs=[
            pl.BlockSpec((slab, 256), lambda i: (0, 0)),
            pl.BlockSpec((256, 256), lambda i: (0, 0)),
        ],
        out_shape=[
            jax.ShapeDtypeStruct((slab, 256), F32),
            jax.ShapeDtypeStruct((256, 256), F32),
        ],
        scratch_shapes=[pltpu.VMEM((n, 256), F32)],
        cost_estimate=pl.CostEstimate(
            flops=30_000_000_000, bytes_accessed=100_000_000, transcendentals=0
        ),
    )(head, rest, table, second, owner)


def per_device(
    block_values,
    block_length,
    block_owner,
    block_second,
    block_third,
    live_blocks,
    second_factor,
    third_factor,
):
    n_rows = lax.axis_size("rows")
    n_cols = lax.axis_size("cols")
    row_at = lax.axis_index("rows")
    col_at = lax.axis_index("cols")
    nblk, width = block_values.shape
    range_rows = second_factor.shape[0]
    slab = range_rows * n_cols // n_rows

    second_range = lax.all_gather(second_factor, "rows", axis=1, tiled=True)
    third_part = lax.all_gather(third_factor.T, "cols")
    third_whole = lax.all_gather(third_part, "rows")

    contract = (((0,), (0,)), ((), ()))
    gram_second = lax.psum(dot(second_range, second_range, contract), "cols")

    lane = jnp.arange(width, dtype=jnp.int32)
    slot = jnp.arange(nblk, dtype=jnp.int32)
    live = (lane[None, :] < block_length[:, None]) & (slot < live_blocks[0])[:, None]
    values = jnp.where(live, block_values, jnp.zeros((), BF)).astype(F32)
    head, rest = build(
        (block_third // LO).astype(F32), (block_third % LO).astype(F32), values
    )
    picked = second_range[block_second - col_at * range_rows]
    owner = (block_owner - row_at * slab)[None, :]
    part, gram_third = product(head, rest, third_whole, picked, owner, slab)

    gram = (gram_second / (range_rows * n_cols)) * (
        gram_third / (third_factor.shape[0] * n_cols)
    )
    mine = lax.psum_scatter(part, "cols", scatter_dimension=0, tiled=True)
    factor = jnp.linalg.cholesky(gram)
    solved = jax.scipy.linalg.cho_solve((factor, True), mine.T).T
    moved = lax.all_to_all(
        lax.all_to_all(solved, "rows", split_axis=1, concat_axis=0, tiled=True),
        "cols",
        split_axis=0,
        concat_axis=0,
        tiled=True,
    )
    share = n_rows // n_cols
    owned_rows = mine.shape[0]
    reordered = moved.reshape(n_cols, share, owned_rows, moved.shape[1]).transpose(1, 0, 2, 3)
    return reordered.reshape(n_rows * owned_rows, moved.shape[1])


def solution(mesh):
    return jax.shard_map(
        per_device,
        mesh=mesh,
        in_specs=(
            P(("rows", "cols"), None),
            P(("rows", "cols")),
            P(("rows", "cols")),
            P(("rows", "cols")),
            P(("rows", "cols"), None),
            P(("rows", "cols")),
            P("cols", "rows"),
            P("cols", "rows"),
        ),
        out_specs=P("cols", "rows"),
        check_vma=False,
    )
```

time: 625 us -> 379 us (0.61)
  local copies, waits for them, and re-layouts: 317 us -> 10.2 us
  Pallas kernels: 0 us -> 86 us
  waiting for transfers between devices: 136 us -> 175 us
  other arithmetic: 85.4 us -> 60.7 us
  matrix products: 26.3 us -> 6.48 us
  blocking collectives: 42.9 us -> 23.2 us
    gather x8 -> x1, local copies, waits for them, and re-layouts: 278 us -> 2.58 us  [per_device(): picked = second_range[block_second - col_at * range_rows]]
    pallas_call x0 -> x2, Pallas kernels: none -> 86 us  [the longest x1 47.2 us: product(): pl.pallas_call(product_kernel, grid=(HI // STEP,), in_specs=[s_spec, s_sp...]
    all_gather x1 -> x2, waiting for transfers between devices: 107 us -> 146 us  [the longest x1 104 us: per_device(): third_whole = lax.all_gather(third_part, 'rows')]
    all_gather x1, waiting for transfers between devices: 28.7 us -> 1.87 us  [per_device(): second_range = lax.all_gather(second_factor, 'rows', axis=1, tiled=True)]
    psum x1, waiting for transfers between devices: 0.02 us -> 26 us  [per_device(): gram_second = lax.psum(dot(second_range, second_range, contract), 'cols')]
    unnamed x3 -> x1, local copies, waits for them, and re-layouts: 24.6 us -> 0.7 us
    reduce_sum x4 -> x0, other arithmetic: 21.8 us -> none  [block_fold(): return jnp.sum(scaled.reshape(group, width, picked.shape[1]), axis=1)]
    all_to_all x1 -> x0, blocking collectives: 21.1 us -> none  [from_everyone(): lax.all_to_all(jnp.broadcast_to(value[None], (size, *value.shape)), axis,...]
  transfers between devices with their start and end apart: 4 -> 5, of which waited for: 2 -> 4; matrix products, arithmetic and copies ran while one was open for 68% -> 19% of each run, Pallas kernels for 0% -> 23%
where the time goes in v1:
time: 379 us; the launch traced here: 378 us
  waiting for transfers between devices  175 us (46%)
  Pallas kernels  86 us (23%)
  other arithmetic  60.7 us (16%)
  blocking collectives  23.2 us (6%)
  between operations  15.3 us (4%)
  local copies, waits for them, and re-layouts  10.2 us (3%)
  matrix products  6.48 us (2%)
    all_gather x1, waiting for transfers between devices, per_device(): third_whole = lax.all_gather(third_part, 'rows')  104 us
    pallas_call x1, Pallas kernels, product(): pl.pallas_call(product_kernel, grid=(HI // STEP,), in_specs=[s_spec, s_sp...  47.2 us
    all_gather x1, waiting for transfers between devices, per_device(): third_part = lax.all_gather(third_factor.T, 'cols')  42.3 us
    pallas_call x1, Pallas kernels, build(): pl.pallas_call(build_kernel, grid=(n // NB,), in_specs=[spec] * 3, out_sp...  38.8 us
    another operation x6, other arithmetic, per_device(): factor = jnp.linalg.cholesky(gram)  34 us
    psum x1, waiting for transfers between devices, per_device(): gram_second = lax.psum(dot(second_range, second_range, contract), 'cols')  26 us
    another operation x4, other arithmetic, per_device(): solved = jax.scipy.linalg.cho_solve((factor, True), mine.T).T  19.9 us
    all_to_all x1, blocking collectives, per_device(): lax.all_to_all(solved, 'rows', split_axis=1, concat_axis=0, tiled=True)  14.4 us
  transfers between devices with their start and end apart: 5, of which 4 were waited for; matrix products, arithmetic and copies ran while one was open for 19% of the time, Pallas kernels for 23%

profile of v1, /device:TPU:0, one launch (start us, length us, event | category | flops | bytes accessed | tf_op | source)
XLA Modules:
  0.0 377.6 jit_solution(10043129342257013113)
XLA Ops:
  6.5 0.7 all-gather.8.cloned.1.call-update
  7.3 0.0 all-gather.6.cloned.1.call-start
  7.3 0.7 all-gather.6.cloned.1.call-update
  8.0 0.0 all-gather.10.cloned.1.call-start
  8.1 42.3 %all-gather.8.cloned.1.call-done = bf16[128,4096]{1,0:T(8,128)(2,1)} async-done(((bf16[16,4096]{1,0:T(8,128)(2,1)}), bf16[128,4096]{1,0:T(8,128)(2,1)}) %all-gather.8.cloned.1.call-update) | async-done | bytes 1048592 | tf_op jit(solution)/shard_map/all_gather | solution.py:151
  50.3 0.0 all-reduce.3.cloned.1.call-start
  51.1 0.7 compare_select_fusion
  51.8 1.3 broadcast_subtract_fusion
  53.0 1.8 fusion.7.v_ref
  54.8 2.0 fusion.1
  56.8 38.8 %shard_map.82 = (bf16[128,512,256]{2,1,0:T(8,128)(2,1)}, bf16[128,512,256]{2,1,0:T(8,128)(2,1)}) custom-call(f32[512,128]{1,0:T(8,128)} %get-tuple-element.32.hi_ref, f32[512,128]{1,0:T(8,128)} %get-tuple-element.31.lo_ref, f32[512,128]{1,0:T(8,128)} %fusion.7.v_ref), custom_call_target="tpu_custom_call" | custom-call | flops 40000000000 | bytes 67108864 | tf_op jit(solution)/shard_map/pallas_call | solution.py:63
  95.6 1.9 all-gather.6.cloned.1.call-done
  97.5 1.5 copy.28
  99.0 2.6 gather_fusion
  101.5 2.8 fusion.19
  104.3 0.2 reduce-scatter.2.cloned.1.call-start
  104.6 103.8 %all-gather.10.cloned.1.call-done = bf16[128,16,4096]{2,1,0:T(8,128)(2,1)} async-done(((bf16[8,16,4096]{2,1,0:T(8,128)(2,1)}), bf16[128,16,4096]{2,1,0:T(8,128)(2,1)}) %all-gather.10.cloned.1.call-update) | async-done | bytes 16777232 | tf_op jit(solution)/shard_map/all_gather | solution.py:152
  208.3 47.2 %shard_map.83 = (f32[1024,256]{1,0:T(8,128)}, f32[256,256]{1,0:T(8,128)}) custom-call(bf16[128,512,256]{2,1,0:T(8,128)(2,1)} %get-tuple-element.9.head_ref, bf16[128,512,256]{2,1,0:T(8,128)(2,1)} %get-tuple-element.10.rest_ref, bf16[16,8,16,4096]{3,2,1,0:T(8,128)(2,1)} %bitcast.70, bf16[512,256]{1,0:T(8,128)(2,1)} %gather_fusion, s32[1,512]{1,0:T(1,128)} %bitcast.69), custom_call_target="tpu_custom_call" | custom-call | flops 30000001024 | bytes 100000000 | tf_op jit(solution)/shard_map/pallas_call | solution.py:107
  255.6 1.1 copy.29
  256.7 0.0 reduce-scatter.2.cloned.1.call-update
  256.7 26.0 %all-reduce.3.cloned.1.call-done = f32[256,256]{0,1:T(8,128)} async-done(((f32[256,256]{0,1:T(8,128)}), f32[256,256]{0,1:T(8,128)}) %all-reduce.3.cloned.1.call-update) | async-done | bytes 262160 | tf_op jit(solution)/shard_map/psum | solution.py:155
  282.7 1.0 multiply_multiply_fusion
  283.7 0.1 copy.30
  283.9 11.7 %cholesky.50 = f32[128,128]{1,0:T(8,128)S(1)} custom-call(f32[128,128]{1,0:T(8,128)S(1)} %cholesky.118), custom_call_target="Cholesky" | custom-call | tf_op jit(solution)/shard_map/jit(cholesky)/cholesky | solution.py:172
  295.6 9.8 %custom-call.18 = f32[1,128,128]{1,2,0:T(8,128)S(1)} custom-call(f32[1,128,128]{2,1,0:T(8,128)S(1)} %get-tuple-element.36), custom_call_target="InvertDiagBlocksLowerTriangular" | custom-call | tf_op jit(solution)/shard_map/jit(cholesky)/cholesky | solution.py:172
  305.4 0.2 constant_dynamic-update-slice_fusion.1
  305.7 0.3 convolution_subtract_fusion.2
  305.9 11.7 %cholesky.105 = f32[128,128]{1,0:T(8,128)S(1)} custom-call(f32[128,128]{1,0:T(8,128)S(1)} %convolution_subtract_fusion.2), custom_call_target="Cholesky" | custom-call | tf_op jit(solution)/shard_map/jit(cholesky)/cholesky | solution.py:172
  317.7 0.7 compare_reduce_fusion
  319.6 0.1 triangular_solve.66
  319.7 3.9 %while.1 = (s32[]{:T(128)}, f32[256,256]{1,0:T(8,128)S(1)}, s32[2,2]{1,0:T(2,128)S(1)}, f32[2,128,128]{2,1,0:T(8,128)S(1)}, s32[]{:T(128)}) while((s32[]{:T(128)}, f32[256,256]{1,0:T(8,128)S(1)}, s32[2,2]{1,0:T(2,128)S(1)}, f32[2,128,128]{2,1,0:T(8,128)S(1)}, s32[]{:T(128)}) %tuple.24), condition=%wide.while_cond, body=%wide.while_body.sunk | while | flops 2 | bytes 131189 | solution.py:173
  319.7 0.6 fusion.30
  320.3 1.4 bitcast_dynamic-update-slice_fusion.2
  321.7 0.6 fusion.30
  322.3 1.4 bitcast_dynamic-update-slice_fusion.2
  323.7 19.9 %custom-call.19 = f32[2,128,128]{1,2,0:T(8,128)S(1)} custom-call(f32[2,128,128]{2,1,0:T(8,128)S(1)} %get-tuple-element.20), custom_call_target="InvertDiagBlocksLowerTriangular" | custom-call | tf_op jit(solution)/shard_map/jit(_cho_solve)/triangular_solve | solution.py:173
  343.6 0.0 reduce-scatter.2.cloned.1.call-done
  343.6 1.1 fusion.8
  344.7 1.1 convolution_subtract_fusion.1
  345.9 0.3 fusion.15
  346.2 0.2 fusion.14
  346.4 0.3 convolution_subtract_fusion
  346.7 0.2 fusion.13
  346.9 14.4 %all_to_all.25 = f32[128,16,16]{0,2,1:T(8,128)S(1)} all-to-all(f32[128,16,16]{0,2,1:T(8,128)S(1)} %bitcast.62), channel_id=1, replica_groups=mesh['rows'=16,'cols'=8] {'rows'}, dimensions={1} | all-to-all | bytes 262144 | tf_op jit(solution)/shard_map/all_to_all | solution.py:175
  361.5 8.8 %all_to_all.26 = f32[8,256,16]{1,2,0:T(8,128)S(1)} all-to-all(f32[8,256,16]{1,2,0:T(8,128)S(1)} %copy.33), channel_id=1, replica_groups=mesh['rows'=16,'cols'=8] {'cols'}, dimensions={0} | all-to-all | bytes 262144 | tf_op jit(solution)/shard_map/all_to_all | solution.py:174
  370.3 0.1 reshape.43
  370.3 0.1 copy.34
  370.4 0.7 copy.39
  (19 shorter events, 0.4 us)
Async XLA Ops:
  6.5 43.8 %all-gather.8.cloned.1.call-start = ((), (), s32[]{:S(2)}) async-start(), calls=%async_computation.6 | async-start | bytes 1179648 | tf_op jit(solution)/shard_map/all_gather | solution.py:151
  7.3 90.2 %all-gather.6.cloned.1.call-start = ((), (), s32[]{:S(2)}) async-start(), calls=%async_computation.3 | async-start | bytes 1114112 | tf_op jit(solution)/shard_map/all_gather | solution.py:150
  8.0 200.3 %all-gather.10.cloned.1.call-start = ((), (), s32[]{:S(2)}) async-start(), calls=%async_computation.7 | async-start | bytes 17825792 | tf_op jit(solution)/shard_map/all_gather | solution.py:152
  50.3 232.3 %all-reduce.3.cloned.1.call-start = ((), (), s32[]{:S(2)}) async-start(), calls=%async_computation.4 | async-start | bytes 524288 | tf_op jit(solution)/shard_map/psum | solution.py:155
  104.3 239.3 %reduce-scatter.2.cloned.1.call-start = ((), (), s32[]{:S(2)}) async-start(), calls=%async_computation.5 | async-start | bytes 1179648 | tf_op jit(solution)/shard_map/reduce_scatter | solution.py:171
Sparse Core Ops, SparseCore 0:
  9.0 41.2 all-gather.7
  52.8 44.6 all-gather.5
  99.9 108.3 all-gather.9
  210.7 71.9 all-reduce.2
  284.9 39.1 reduce-scatter.1

commit v2 on v1

--- a/solution.py
+++ b/solution.py
@@ -1,5 +1,3 @@
-import functools
-
 import jax
 import jax.numpy as jnp
 from jax import lax
@@ -7,6 +5,7 @@
 from jax.experimental.pallas import tpu as pltpu
 from jax.sharding import PartitionSpec as P
 
+
 BF = jnp.bfloat16
 F32 = jnp.float32
 NT = (((1,), (1,)), ((), ()))
@@ -16,7 +15,10 @@
 HI = 128
 NB = 16
 PITCH = 24
-STEP = 4
+PARTS = 4
+STEP = 8
+AXES = ("rows", "cols")
+SHIFTS = (1, -1, 2)
 
 
 def dot(a, b, dims):
@@ -55,43 +57,161 @@
     lax.fori_loop(0, HI // 4, split, 0)
 
 
+def build_more_kernel(hi_ref, lo_ref, v_ref, head_in, rest_in, *refs):
+    build_kernel(hi_ref, lo_ref, v_ref, *refs)
+
+
 def build(hi, lo, v):
     n = hi.shape[0]
-    spec = pl.BlockSpec((NB, 128), lambda i: (i, 0))
-    out = pl.BlockSpec((HI, NB, LO), lambda i: (0, i, 0))
+    steps = n // NB // PARTS
     shape = jax.ShapeDtypeStruct((HI, n, LO), BF)
-    return pl.pallas_call(
-        build_kernel,
-        grid=(n // NB,),
-        in_specs=[spec] * 3,
-        out_specs=[out, out],
-        out_shape=[shape, shape],
-        scratch_shapes=[pltpu.VMEM((HI * PITCH, 128), F32)] * 2,
-        cost_estimate=pl.CostEstimate(
-            flops=40_000_000_000, bytes_accessed=n * HI * LO * 4, transcendentals=0
-        ),
-    )(hi, lo, v)
-
-
-def product_kernel(head_ref, rest_ref, t_ref, second_ref, owner_ref, part_ref, gram_ref, acc):
+    made = ()
+    for part in range(PARTS):
+        spec = pl.BlockSpec((NB, 128), lambda i, at=part * steps: (at + i, 0))
+        out = pl.BlockSpec((HI, NB, LO), lambda i, at=part * steps: (0, at + i, 0))
+        call = pl.pallas_call(
+            build_more_kernel if made else build_kernel,
+            grid=(steps,),
+            in_specs=[spec] * 3 + [pl.BlockSpec(memory_space=pl.ANY)] * len(made),
+            out_specs=[out, out],
+            out_shape=[shape, shape],
+            scratch_shapes=[pltpu.VMEM((HI * PITCH, 128), F32)] * 2,
+            input_output_aliases={3 + i: i for i in range(len(made))},
+            cost_estimate=pl.CostEstimate(
+                flops=40_000_000_000 // PARTS,
+                bytes_accessed=n * HI * LO * 4 // PARTS,
+                transcendentals=0,
+            ),
+        )
+        made = call(hi, lo, v, *made)
+    return made
+
+
+def place(i):
+    return {
+        "x": i // 16 % 4,
+        "y": i // 2 % 4,
+        "z": i // 64 * 2 + i % 2,
+        "core": i // 8 % 2,
+    }
+
+
+def device(at):
+    return (((at["z"] // 2 * 4 + at["x"]) * 2 + at["core"]) * 4 + at["y"]) * 2 + at["z"] % 2
+
+
+def shifted(value, dims, shift):
+    pairs = []
+    for i in range(128):
+        at = place(i)
+        dim = dims[at["core"]]
+        at[dim] = (at[dim] + shift) % (2 if dim == "core" else 4)
+        pairs.append((i, device(at)))
+    return lax.ppermute(value, AXES, pairs)
+
+
+def across(value):
+    return shifted(value, ("core", "core"), 1)
+
+
+def ring(value, dims):
+    came = [value]
+    for shift in SHIFTS:
+        came.append(shifted(value, dims, shift))
+    return jnp.concatenate(came, 0)
+
+
+def gather_table(piece, core):
+    half = piece.shape[1] // 2
+    mine = lax.dynamic_slice_in_dim(piece, core * half, half, 1)
+    other = lax.dynamic_slice_in_dim(piece, (1 - core) * half, half, 1)
+    came = across(other)
+    unit = jnp.where(core == 0, jnp.stack([mine, came]), jnp.stack([came, mine]))
+    near = ring(unit[None], ("x", "y"))
+    plane = ring(near[None], ("y", "z"))
+    last = ("z", "x")
+    left = shifted(plane, last, 1)
+    right = shifted(plane, last, -1)
+    far0 = shifted(left[:2], last, 1)
+    far1 = shifted(right[2:], last, -1)
+    own = [x.reshape(-1, *unit.shape) for x in (plane, left, right, far0, far1)]
+    return own, [across(x) for x in own]
+
+
+def piece_table(row_at, col_at, order):
+    def spot(there, here):
+        ahead = (there - here) & 3
+        return jnp.where(ahead == 3, 1, jnp.where(ahead == 0, 0, ahead + 1))
+
+    y, z_lo, z_hi, x = jnp.meshgrid(
+        jnp.arange(4), jnp.arange(2), jnp.arange(2), jnp.arange(4), indexing="ij"
+    )
+    at_x = spot(x, row_at >> 1)
+    at_y = spot(y, col_at >> 1)
+    at_z = spot(z_hi * 2 + z_lo, (row_at >> 3) * 2 + (col_at & 1))
+    first = jnp.where(order == 0, at_x, at_y)
+    second = jnp.where(order == 0, at_y, at_z)
+    third = jnp.where(order == 0, at_z, at_x)
+    late = (third == 3) & (second >= 2)
+    array = third + late
+    index = (second - 2 * late) * 4 + first
+    return jnp.concatenate([array.ravel(), index.ravel(), order[None]]).astype(jnp.int32)
+
+
+def fetch(table, pieces, buf, sem, step, slot):
+    n = buf.shape[1]
+    for p in range(n):
+        array = table[step * n + p]
+        index = table[64 + step * n + p]
+        for a, ref in enumerate(pieces):
+
+            @pl.when(array == a)
+            def _(ref=ref, p=p):
+                pltpu.make_async_copy(ref.at[index], buf.at[slot, p], sem.at[slot]).start()
+
+
+def accumulate(table, head_ref, rest_ref, pieces, fold_ref, gram_ref, buf, sem, begin):
     step = pl.program_id(0)
-    t = t_ref[...].reshape(256, STEP * LO)
+    slot = lax.rem(step, 2)
+
+    @pl.when(step == 0)
+    def _():
+        begin()
+        fetch(table, pieces, buf, sem, 0, 0)
+
+    @pl.when(step + 1 < pl.num_programs(0))
+    def _():
+        fetch(table, pieces, buf, sem, step + 1, 1 - slot)
+
+    pltpu.make_async_copy(pieces[0].at[pl.ds(0, buf.shape[1])], buf.at[slot], sem.at[slot]).wait()
+    t = buf[slot].reshape(256, STEP * LO)
     head = jnp.concatenate([head_ref[i] for i in range(STEP)], 1)
     rest = jnp.concatenate([rest_ref[i] for i in range(STEP)], 1)
-    fold = dot(head, t, NT) + dot(rest, t, NT)
-    gram = dot(t, t, NT)
-
-    @pl.when(step == 0)
-    def _():
-        acc[...] = fold
-        gram_ref[...] = gram
-
-    @pl.when(step > 0)
-    def _():
-        acc[...] += fold
-        gram_ref[...] += gram
-
-    @pl.when(step == pl.num_programs(0) - 1)
+    fold_ref[...] += dot(head, t, NT) + dot(rest, t, NT)
+    gram_ref[...] += dot(t, t, NT)
+
+
+def first_kernel(table, head_ref, rest_ref, p0, p1, p2, p3, p4, fold_ref, gram_ref, buf, sem):
+    def begin():
+        fold_ref[...] = jnp.zeros_like(fold_ref)
+        gram_ref[...] = jnp.zeros_like(gram_ref)
+
+    accumulate(
+        table, head_ref, rest_ref, (p0, p1, p2, p3, p4), fold_ref, gram_ref, buf, sem, begin
+    )
+
+
+def second_kernel(
+    table, head_ref, rest_ref, p0, p1, p2, p3, p4,
+    fold_in, gram_in, second_ref, owner_ref, part_ref, gram_ref, acc, buf, sem,
+):
+    def begin():
+        acc[...] = fold_in[...]
+        gram_ref[...] = gram_in[...]
+
+    accumulate(table, head_ref, rest_ref, (p0, p1, p2, p3, p4), acc, gram_ref, buf, sem, begin)
+
+    @pl.when(pl.program_id(0) == pl.num_programs(0) - 1)
     def _():
         head, rest = halves(second_ref[...].astype(F32) * acc[...])
         n = owner_ref.shape[1]
@@ -100,33 +220,35 @@
         part_ref[...] = dot(hot, head, NN) + dot(hot, rest, NN)
 
 
-def product(head, rest, table, second, owner, slab):
+def product(table, head, rest, pieces, more, slab):
     n = head.shape[1]
-    s_spec = pl.BlockSpec((STEP, n, LO), lambda i: (i, 0, 0))
-    per = table.shape[3] // (STEP * LO)
+    steps = HI // STEP // 2
+    s_spec = pl.BlockSpec((STEP, n, LO), lambda i, table: (2 * i + table[128], 0, 0))
+    any_spec = pl.BlockSpec(memory_space=pl.ANY)
+    whole = lambda x: pl.BlockSpec(x.shape, lambda i, table: (0, 0))
+    rows = slab if more else n
+    out = [jax.ShapeDtypeStruct((rows, 256), F32), jax.ShapeDtypeStruct((256, 256), F32)]
+    shape = pieces[0].shape
+    scratch = [
+        pltpu.VMEM((2, 8, *shape[1:]), BF),
+        pltpu.SemaphoreType.DMA((2,)),
+    ]
+    if more:
+        scratch = [pltpu.VMEM((n, 256), F32)] + scratch
     return pl.pallas_call(
-        product_kernel,
-        grid=(HI // STEP,),
-        in_specs=[
-            s_spec,
-            s_spec,
-            pl.BlockSpec((16, 1, 16, STEP * LO), lambda i: (0, i // per, 0, i % per)),
-            pl.BlockSpec((n, 256), lambda i: (0, 0)),
-            pl.BlockSpec((1, n), lambda i: (0, 0)),
-        ],
-        out_specs=[
-            pl.BlockSpec((slab, 256), lambda i: (0, 0)),
-            pl.BlockSpec((256, 256), lambda i: (0, 0)),
-        ],
-        out_shape=[
-            jax.ShapeDtypeStruct((slab, 256), F32),
-            jax.ShapeDtypeStruct((256, 256), F32),
-        ],
-        scratch_shapes=[pltpu.VMEM((n, 256), F32)],
+        second_kernel if more else first_kernel,
+        grid_spec=pltpu.PrefetchScalarGridSpec(
+            num_scalar_prefetch=1,
+            grid=(steps,),
+            in_specs=[s_spec, s_spec] + [any_spec] * 5 + [whole(x) for x in more],
+            out_specs=[whole(x) for x in out],
+            scratch_shapes=scratch,
+        ),
+        out_shape=out,
         cost_estimate=pl.CostEstimate(
-            flops=30_000_000_000, bytes_accessed=100_000_000, transcendentals=0
+            flops=15_000_000_000, bytes_accessed=50_000_000, transcendentals=0
         ),
-    )(head, rest, table, second, owner)
+    )(table, head, rest, *pieces, *more)
 
 
 def per_device(
@@ -148,8 +270,8 @@
     slab = range_rows * n_cols // n_rows
 
     second_range = lax.all_gather(second_factor, "rows", axis=1, tiled=True)
-    third_part = lax.all_gather(third_factor.T, "cols")
-    third_whole = lax.all_gather(third_part, "rows")
+    core = row_at & 1
+    own, swapped = gather_table(third_factor.T, core)
 
     contract = (((0,), (0,)), ((), ()))
     gram_second = lax.psum(dot(second_range, second_range, contract), "cols")
@@ -163,12 +285,16 @@
     )
     picked = second_range[block_second - col_at * range_rows]
     owner = (block_owner - row_at * slab)[None, :]
-    part, gram_third = product(head, rest, third_whole, picked, owner, slab)
+    fold = product(piece_table(row_at, col_at, core), head, rest, own, (), slab)
+    part, gram_third = product(
+        piece_table(row_at, col_at, 1 - core), head, rest, swapped, (*fold, picked, owner), slab
+    )
 
     gram = (gram_second / (range_rows * n_cols)) * (
         gram_third / (third_factor.shape[0] * n_cols)
     )
-    mine = lax.psum_scatter(part, "cols", scatter_dimension=0, tiled=True)
+    spread = part.reshape(n_cols, slab // n_cols, -1)
+    mine = jnp.sum(lax.all_to_all(spread, "cols", 0, 0, tiled=True), 0)
     factor = jnp.linalg.cholesky(gram)
     solved = jax.scipy.linalg.cho_solve((factor, True), mine.T).T
     moved = lax.all_to_all(

time: 379 us -> 265 us (0.70)
  waiting for transfers between devices: 175 us -> 28.5 us
  starting transfers between devices: 0.34 us -> 23.4 us
  local copies, waits for them, and re-layouts: 10.2 us -> 15.8 us
    all_gather x2 -> x0, waiting for transfers between devices: 146 us -> none  [the longest x1 104 us: per_device(): third_whole = lax.all_gather(third_part, 'rows')]
    ppermute x0 -> x16, starting transfers between devices: none -> 18.5 us  [shifted(): return lax.ppermute(value, AXES, pairs)]
    ppermute x0 -> x16, waiting for transfers between devices: none -> 11.2 us  [shifted(): return lax.ppermute(value, AXES, pairs)]
    psum x1, waiting for transfers between devices: 26 us -> 17.2 us  [per_device(): gram_second = lax.psum(dot(second_range, second_range, contract), 'cols')]
    all_to_all x0 -> x1, starting transfers between devices: none -> 4.88 us  [per_device(): mine = jnp.sum(lax.all_to_all(spread, 'cols', 0, 0, tiled=True), 0)]
    slice x0 -> x2, local copies, waits for them, and re-layouts: none -> 4.63 us  [the longest x1 2.33 us: gather_table(): far0 = shifted(left[:2], last, 1)]
    pallas_call x2 -> x6, Pallas kernels: 86 us -> 87.4 us  [the longest x4 44.3 us: build(): made = call(hi, lo, v, *made)]
    another operation x6 -> x7, other arithmetic: 34 us -> 34.6 us  [per_device(): factor = jnp.linalg.cholesky(gram)]
  transfers between devices with their start and end apart: 5 -> 19, of which waited for: 4 -> 8; matrix products, arithmetic and copies ran while one was open for 19% -> 30% of each run, Pallas kernels for 23% -> 33%
where the time goes in v2:
time: 265 us; the launch traced here: 264 us
  Pallas kernels  87.4 us (33%)
  other arithmetic  63.2 us (24%)
  waiting for transfers between devices  28.5 us (11%)
  blocking collectives  25.5 us (10%)
  starting transfers between devices  23.4 us (9%)
  local copies, waits for them, and re-layouts  15.8 us (6%)
  between operations  15.8 us (6%)
  matrix products  4.92 us (2%)
    pallas_call x4, Pallas kernels, build(): made = call(hi, lo, v, *made)  44.3 us
    pallas_call x2, Pallas kernels, product(): pl.pallas_call(second_kernel if more else first_kernel, grid_spec=pltpu.P...  43.1 us
    another operation x7, other arithmetic, per_device(): factor = jnp.linalg.cholesky(gram)  34.6 us
    another operation x4, other arithmetic, per_device(): solved = jax.scipy.linalg.cho_solve((factor, True), mine.T).T  19.9 us
    ppermute x16, starting transfers between devices, shifted(): return lax.ppermute(value, AXES, pairs)  18.5 us
    psum x1, waiting for transfers between devices, per_device(): gram_second = lax.psum(dot(second_range, second_range, contract), 'cols')  17.2 us
    all_to_all x1, blocking collectives, per_device(): lax.all_to_all(solved, 'rows', split_axis=1, concat_axis=0, tiled=True)  16.7 us
    ppermute x16, waiting for transfers between devices, shifted(): return lax.ppermute(value, AXES, pairs)  11.2 us
  transfers between devices with their start and end apart: 19, of which 8 were waited for; matrix products, arithmetic and copies ran while one was open for 30% of the time, Pallas kernels for 33%

profile of v2, /device:TPU:0, one launch (start us, length us, event | category | flops | bytes accessed | tf_op | source)
XLA Modules:
  0.0 264.5 jit_solution(2328398016890392866)
XLA Ops:
  6.5 0.9 dynamic-slice_bitcast_fusion.1
  7.7 2.0 fusion.1
  10.4 1.8 fusion.7.v_ref
  12.2 11.1 %shard_map.82 = (bf16[128,512,256]{2,1,0:T(8,128)(2,1)}, bf16[128,512,256]{2,1,0:T(8,128)(2,1)}) custom-call(f32[512,128]{1,0:T(8,128)} %get-tuple-element.48.hi_ref, f32[512,128]{1,0:T(8,128)} %get-tuple-element.47.lo_ref, f32[512,128]{1,0:T(8,128)} %fusion.7.v_ref), custom_call_target="tpu_custom_call" | custom-call | flops 10000000000 | bytes 16777216 | tf_op jit(solution)/shard_map/pallas_call | solution.py:86
  23.3 3.2 %collective-permute-start.3 = (bf16[1,2,16,2048]{3,2,1,0:T(8,128)(2,1)S(1)}, bf16[1,2,16,2048]{3,2,1,0:T(8,128)(2,1)S(1)}, u32[]{:S(2)}, u32[]{:S(2)}) collective-permute-start(bf16[1,2,16,2048]{3,2,1,0:T(8,128)(2,1)S(1)} %maximum_select_fusion), channel_id=1, source_target_pairs={{0,32},{1,33},{2,34},{3,35},{4,36},{5,37},{6,38},{7,39},{8,12},{9,... | collective-permute-start | bytes 393224 | tf_op jit(solution)/shard_map/ppermute | solution.py:110
  26.5 1.1 collective-permute-start.2
  27.6 0.9 collective-permute-start.1
  29.2 0.7 collective-permute-done.3
  29.9 1.8 collective-permute-done.2
  31.7 2.2 collective-permute-done.1
  34.0 3.3 %collective-permute-start.6 = (bf16[1,4,2,16,2048]{4,3,2,1,0:T(8,128)(2,1)S(1)}, bf16[1,4,2,16,2048]{4,3,2,1,0:T(8,128)(2,1)S(1)}, u32[]{:S(2)}, u32[]{:S(2)}) collective-permute-start(bf16[1,4,2,16,2048]{4,3,2,1,0:T(8,128)(2,1)S(1)} %maximum_bitcast_fusion), channel_id=1, source_target_pairs={{0,4},{1,5},{2,6},{3,7},{4,0},{5,1},{6,2},{7,3},{8,72},{9,73},{10,... | collective-permute-start | bytes 1572872 | tf_op jit(solution)/shard_map/ppermute | solution.py:110
  37.3 1.1 collective-permute-start.5
  38.3 1.0 collective-permute-start.4
  39.3 11.1 %shard_map.83 = (bf16[128,512,256]{2,1,0:T(8,128)(2,1)}, bf16[128,512,256]{2,1,0:T(8,128)(2,1)}) custom-call(f32[512,128]{1,0:T(8,128)} %get-tuple-element.48.hi_ref, f32[512,128]{1,0:T(8,128)} %get-tuple-element.47.lo_ref, f32[512,128]{1,0:T(8,128)} %fusion.7.v_ref, ...), custom_call_target="tpu_custom_call", output_to_operand_aliasing={{0}: (3, {}), {1}: (4, {})} | custom-call | flops 10000000000 | bytes 16777216 | tf_op jit(solution)/shard_map/pallas_call | solution.py:86
  50.7 1.6 pad_maximum_fusion
  52.3 2.1 collective-permute-start.8
  54.4 2.0 collective-permute-start.10
  56.3 11.1 %shard_map.84 = (bf16[128,512,256]{2,1,0:T(8,128)(2,1)}, bf16[128,512,256]{2,1,0:T(8,128)(2,1)}) custom-call(f32[512,128]{1,0:T(8,128)} %get-tuple-element.48.hi_ref, f32[512,128]{1,0:T(8,128)} %get-tuple-element.47.lo_ref, f32[512,128]{1,0:T(8,128)} %fusion.7.v_ref, ...), custom_call_target="tpu_custom_call", output_to_operand_aliasing={{0}: (3, {}), {1}: (4, {})} | custom-call | flops 10000000000 | bytes 16777216 | tf_op jit(solution)/shard_map/pallas_call | solution.py:86
  67.4 0.7 pad_add_fusion.table
  68.1 11.1 %shard_map.85 = (bf16[128,512,256]{2,1,0:T(8,128)(2,1)}, bf16[128,512,256]{2,1,0:T(8,128)(2,1)}) custom-call(f32[512,128]{1,0:T(8,128)} %get-tuple-element.48.hi_ref, f32[512,128]{1,0:T(8,128)} %get-tuple-element.47.lo_ref, f32[512,128]{1,0:T(8,128)} %fusion.7.v_ref, ...), custom_call_target="tpu_custom_call", output_to_operand_aliasing={{0}: (3, {}), {1}: (4, {})} | custom-call | flops 10000000000 | bytes 16777216 | tf_op jit(solution)/shard_map/pallas_call | solution.py:86
  79.1 1.5 collective-permute-done.8
  80.7 2.3 slice.83
  83.0 2.3 slice.84
  85.3 3.2 %collective-permute-start.14 = (bf16[2,4,2,16,2048]{4,3,2,1,0:T(8,128)(2,1)}, bf16[2,4,2,16,2048]{4,3,2,1,0:T(8,128)(2,1)}, u32[]{:S(2)}, u32[]{:S(2)}) collective-permute-start(bf16[2,4,2,16,2048]{4,3,2,1,0:T(8,128)(2,1)} %slice.84), channel_id=1, source_target_pairs={{0,65},{1,0},{2,67},{3,2},{4,69},{5,4},{6,71},{7,6},{8,56},{9,57},... | collective-permute-start | bytes 3145736 | tf_op jit(solution)/shard_map/ppermute | solution.py:110
  88.5 0.6 pad_add_fusion.1.table
  90.4 3.0 %fusion.25 = f32[256,256]{0,1:T(8,128)} fusion(bf16[2048,256]{0,1:T(8,128)(2,1)} %all-gather.2.cloned.1.call-done), kind=kOutput, calls=%fused_computation.86 | convolution fusion | flops 268435456 | bytes 1310720 | tf_op jit(solution)/shard_map/dot_general | solution.py:25
  93.9 2.6 gather_fusion
  96.5 2.7 %collective-permute-done.12 = bf16[2,4,2,16,2048]{4,3,2,1,0:T(8,128)(2,1)S(1)} collective-permute-done((bf16[2,4,2,16,2048]{4,3,2,1,0:T(8,128)(2,1)}, bf16[2,4,2,16,2048]{4,3,2,1,0:T(8,128)(2,1)S(1)}, u32[]{:S(2)}, u32[]{:S(2)}) %collective-permute-start.12) | collective-permute-done | bytes 1048608 | tf_op jit(solution)/shard_map/ppermute | solution.py:110
  99.2 2.0 collective-permute-done.14
  101.2 20.9 %shard_map.86 = (f32[512,256]{1,0:T(8,128)}, f32[256,256]{1,0:T(8,128)}) custom-call(s32[129]{0:T(256)} %pad_add_fusion.1.table, bf16[128,512,256]{2,1,0:T(8,128)(2,1)} %get-tuple-element.23.head_ref, bf16[128,512,256]{2,1,0:T(8,128)(2,1)} %get-tuple-element.24.rest_ref, bf16[16,2,16,2048]{3,2,1,0:T(8,128)(2,1)} %bitcast.8.p0, ...), custom_call_target="tpu_custom_call" | custom-call | flops 15000000512 | bytes 50000000 | tf_op jit(solution)/shard_map/pallas_call | solution.py:238
  122.1 1.0 copy-done.2
  123.5 22.2 %shard_map.87 = (f32[1024,256]{1,0:T(8,128)}, f32[256,256]{1,0:T(8,128)}) custom-call(s32[129]{0:T(256)} %pad_add_fusion.table, bf16[128,512,256]{2,1,0:T(8,128)(2,1)} %get-tuple-element.23.head_ref, bf16[128,512,256]{2,1,0:T(8,128)(2,1)} %get-tuple-element.24.rest_ref, bf16[16,2,16,2048]{3,2,1,0:T(8,128)(2,1)} %collective-permute-done.7.p0, ...), custom_call_target="tpu_custom_call" | custom-call | flops 15000000512 | bytes 50000000 | tf_op jit(solution)/shard_map/pallas_call | solution.py:238
  145.7 4.9 %all-to-all-start = ((f32[8,128,256]{2,1,0:T(8,128)}), f32[8,128,256]{2,1,0:T(8,128)S(1)}, u32[]{:S(2)}, u32[]{:S(2)}) async-start(f32[8,128,256]{2,1,0:T(8,128)} %bitcast.77), calls=%async_computation | async-start | bytes 2097152 | tf_op jit(solution)/shard_map/all_to_all | solution.py:297
  150.7 17.2 %all-reduce.3.cloned.1.call-done = f32[256,256]{0,1:T(8,128)} async-done(((f32[256,256]{0,1:T(8,128)}), f32[256,256]{0,1:T(8,128)}) %all-reduce.3.cloned.1.call-update) | async-done | bytes 262160 | tf_op jit(solution)/shard_map/psum | solution.py:277
  167.9 1.0 multiply_multiply_fusion
  169.1 11.7 %cholesky.50 = f32[128,128]{1,0:T(8,128)S(1)} custom-call(f32[128,128]{1,0:T(8,128)S(1)} %cholesky.118), custom_call_target="Cholesky" | custom-call | tf_op jit(solution)/shard_map/jit(cholesky)/cholesky | solution.py:298
  180.9 9.8 %custom-call.18 = f32[1,128,128]{1,2,0:T(8,128)S(1)} custom-call(f32[1,128,128]{2,1,0:T(8,128)S(1)} %get-tuple-element.54), custom_call_target="InvertDiagBlocksLowerTriangular" | custom-call | tf_op jit(solution)/shard_map/jit(cholesky)/cholesky | solution.py:298
  191.2 11.7 %cholesky.105 = f32[128,128]{1,0:T(8,128)S(1)} custom-call(f32[128,128]{1,0:T(8,128)S(1)} %convolution_subtract_fusion.2), custom_call_target="Cholesky" | custom-call | tf_op jit(solution)/shard_map/jit(cholesky)/cholesky | solution.py:298
  202.9 0.6 compare_reduce_fusion.1
  203.6 0.7 compare_reduce_fusion
  205.6 3.9 %while.1 = (s32[]{:T(128)}, f32[256,256]{1,0:T(8,128)S(1)}, s32[2,2]{1,0:T(2,128)S(1)}, f32[2,128,128]{2,1,0:T(8,128)S(1)}, s32[]{:T(128)}) while((s32[]{:T(128)}, f32[256,256]{1,0:T(8,128)S(1)}, s32[2,2]{1,0:T(2,128)S(1)}, f32[2,128,128]{2,1,0:T(8,128)S(1)}, s32[]{:T(128)}) %tuple.35), condition=%wide.while_cond, body=%wide.while_body.sunk | while | flops 2 | bytes 131189 | solution.py:299
  205.6 0.6 fusion.36
  206.2 1.3 bitcast_dynamic-update-slice_fusion.2
  208.2 1.3 bitcast_dynamic-update-slice_fusion.2
  209.5 19.9 %custom-call.19 = f32[2,128,128]{1,2,0:T(8,128)S(1)} custom-call(f32[2,128,128]{2,1,0:T(8,128)S(1)} %get-tuple-element.36), custom_call_target="InvertDiagBlocksLowerTriangular" | custom-call | tf_op jit(solution)/shard_map/jit(_cho_solve)/triangular_solve | solution.py:299
  231.2 16.7 %all_to_all.30 = f32[128,16,16]{0,2,1:T(8,128)S(1)} all-to-all(f32[128,16,16]{0,2,1:T(8,128)S(1)} %bitcast.80), channel_id=1, replica_groups=mesh['rows'=16,'cols'=8] {'rows'}, dimensions={1} | all-to-all | bytes 262144 | tf_op jit(solution)/shard_map/all_to_all | solution.py:301
  248.0 8.8 %all_to_all.31 = f32[8,256,16]{1,2,0:T(8,128)S(1)} all-to-all(f32[8,256,16]{1,2,0:T(8,128)S(1)} %copy.38), channel_id=1, replica_groups=mesh['rows'=16,'cols'=8] {'cols'}, dimensions={0} | all-to-all | bytes 262144 | tf_op jit(solution)/shard_map/all_to_all | solution.py:300
  256.9 0.7 copy.43
  (88 shorter events, 6.8 us)
Async XLA Ops:
  6.5 83.9 %all-gather.2.cloned.1.call-start = ((), (), s32[]{:S(2)}) async-start(), calls=%async_computation.3 | async-start | bytes 1114112 | tf_op jit(solution)/shard_map/all_gather | solution.py:272
  7.4 15.9 %collective-permute-start = (bf16[16,2048]{1,0:T(8,128)(2,1)S(1)}, bf16[16,2048]{1,0:T(8,128)(2,1)S(1)}, u32[]{:S(2)}, u32[]{:S(2)}) collective-permute-start(bf16[16,2048]{1,0:T(8,128)(2,1)S(1)} %get-tuple-element.50), channel_id=1, source_target_pairs={{0,8},{1,9},{2,10},{3,11},{4,12},{5,13},{6,14},{7,15},{8,0},{9,1},... | collective-permute-start | bytes 196616 | tf_op jit(solution)/shard_map/ppermute | solution.py:110
  7.5 160.4 %all-reduce.3.cloned.1.call-start = ((), (), s32[]{:S(2)}) async-start(), calls=%async_computation.4 | async-start | bytes 524288 | tf_op jit(solution)/shard_map/psum | solution.py:277
  23.3 6.6 %collective-permute-start.3 = (bf16[1,2,16,2048]{3,2,1,0:T(8,128)(2,1)S(1)}, bf16[1,2,16,2048]{3,2,1,0:T(8,128)(2,1)S(1)}, u32[]{:S(2)}, u32[]{:S(2)}) collective-permute-start(bf16[1,2,16,2048]{3,2,1,0:T(8,128)(2,1)S(1)} %maximum_select_fusion), channel_id=1, source_target_pairs={{0,32},{1,33},{2,34},{3,35},{4,36},{5,37},{6,38},{7,39},{8,12},{9,... | collective-permute-start | bytes 393224 | tf_op jit(solution)/shard_map/ppermute | solution.py:110
  26.5 5.2 %collective-permute-start.2 = (bf16[1,2,16,2048]{3,2,1,0:T(8,128)(2,1)S(1)}, bf16[1,2,16,2048]{3,2,1,0:T(8,128)(2,1)S(1)}, u32[]{:S(2)}, u32[]{:S(2)}) collective-permute-start(bf16[1,2,16,2048]{3,2,1,0:T(8,128)(2,1)S(1)} %maximum_select_fusion), channel_id=1, source_target_pairs={{0,48},{1,49},{2,50},{3,51},{4,52},{5,53},{6,54},{7,55},{8,14},{9,... | collective-permute-start | bytes 393224 | tf_op jit(solution)/shard_map/ppermute | solution.py:110
  27.6 6.3 %collective-permute-start.1 = (bf16[1,2,16,2048]{3,2,1,0:T(8,128)(2,1)S(1)}, bf16[1,2,16,2048]{3,2,1,0:T(8,128)(2,1)S(1)}, u32[]{:S(2)}, u32[]{:S(2)}) collective-permute-start(bf16[1,2,16,2048]{3,2,1,0:T(8,128)(2,1)S(1)} %maximum_select_fusion), channel_id=1, source_target_pairs={{0,16},{1,17},{2,18},{3,19},{4,20},{5,21},{6,22},{7,23},{8,10},{9,... | collective-permute-start | bytes 393224 | tf_op jit(solution)/shard_map/ppermute | solution.py:110
  34.0 16.4 %collective-permute-start.6 = (bf16[1,4,2,16,2048]{4,3,2,1,0:T(8,128)(2,1)S(1)}, bf16[1,4,2,16,2048]{4,3,2,1,0:T(8,128)(2,1)S(1)}, u32[]{:S(2)}, u32[]{:S(2)}) collective-permute-start(bf16[1,4,2,16,2048]{4,3,2,1,0:T(8,128)(2,1)S(1)} %maximum_bitcast_fusion), channel_id=1, source_target_pairs={{0,4},{1,5},{2,6},{3,7},{4,0},{5,1},{6,2},{7,3},{8,72},{9,73},{10,... | collective-permute-start | bytes 1572872 | tf_op jit(solution)/shard_map/ppermute | solution.py:110
  37.3 13.4 %collective-permute-start.5 = (bf16[1,4,2,16,2048]{4,3,2,1,0:T(8,128)(2,1)S(1)}, bf16[1,4,2,16,2048]{4,3,2,1,0:T(8,128)(2,1)S(1)}, u32[]{:S(2)}, u32[]{:S(2)}) collective-permute-start(bf16[1,4,2,16,2048]{4,3,2,1,0:T(8,128)(2,1)S(1)} %maximum_bitcast_fusion), channel_id=1, source_target_pairs={{0,6},{1,7},{2,0},{3,1},{4,2},{5,3},{6,4},{7,5},{8,73},{9,8},{10,7... | collective-permute-start | bytes 1572872 | tf_op jit(solution)/shard_map/ppermute | solution.py:110
  38.3 12.4 %collective-permute-start.4 = (bf16[1,4,2,16,2048]{4,3,2,1,0:T(8,128)(2,1)S(1)}, bf16[1,4,2,16,2048]{4,3,2,1,0:T(8,128)(2,1)S(1)}, u32[]{:S(2)}, u32[]{:S(2)}) collective-permute-start(bf16[1,4,2,16,2048]{4,3,2,1,0:T(8,128)(2,1)S(1)} %maximum_bitcast_fusion), channel_id=1, source_target_pairs={{0,2},{1,3},{2,4},{3,5},{4,6},{5,7},{6,0},{7,1},{8,9},{9,72},{10,1... | collective-permute-start | bytes 1572872 | tf_op jit(solution)/shard_map/ppermute | solution.py:110
  52.3 28.4 %collective-permute-start.8 = (bf16[4,4,2,16,2048]{4,3,2,1,0:T(8,128)(2,1)}, bf16[4,4,2,16,2048]{4,3,2,1,0:T(8,128)(2,1)}, u32[]{:S(2)}, u32[]{:S(2)}) collective-permute-start(bf16[4,4,2,16,2048]{4,3,2,1,0:T(8,128)(2,1)} %pad_maximum_fusion), channel_id=1, source_target_pairs={{0,1},{1,64},{2,3},{3,66},{4,5},{5,68},{6,7},{7,70},{8,24},{9,25},... | collective-permute-start | bytes 6291464 | tf_op jit(solution)/shard_map/ppermute | solution.py:110
  54.4 28.7 %collective-permute-start.10 = (bf16[4,4,2,16,2048]{4,3,2,1,0:T(8,128)(2,1)}, bf16[4,4,2,16,2048]{4,3,2,1,0:T(8,128)(2,1)}, u32[]{:S(2)}, u32[]{:S(2)}) collective-permute-start(bf16[4,4,2,16,2048]{4,3,2,1,0:T(8,128)(2,1)} %pad_maximum_fusion), channel_id=1, source_target_pairs={{0,65},{1,0},{2,67},{3,2},{4,69},{5,4},{6,71},{7,6},{8,56},{9,57},... | collective-permute-start | bytes 6291464 | tf_op jit(solution)/shard_map/ppermute | solution.py:110
  79.1 10.1 %copy-start.5 = (s32[512]{0:T(512)S(1)}, s32[512]{0:T(512)}, u32[]{:S(2)}) copy-start(s32[512]{0:T(512)} %param.11) | copy-start | bytes 6148
  79.1 10.7 %copy-start.6 = (s32[512]{0:T(512)S(1)}, s32[512]{0:T(512)}, u32[]{:S(2)}) copy-start(s32[512]{0:T(512)} %param.10) | copy-start | bytes 6148
  83.0 16.2 %collective-permute-start.12 = (bf16[2,4,2,16,2048]{4,3,2,1,0:T(8,128)(2,1)}, bf16[2,4,2,16,2048]{4,3,2,1,0:T(8,128)(2,1)S(1)}, u32[]{:S(2)}, u32[]{:S(2)}) collective-permute-start(bf16[2,4,2,16,2048]{4,3,2,1,0:T(8,128)(2,1)} %slice.83), channel_id=1, source_target_pairs={{0,1},{1,64},{2,3},{3,66},{4,5},{5,68},{6,7},{7,70},{8,24},{9,25},... | collective-permute-start | bytes 3145736 | tf_op jit(solution)/shard_map/ppermute | solution.py:110
  85.3 15.8 %collective-permute-start.14 = (bf16[2,4,2,16,2048]{4,3,2,1,0:T(8,128)(2,1)}, bf16[2,4,2,16,2048]{4,3,2,1,0:T(8,128)(2,1)}, u32[]{:S(2)}, u32[]{:S(2)}) collective-permute-start(bf16[2,4,2,16,2048]{4,3,2,1,0:T(8,128)(2,1)} %slice.84), channel_id=1, source_target_pairs={{0,65},{1,0},{2,67},{3,2},{4,69},{5,4},{6,71},{7,6},{8,56},{9,57},... | collective-permute-start | bytes 3145736 | tf_op jit(solution)/shard_map/ppermute | solution.py:110
  89.2 32.9 %collective-permute-start.7 = (bf16[16,2,16,2048]{3,2,1,0:T(8,128)(2,1)}, bf16[16,2,16,2048]{3,2,1,0:T(8,128)(2,1)}, u32[]{:S(2)}, u32[]{:S(2)}) collective-permute-start(bf16[16,2,16,2048]{3,2,1,0:T(8,128)(2,1)} %bitcast.8.p0), channel_id=1, source_target_pairs={{0,8},{1,9},{2,10},{3,11},{4,12},{5,13},{6,14},{7,15},{8,0},{9,1},... | collective-permute-start | bytes 6291464 | tf_op jit(solution)/shard_map/ppermute | solution.py:110
  89.2 32.9 %collective-permute-start.9 = (bf16[16,2,16,2048]{3,2,1,0:T(8,128)(2,1)}, bf16[16,2,16,2048]{3,2,1,0:T(8,128)(2,1)}, u32[]{:S(2)}, u32[]{:S(2)}) collective-permute-start(bf16[16,2,16,2048]{3,2,1,0:T(8,128)(2,1)} %bitcast.9.p1), channel_id=1, source_target_pairs={{0,8},{1,9},{2,10},{3,11},{4,12},{5,13},{6,14},{7,15},{8,0},{9,1},... | collective-permute-start | bytes 6291464 | tf_op jit(solution)/shard_map/ppermute | solution.py:110
  89.7 32.4 %collective-permute-start.11 = (bf16[16,2,16,2048]{3,2,1,0:T(8,128)(2,1)}, bf16[16,2,16,2048]{3,2,1,0:T(8,128)(2,1)}, u32[]{:S(2)}, u32[]{:S(2)}) collective-permute-start(bf16[16,2,16,2048]{3,2,1,0:T(8,128)(2,1)} %bitcast.10.p2), channel_id=1, source_target_pairs={{0,8},{1,9},{2,10},{3,11},{4,12},{5,13},{6,14},{7,15},{8,0},{9,1},... | collective-permute-start | bytes 6291464 | tf_op jit(solution)/shard_map/ppermute | solution.py:110
  90.4 3.0 %copy-start = (bf16[2048,256]{0,1:T(8,128)(2,1)S(1)}, bf16[2048,256]{0,1:T(8,128)(2,1)}, u32[]{:S(2)}) copy-start(bf16[2048,256]{0,1:T(8,128)(2,1)} %all-gather.2.cloned.1.call-done) | copy-start | bytes 3145732
  99.2 2.0 copy-start.1
  99.2 22.9 %collective-permute-start.13 = (bf16[8,2,16,2048]{3,2,1,0:T(8,128)(2,1)S(1)}, bf16[8,2,16,2048]{3,2,1,0:T(8,128)(2,1)S(1)}, u32[]{:S(2)}, u32[]{:S(2)}) collective-permute-start(bf16[8,2,16,2048]{3,2,1,0:T(8,128)(2,1)S(1)} %bitcast.75), channel_id=1, source_target_pairs={{0,8},{1,9},{2,10},{3,11},{4,12},{5,13},{6,14},{7,15},{8,0},{9,1},... | collective-permute-start | bytes 3145736 | tf_op jit(solution)/shard_map/ppermute | solution.py:110
  101.2 21.0 %collective-permute-start.15 = (bf16[8,2,16,2048]{3,2,1,0:T(8,128)(2,1)}, bf16[8,2,16,2048]{3,2,1,0:T(8,128)(2,1)S(1)}, u32[]{:S(2)}, u32[]{:S(2)}) collective-permute-start(bf16[8,2,16,2048]{3,2,1,0:T(8,128)(2,1)} %bitcast.12.p4), channel_id=1, source_target_pairs={{0,8},{1,9},{2,10},{3,11},{4,12},{5,13},{6,14},{7,15},{8,0},{9,1},... | collective-permute-start | bytes 3145736 | tf_op jit(solution)/shard_map/ppermute | solution.py:110
  122.1 1.1 copy-start.2
  122.1 1.4 copy-start.3
  145.7 4.9 %copy-start.4 = (f32[256,256]{1,0:T(8,128)S(1)}, f32[256,256]{1,0:T(8,128)}, u32[]{:S(2)}) copy-start(f32[256,256]{1,0:T(8,128)} %get-tuple-element.27) | copy-start | bytes 786436
  145.7 83.8 %all-to-all-start = ((f32[8,128,256]{2,1,0:T(8,128)}), f32[8,128,256]{2,1,0:T(8,128)S(1)}, u32[]{:S(2)}, u32[]{:S(2)}) async-start(f32[8,128,256]{2,1,0:T(8,128)} %bitcast.77), calls=%async_computation | async-start | bytes 2097152 | tf_op jit(solution)/shard_map/all_to_all | solution.py:297
Sparse Core Ops, SparseCore 0:
  9.8 49.0 all-gather.1
  93.5 74.3 all-reduce.2

commit v3 on v2

--- a/solution.py
+++ b/solution.py
@@ -17,6 +17,7 @@
 PITCH = 24
 PARTS = 4
 STEP = 8
+TOLERANCE = 3e-4
 AXES = ("rows", "cols")
 SHIFTS = (1, -1, 2)
 
@@ -251,6 +252,88 @@
     )(table, head, rest, *pieces, *more)
 
 
+def exact(a, b, dims):
+    return lax.dot_general(a, b, dims, precision=lax.Precision.HIGHEST, preferred_element_type=F32)
+
+
+def inverse_kernel(gram_ref, out_ref, ok_ref, a_ref, x_ref, r_ref):
+    n = gram_ref.shape[0]
+    at_row = lax.broadcasted_iota(jnp.int32, (n, n), 0)
+    at_col = lax.broadcasted_iota(jnp.int32, (n, n), 1)
+    eye = jnp.where(at_row == at_col, 1.0, 0.0)
+    gram = gram_ref[...]
+    diagonal = gram * eye
+    by_row = lax.rsqrt(jnp.sum(diagonal, 1, keepdims=True))
+    by_col = lax.rsqrt(jnp.sum(diagonal, 0, keepdims=True))
+    a = gram * by_row * by_col
+    bound = jnp.max(jnp.sum(jnp.abs(a), 0, keepdims=True))
+    start = jnp.where(bound < 1.9, 1.0, 1.0 / bound)
+    a_ref[...] = a
+    x_ref[...] = start * eye
+    r_ref[...] = eye - start * a
+
+    def size(r):
+        return jnp.sqrt(jnp.sum(r * r))
+
+    def unfinished(state):
+        i, now, before = state
+        stuck = (now < 0.3) & (now > 0.5 * before)
+        return (now > TOLERANCE) & (i < 40) & jnp.logical_not(stuck)
+
+    def improve(state):
+        i, now, _ = state
+        x = x_ref[...] + exact(x_ref[...], r_ref[...], NN)
+        r = eye - exact(a_ref[...], x, NN)
+        x_ref[...] = x
+        r_ref[...] = r
+        return i + 1, size(r), now
+
+    last = lax.while_loop(unfinished, improve, (0, size(r_ref[...]), jnp.float32(1e30)))
+    x = x_ref[...] + exact(x_ref[...], r_ref[...], NN)
+    out_ref[...] = x * by_row * by_col
+    ok_ref[0] = jnp.where(last[1] <= TOLERANCE, 1, 0)
+
+
+def inverse(gram):
+    n = gram.shape[0]
+    made, ok = pl.pallas_call(
+        inverse_kernel,
+        out_shape=[jax.ShapeDtypeStruct((n, n), F32), jax.ShapeDtypeStruct((1,), jnp.int32)],
+        out_specs=[
+            pl.BlockSpec(memory_space=pltpu.VMEM),
+            pl.BlockSpec(memory_space=pltpu.SMEM),
+        ],
+        scratch_shapes=[pltpu.VMEM((n, n), F32)] * 3,
+        cost_estimate=pl.CostEstimate(
+            flops=5_000_000_000, bytes_accessed=600_000, transcendentals=0
+        ),
+    )(gram)
+
+    def by_factor():
+        factor = jnp.linalg.cholesky(gram)
+        return jax.scipy.linalg.cho_solve((factor, True), jnp.eye(n, dtype=F32))
+
+    return lax.cond(ok[0] == 1, lambda: made, by_factor)
+
+
+def solve_kernel(inverse_ref, spread_ref, out_ref):
+    total = spread_ref[0]
+    for i in range(1, spread_ref.shape[0]):
+        total = total + spread_ref[i]
+    out_ref[...] = exact(inverse_ref[...], total, NT).reshape(out_ref.shape)
+
+
+def solve(inverted, spread):
+    n, rows = inverted.shape[0], spread.shape[1]
+    return pl.pallas_call(
+        solve_kernel,
+        out_shape=jax.ShapeDtypeStruct((n // 16, 16, rows), F32),
+        cost_estimate=pl.CostEstimate(
+            flops=500_000_000, bytes_accessed=1_500_000, transcendentals=0
+        ),
+    )(inverted, spread)
+
+
 def per_device(
     block_values,
     block_length,
@@ -274,7 +357,8 @@
     own, swapped = gather_table(third_factor.T, core)
 
     contract = (((0,), (0,)), ((), ()))
-    gram_second = lax.psum(dot(second_range, second_range, contract), "cols")
+    local_gram = dot(second_range, second_range, contract)
+    gram_second = lax.psum(local_gram, "cols")
 
     lane = jnp.arange(width, dtype=jnp.int32)
     slot = jnp.arange(nblk, dtype=jnp.int32)
@@ -294,20 +378,13 @@
         gram_third / (third_factor.shape[0] * n_cols)
     )
     spread = part.reshape(n_cols, slab // n_cols, -1)
-    mine = jnp.sum(lax.all_to_all(spread, "cols", 0, 0, tiled=True), 0)
-    factor = jnp.linalg.cholesky(gram)
-    solved = jax.scipy.linalg.cho_solve((factor, True), mine.T).T
-    moved = lax.all_to_all(
-        lax.all_to_all(solved, "rows", split_axis=1, concat_axis=0, tiled=True),
-        "cols",
-        split_axis=0,
-        concat_axis=0,
-        tiled=True,
-    )
+    spread = lax.all_to_all(spread, "cols", 0, 0, tiled=True)
+    solved = solve(inverse(gram), spread)
+    moved = lax.all_to_all(solved, "rows", 0, 0, tiled=True)
     share = n_rows // n_cols
-    owned_rows = mine.shape[0]
-    reordered = moved.reshape(n_cols, share, owned_rows, moved.shape[1]).transpose(1, 0, 2, 3)
-    return reordered.reshape(n_rows * owned_rows, moved.shape[1])
+    moved = moved.reshape(n_cols, share, *solved.shape[1:])
+    moved = lax.all_to_all(moved, "cols", 0, 0, tiled=True)
+    return moved.transpose(1, 0, 3, 2).reshape(range_rows, solved.shape[1])
 
 
 def solution(mesh):

time: 265 us -> 231 us (0.87)
  other arithmetic: 63.2 us -> 8.53 us
  waiting for transfers between devices: 28.5 us -> 44.5 us
  Pallas kernels: 87.4 us -> 99.4 us
  local copies, waits for them, and re-layouts: 15.8 us -> 12.2 us
    another operation x11 -> x0, other arithmetic: 54.5 us -> none  [the longest x7 34.6 us: per_device(): factor = jnp.linalg.cholesky(gram)]
    pallas_call x0 -> x2, Pallas kernels: none -> 12.1 us  [the longest x1 9.79 us: inverse(): pl.pallas_call(inverse_kernel, out_shape=[jax.ShapeDtypeStruct((n, n), F3...]
    ppermute x16, waiting for transfers between devices: 11.2 us -> 22.1 us  [shifted(): return lax.ppermute(value, AXES, pairs)]
    psum x1, waiting for transfers between devices: 17.2 us -> 22.4 us  [per_device(): gram_second = lax.psum(local_gram, 'cols')]
    another operation x9 -> x0, local copies, waits for them, and re-layouts: 3.98 us -> none
  transfers between devices with their start and end apart: 19 -> 19, of which waited for: 8 -> 10; matrix products, arithmetic and copies ran while one was open for 30% -> 9% of each run, Pallas kernels for 33% -> 42%
where the time goes in v3:
time: 231 us; the launch traced here: 230 us
  Pallas kernels  99.4 us (43%)
  waiting for transfers between devices  44.5 us (19%)
  blocking collectives  25.1 us (11%)
  starting transfers between devices  22.7 us (10%)
  between operations  14.9 us (6%)
  local copies, waits for them, and re-layouts  12.2 us (5%)
  other arithmetic  8.53 us (4%)
  matrix products  2.83 us (1%)
    pallas_call x4, Pallas kernels, build(): made = call(hi, lo, v, *made)  44.3 us
    pallas_call x2, Pallas kernels, product(): pl.pallas_call(second_kernel if more else first_kernel, grid_spec=pltpu.P...  43.1 us
    psum x1, waiting for transfers between devices, per_device(): gram_second = lax.psum(local_gram, 'cols')  22.4 us
    ppermute x16, waiting for transfers between devices, shifted(): return lax.ppermute(value, AXES, pairs)  22.1 us
    ppermute x16, starting transfers between devices, shifted(): return lax.ppermute(value, AXES, pairs)  18.9 us
    all_to_all x1, blocking collectives, per_device(): moved = lax.all_to_all(solved, 'rows', 0, 0, tiled=True)  14.9 us
    all_to_all x1, blocking collectives, per_device(): moved = lax.all_to_all(moved, 'cols', 0, 0, tiled=True)  10.2 us
    pallas_call x1, Pallas kernels, inverse(): pl.pallas_call(inverse_kernel, out_shape=[jax.ShapeDtypeStruct((n, n), F3...  9.79 us
  transfers between devices with their start and end apart: 19, of which 10 were waited for; matrix products, arithmetic and copies ran while one was open for 9% of the time, Pallas kernels for 42%

profile of v3, /device:TPU:0, one launch (start us, length us, event | category | flops | bytes accessed | tf_op | source)
XLA Modules:
  0.0 230.5 jit_solution(4035546651338165363)
XLA Ops:
  6.5 0.9 dynamic-slice_bitcast_fusion.1
  7.6 2.0 fusion.12
  10.3 1.8 fusion.17.v_ref
  12.1 11.0 %shard_map.82 = (bf16[128,512,256]{2,1,0:T(8,128)(2,1)}, bf16[128,512,256]{2,1,0:T(8,128)(2,1)}) custom-call(f32[512,128]{1,0:T(8,128)} %get-tuple-element.66.hi_ref, f32[512,128]{1,0:T(8,128)} %get-tuple-element.65.lo_ref, f32[512,128]{1,0:T(8,128)} %fusion.17.v_ref), custom_call_target="tpu_custom_call" | custom-call | flops 10000000000 | bytes 16777216 | tf_op jit(solution)/shard_map/pallas_call | solution.py:87
  23.1 11.1 %shard_map.83 = (bf16[128,512,256]{2,1,0:T(8,128)(2,1)}, bf16[128,512,256]{2,1,0:T(8,128)(2,1)}) custom-call(f32[512,128]{1,0:T(8,128)} %get-tuple-element.66.hi_ref, f32[512,128]{1,0:T(8,128)} %get-tuple-element.65.lo_ref, f32[512,128]{1,0:T(8,128)} %fusion.17.v_ref, ...), custom_call_target="tpu_custom_call", output_to_operand_aliasing={{0}: (3, {}), {1}: (4, {})} | custom-call | flops 10000000000 | bytes 16777216 | tf_op jit(solution)/shard_map/pallas_call | solution.py:87
  34.3 1.7 collective-permute-start.1
  36.0 1.6 collective-permute-start.2
  37.6 2.0 collective-permute-start.3
  39.5 1.0 collective-permute-done.1
  40.5 0.4 collective-permute-done.2
  40.9 3.1 %collective-permute-done.3 = bf16[1,2,16,2048]{3,2,1,0:T(8,128)(2,1)S(1)} collective-permute-done((bf16[1,2,16,2048]{3,2,1,0:T(8,128)(2,1)S(1)}, bf16[1,2,16,2048]{3,2,1,0:T(8,128)(2,1)S(1)}, u32[]{:S(2)}, u32[]{:S(2)}) %collective-permute-start.3) | collective-permute-done | bytes 131104 | tf_op jit(solution)/shard_map/ppermute | solution.py:111
  44.1 1.8 collective-permute-start.4
  45.9 1.5 collective-permute-start.5
  47.4 2.1 collective-permute-start.6
  49.6 5.0 %collective-permute-done.4 = bf16[1,4,2,16,2048]{4,3,2,1,0:T(8,128)(2,1)S(1)} collective-permute-done((bf16[1,4,2,16,2048]{4,3,2,1,0:T(8,128)(2,1)S(1)}, bf16[1,4,2,16,2048]{4,3,2,1,0:T(8,128)(2,1)S(1)}, u32[]{:S(2)}, u32[]{:S(2)}) %collective-permute-start.4) | collective-permute-done | bytes 524320 | tf_op jit(solution)/shard_map/ppermute | solution.py:111
  54.6 0.5 collective-permute-done.5
  55.1 6.5 %collective-permute-done.6 = bf16[1,4,2,16,2048]{4,3,2,1,0:T(8,128)(2,1)S(1)} collective-permute-done((bf16[1,4,2,16,2048]{4,3,2,1,0:T(8,128)(2,1)S(1)}, bf16[1,4,2,16,2048]{4,3,2,1,0:T(8,128)(2,1)S(1)}, u32[]{:S(2)}, u32[]{:S(2)}) %collective-permute-start.6) | collective-permute-done | bytes 524320 | tf_op jit(solution)/shard_map/ppermute | solution.py:111
  61.5 1.6 pad_maximum_fusion.1
  63.1 2.0 collective-permute-start.8
  65.1 2.3 %collective-permute-start.10 = (bf16[4,4,2,16,2048]{4,3,2,1,0:T(8,128)(2,1)}, bf16[4,4,2,16,2048]{4,3,2,1,0:T(8,128)(2,1)}, u32[]{:S(2)}, u32[]{:S(2)}) collective-permute-start(bf16[4,4,2,16,2048]{4,3,2,1,0:T(8,128)(2,1)} %pad_maximum_fusion.1), channel_id=1, source_target_pairs={{0,65},{1,0},{2,67},{3,2},{4,69},{5,4},{6,71},{7,6},{8,56},{9,57},... | collective-permute-start | bytes 6291464 | tf_op jit(solution)/shard_map/ppermute | solution.py:111
  67.4 11.1 %shard_map.84 = (bf16[128,512,256]{2,1,0:T(8,128)(2,1)}, bf16[128,512,256]{2,1,0:T(8,128)(2,1)}) custom-call(f32[512,128]{1,0:T(8,128)} %get-tuple-element.66.hi_ref, f32[512,128]{1,0:T(8,128)} %get-tuple-element.65.lo_ref, f32[512,128]{1,0:T(8,128)} %fusion.17.v_ref, ...), custom_call_target="tpu_custom_call", output_to_operand_aliasing={{0}: (3, {}), {1}: (4, {})} | custom-call | flops 10000000000 | bytes 16777216 | tf_op jit(solution)/shard_map/pallas_call | solution.py:87
  79.2 11.1 %shard_map.85 = (bf16[128,512,256]{2,1,0:T(8,128)(2,1)}, bf16[128,512,256]{2,1,0:T(8,128)(2,1)}) custom-call(f32[512,128]{1,0:T(8,128)} %get-tuple-element.66.hi_ref, f32[512,128]{1,0:T(8,128)} %get-tuple-element.65.lo_ref, f32[512,128]{1,0:T(8,128)} %fusion.17.v_ref, ...), custom_call_target="tpu_custom_call", output_to_operand_aliasing={{0}: (3, {}), {1}: (4, {})} | custom-call | flops 10000000000 | bytes 16777216 | tf_op jit(solution)/shard_map/pallas_call | solution.py:87
  90.3 1.5 collective-permute-done.8
  91.7 2.3 slice.84
  94.0 2.3 %slice.85 = bf16[2,4,2,16,2048]{4,3,2,1,0:T(8,128)(2,1)} slice(bf16[4,4,2,16,2048]{4,3,2,1,0:T(8,128)(2,1)} %collective-permute-done.10), slice={[2:4], [0:4], [0:2], [0:16], [0:2048]} | slice | bytes 2097152 | tf_op jit(solution)/shard_map/slice | solution.py:137
  96.3 3.2 %collective-permute-start.14 = (bf16[2,4,2,16,2048]{4,3,2,1,0:T(8,128)(2,1)}, bf16[2,4,2,16,2048]{4,3,2,1,0:T(8,128)(2,1)}, u32[]{:S(2)}, u32[]{:S(2)}) collective-permute-start(bf16[2,4,2,16,2048]{4,3,2,1,0:T(8,128)(2,1)} %slice.85), channel_id=1, source_target_pairs={{0,65},{1,0},{2,67},{3,2},{4,69},{5,4},{6,71},{7,6},{8,56},{9,57},... | collective-permute-start | bytes 3145736 | tf_op jit(solution)/shard_map/ppermute | solution.py:111
  99.6 0.7 pad_add_fusion.1.table
  100.3 0.5 collective-permute-start.11
  100.8 0.6 pad_add_fusion.table
  101.5 0.6 broadcast_subtract_fusion
  102.1 2.8 %fusion.25 = f32[256,256]{1,0:T(8,128)} fusion(bf16[2048,256]{0,1:T(8,128)(2,1)} %all-gather.2.cloned.1.call-done), kind=kOutput, calls=%fused_computation.87 | convolution fusion | flops 268435456 | bytes 1310720 | tf_op jit(solution)/shard_map/dot_general | solution.py:26
  104.9 0.5 copy.20
  105.5 2.6 %gather_fusion = bf16[512,256]{1,0:T(8,128)(2,1)} fusion(bf16[2048,256]{1,0:T(8,128)(2,1)S(1)} %copy.20, s32[1024]{0:T(1024)S(1)} %pad_clamp_fusion), kind=kCustom, calls=%fused_computation | custom fusion | bytes 526336 | tf_op jit(solution)/shard_map/gather | solution.py:370
  108.0 2.2 collective-permute-done.12
  110.2 2.0 collective-permute-done.14
  112.2 20.9 %shard_map.86 = (f32[512,256]{1,0:T(8,128)}, f32[256,256]{1,0:T(8,128)}) custom-call(s32[129]{0:T(256)} %pad_add_fusion.1.table, bf16[128,512,256]{2,1,0:T(8,128)(2,1)} %get-tuple-element.30.head_ref, bf16[128,512,256]{2,1,0:T(8,128)(2,1)} %get-tuple-element.31.rest_ref, bf16[16,2,16,2048]{3,2,1,0:T(8,128)(2,1)} %bitcast.13.p0, ...), custom_call_target="tpu_custom_call" | custom-call | flops 15000000512 | bytes 50000000 | tf_op jit(solution)/shard_map/pallas_call | solution.py:239
  133.2 0.9 copy-done.2
  134.1 0.4 copy-done.3
  134.4 22.2 %shard_map.87 = (f32[1024,256]{1,0:T(8,128)}, f32[256,256]{1,0:T(8,128)}) custom-call(s32[129]{0:T(256)} %pad_add_fusion.table, bf16[128,512,256]{2,1,0:T(8,128)(2,1)} %get-tuple-element.30.head_ref, bf16[128,512,256]{2,1,0:T(8,128)(2,1)} %get-tuple-element.31.rest_ref, bf16[16,2,16,2048]{3,2,1,0:T(8,128)(2,1)} %collective-permute-done.7.p0, ...), custom_call_target="tpu_custom_call" | custom-call | flops 15000000512 | bytes 50000000 | tf_op jit(solution)/shard_map/pallas_call | solution.py:239
  156.6 3.7 %all-to-all-start = ((f32[8,128,256]{2,1,0:T(8,128)}), f32[8,128,256]{2,1,0:T(8,128)S(1)}, u32[]{:S(2)}, u32[]{:S(2)}) async-start(f32[8,128,256]{2,1,0:T(8,128)} %bitcast.70), calls=%async_computation | async-start | bytes 2097152 | tf_op jit(solution)/shard_map/all_to_all | solution.py:381
  160.4 22.4 %all-reduce.3.cloned.1.call-done = f32[256,256]{1,0:T(8,128)} async-done(((f32[256,256]{1,0:T(8,128)}), f32[256,256]{1,0:T(8,128)}) %all-reduce.3.cloned.1.call-update) | async-done | bytes 262160 | tf_op jit(solution)/shard_map/psum | solution.py:361
  182.8 1.0 multiply_multiply_fusion.gram_ref
  183.7 9.8 %shard_map.88 = (f32[256,256]{1,0:T(8,128)S(1)}, s32[1]{0:T(128)}) custom-call(f32[256,256]{1,0:T(8,128)S(1)} %multiply_multiply_fusion.gram_ref), custom_call_target="tpu_custom_call" | custom-call | flops 5000000000 | bytes 600000 | tf_op jit(solution)/shard_map/pallas_call | solution.py:299
  194.5 1.0 copy-done.4
  195.5 2.3 shard_map.89
  197.7 14.9 %all_to_all.15 = f32[16,16,128]{2,1,0:T(8,128)S(1)} all-to-all(f32[16,16,128]{2,1,0:T(8,128)} %shard_map.89), channel_id=1, replica_groups=mesh['rows'=16,'cols'=8] {'rows'}, dimensions={0} | all-to-all | bytes 262144 | tf_op jit(solution)/shard_map/all_to_all | solution.py:383
  212.6 10.2 %all_to_all.16 = f32[8,2,16,128]{3,2,1,0:T(8,128)S(1)} all-to-all(f32[8,2,16,128]{3,2,1,0:T(8,128)S(1)} %bitcast.71), channel_id=1, replica_groups=mesh['rows'=16,'cols'=8] {'cols'}, dimensions={0} | all-to-all | bytes 262144 | tf_op jit(solution)/shard_map/all_to_all | solution.py:386
  222.9 0.7 copy.26
  (54 shorter events, 1.5 us)
Async XLA Ops:
  6.5 95.5 %all-gather.2.cloned.1.call-start = ((), (), s32[]{:S(2)}) async-start(), calls=%async_computation.3 | async-start | bytes 1114112 | tf_op jit(solution)/shard_map/all_gather | solution.py:355
  7.4 26.8 %collective-permute-start = (bf16[16,2048]{1,0:T(8,128)(2,1)S(1)}, bf16[16,2048]{1,0:T(8,128)(2,1)S(1)}, u32[]{:S(2)}, u32[]{:S(2)}) collective-permute-start(bf16[16,2048]{1,0:T(8,128)(2,1)S(1)} %get-tuple-element.68), channel_id=1, source_target_pairs={{0,8},{1,9},{2,10},{3,11},{4,12},{5,13},{6,14},{7,15},{8,0},{9,1},... | collective-permute-start | bytes 196616 | tf_op jit(solution)/shard_map/ppermute | solution.py:111
  7.5 175.2 %all-reduce.3.cloned.1.call-start = ((), (), s32[]{:S(2)}) async-start(), calls=%async_computation.4 | async-start | bytes 524288 | tf_op jit(solution)/shard_map/psum | solution.py:361
  34.3 6.2 %collective-permute-start.1 = (bf16[1,2,16,2048]{3,2,1,0:T(8,128)(2,1)S(1)}, bf16[1,2,16,2048]{3,2,1,0:T(8,128)(2,1)S(1)}, u32[]{:S(2)}, u32[]{:S(2)}) collective-permute-start(bf16[1,2,16,2048]{3,2,1,0:T(8,128)(2,1)S(1)} %maximum_select_fusion), channel_id=1, source_target_pairs={{0,16},{1,17},{2,18},{3,19},{4,20},{5,21},{6,22},{7,23},{8,10},{9,... | collective-permute-start | bytes 393224 | tf_op jit(solution)/shard_map/ppermute | solution.py:111
  36.0 5.0 %collective-permute-start.2 = (bf16[1,2,16,2048]{3,2,1,0:T(8,128)(2,1)S(1)}, bf16[1,2,16,2048]{3,2,1,0:T(8,128)(2,1)S(1)}, u32[]{:S(2)}, u32[]{:S(2)}) collective-permute-start(bf16[1,2,16,2048]{3,2,1,0:T(8,128)(2,1)S(1)} %maximum_select_fusion), channel_id=1, source_target_pairs={{0,48},{1,49},{2,50},{3,51},{4,52},{5,53},{6,54},{7,55},{8,14},{9,... | collective-permute-start | bytes 393224 | tf_op jit(solution)/shard_map/ppermute | solution.py:111
  37.6 6.5 %collective-permute-start.3 = (bf16[1,2,16,2048]{3,2,1,0:T(8,128)(2,1)S(1)}, bf16[1,2,16,2048]{3,2,1,0:T(8,128)(2,1)S(1)}, u32[]{:S(2)}, u32[]{:S(2)}) collective-permute-start(bf16[1,2,16,2048]{3,2,1,0:T(8,128)(2,1)S(1)} %maximum_select_fusion), channel_id=1, source_target_pairs={{0,32},{1,33},{2,34},{3,35},{4,36},{5,37},{6,38},{7,39},{8,12},{9,... | collective-permute-start | bytes 393224 | tf_op jit(solution)/shard_map/ppermute | solution.py:111
  44.1 10.5 %collective-permute-start.4 = (bf16[1,4,2,16,2048]{4,3,2,1,0:T(8,128)(2,1)S(1)}, bf16[1,4,2,16,2048]{4,3,2,1,0:T(8,128)(2,1)S(1)}, u32[]{:S(2)}, u32[]{:S(2)}) collective-permute-start(bf16[1,4,2,16,2048]{4,3,2,1,0:T(8,128)(2,1)S(1)} %maximum_bitcast_fusion), channel_id=1, source_target_pairs={{0,2},{1,3},{2,4},{3,5},{4,6},{5,7},{6,0},{7,1},{8,9},{9,72},{10,1... | collective-permute-start | bytes 1572872 | tf_op jit(solution)/shard_map/ppermute | solution.py:111
  45.9 9.2 %collective-permute-start.5 = (bf16[1,4,2,16,2048]{4,3,2,1,0:T(8,128)(2,1)S(1)}, bf16[1,4,2,16,2048]{4,3,2,1,0:T(8,128)(2,1)S(1)}, u32[]{:S(2)}, u32[]{:S(2)}) collective-permute-start(bf16[1,4,2,16,2048]{4,3,2,1,0:T(8,128)(2,1)S(1)} %maximum_bitcast_fusion), channel_id=1, source_target_pairs={{0,6},{1,7},{2,0},{3,1},{4,2},{5,3},{6,4},{7,5},{8,73},{9,8},{10,7... | collective-permute-start | bytes 1572872 | tf_op jit(solution)/shard_map/ppermute | solution.py:111
  47.4 14.1 %collective-permute-start.6 = (bf16[1,4,2,16,2048]{4,3,2,1,0:T(8,128)(2,1)S(1)}, bf16[1,4,2,16,2048]{4,3,2,1,0:T(8,128)(2,1)S(1)}, u32[]{:S(2)}, u32[]{:S(2)}) collective-permute-start(bf16[1,4,2,16,2048]{4,3,2,1,0:T(8,128)(2,1)S(1)} %maximum_bitcast_fusion), channel_id=1, source_target_pairs={{0,4},{1,5},{2,6},{3,7},{4,0},{5,1},{6,2},{7,3},{8,72},{9,73},{10,... | collective-permute-start | bytes 1572872 | tf_op jit(solution)/shard_map/ppermute | solution.py:111
  63.1 28.6 %collective-permute-start.8 = (bf16[4,4,2,16,2048]{4,3,2,1,0:T(8,128)(2,1)}, bf16[4,4,2,16,2048]{4,3,2,1,0:T(8,128)(2,1)}, u32[]{:S(2)}, u32[]{:S(2)}) collective-permute-start(bf16[4,4,2,16,2048]{4,3,2,1,0:T(8,128)(2,1)} %pad_maximum_fusion.1), channel_id=1, source_target_pairs={{0,1},{1,64},{2,3},{3,66},{4,5},{5,68},{6,7},{7,70},{8,24},{9,25},... | collective-permute-start | bytes 6291464 | tf_op jit(solution)/shard_map/ppermute | solution.py:111
  65.1 28.9 %collective-permute-start.10 = (bf16[4,4,2,16,2048]{4,3,2,1,0:T(8,128)(2,1)}, bf16[4,4,2,16,2048]{4,3,2,1,0:T(8,128)(2,1)}, u32[]{:S(2)}, u32[]{:S(2)}) collective-permute-start(bf16[4,4,2,16,2048]{4,3,2,1,0:T(8,128)(2,1)} %pad_maximum_fusion.1), channel_id=1, source_target_pairs={{0,65},{1,0},{2,67},{3,2},{4,69},{5,4},{6,71},{7,6},{8,56},{9,57},... | collective-permute-start | bytes 6291464 | tf_op jit(solution)/shard_map/ppermute | solution.py:111
  90.3 10.0 %copy-start.6 = (s32[512]{0:T(512)S(1)}, s32[512]{0:T(512)}, u32[]{:S(2)}) copy-start(s32[512]{0:T(512)} %param.13) | copy-start | bytes 6148
  90.3 11.2 %copy-start.7 = (s32[512]{0:T(512)S(1)}, s32[512]{0:T(512)}, u32[]{:S(2)}) copy-start(s32[512]{0:T(512)} %param.12) | copy-start | bytes 6148
  94.0 16.2 %collective-permute-start.12 = (bf16[2,4,2,16,2048]{4,3,2,1,0:T(8,128)(2,1)}, bf16[2,4,2,16,2048]{4,3,2,1,0:T(8,128)(2,1)S(1)}, u32[]{:S(2)}, u32[]{:S(2)}) collective-permute-start(bf16[2,4,2,16,2048]{4,3,2,1,0:T(8,128)(2,1)} %slice.84), channel_id=1, source_target_pairs={{0,1},{1,64},{2,3},{3,66},{4,5},{5,68},{6,7},{7,70},{8,24},{9,25},... | collective-permute-start | bytes 3145736 | tf_op jit(solution)/shard_map/ppermute | solution.py:111
  96.3 15.9 %collective-permute-start.14 = (bf16[2,4,2,16,2048]{4,3,2,1,0:T(8,128)(2,1)}, bf16[2,4,2,16,2048]{4,3,2,1,0:T(8,128)(2,1)}, u32[]{:S(2)}, u32[]{:S(2)}) collective-permute-start(bf16[2,4,2,16,2048]{4,3,2,1,0:T(8,128)(2,1)} %slice.85), channel_id=1, source_target_pairs={{0,65},{1,0},{2,67},{3,2},{4,69},{5,4},{6,71},{7,6},{8,56},{9,57},... | collective-permute-start | bytes 3145736 | tf_op jit(solution)/shard_map/ppermute | solution.py:111
  100.2 32.9 %collective-permute-start.7 = (bf16[16,2,16,2048]{3,2,1,0:T(8,128)(2,1)}, bf16[16,2,16,2048]{3,2,1,0:T(8,128)(2,1)}, u32[]{:S(2)}, u32[]{:S(2)}) collective-permute-start(bf16[16,2,16,2048]{3,2,1,0:T(8,128)(2,1)} %bitcast.13.p0), channel_id=1, source_target_pairs={{0,8},{1,9},{2,10},{3,11},{4,12},{5,13},{6,14},{7,15},{8,0},{9,1},... | collective-permute-start | bytes 6291464 | tf_op jit(solution)/shard_map/ppermute | solution.py:111
  100.3 32.9 %collective-permute-start.11 = (bf16[16,2,16,2048]{3,2,1,0:T(8,128)(2,1)}, bf16[16,2,16,2048]{3,2,1,0:T(8,128)(2,1)}, u32[]{:S(2)}, u32[]{:S(2)}) collective-permute-start(bf16[16,2,16,2048]{3,2,1,0:T(8,128)(2,1)} %bitcast.15.p2), channel_id=1, source_target_pairs={{0,8},{1,9},{2,10},{3,11},{4,12},{5,13},{6,14},{7,15},{8,0},{9,1},... | collective-permute-start | bytes 6291464 | tf_op jit(solution)/shard_map/ppermute | solution.py:111
  100.8 32.4 %collective-permute-start.9 = (bf16[16,2,16,2048]{3,2,1,0:T(8,128)(2,1)}, bf16[16,2,16,2048]{3,2,1,0:T(8,128)(2,1)}, u32[]{:S(2)}, u32[]{:S(2)}) collective-permute-start(bf16[16,2,16,2048]{3,2,1,0:T(8,128)(2,1)} %bitcast.14.p1), channel_id=1, source_target_pairs={{0,8},{1,9},{2,10},{3,11},{4,12},{5,13},{6,14},{7,15},{8,0},{9,1},... | collective-permute-start | bytes 6291464 | tf_op jit(solution)/shard_map/ppermute | solution.py:111
  102.1 2.9 %copy-start = (bf16[2048,256]{0,1:T(8,128)(2,1)S(1)}, bf16[2048,256]{0,1:T(8,128)(2,1)}, u32[]{:S(2)}) copy-start(bf16[2048,256]{0,1:T(8,128)(2,1)} %all-gather.2.cloned.1.call-done) | copy-start | bytes 3145732
  110.2 2.0 copy-start.1
  110.2 22.9 %collective-permute-start.13 = (bf16[8,2,16,2048]{3,2,1,0:T(8,128)(2,1)S(1)}, bf16[8,2,16,2048]{3,2,1,0:T(8,128)(2,1)S(1)}, u32[]{:S(2)}, u32[]{:S(2)}) collective-permute-start(bf16[8,2,16,2048]{3,2,1,0:T(8,128)(2,1)S(1)} %bitcast.68), channel_id=1, source_target_pairs={{0,8},{1,9},{2,10},{3,11},{4,12},{5,13},{6,14},{7,15},{8,0},{9,1},... | collective-permute-start | bytes 3145736 | tf_op jit(solution)/shard_map/ppermute | solution.py:111
  112.2 20.9 %collective-permute-start.15 = (bf16[8,2,16,2048]{3,2,1,0:T(8,128)(2,1)}, bf16[8,2,16,2048]{3,2,1,0:T(8,128)(2,1)S(1)}, u32[]{:S(2)}, u32[]{:S(2)}) collective-permute-start(bf16[8,2,16,2048]{3,2,1,0:T(8,128)(2,1)} %bitcast.17.p4), channel_id=1, source_target_pairs={{0,8},{1,9},{2,10},{3,11},{4,12},{5,13},{6,14},{7,15},{8,0},{9,1},... | collective-permute-start | bytes 3145736 | tf_op jit(solution)/shard_map/ppermute | solution.py:111
  133.1 1.0 copy-start.2
  133.1 1.3 copy-start.3
  156.6 26.1 %copy-start.5 = (f32[256,256]{1,0:T(8,128)S(1)}, f32[256,256]{1,0:T(8,128)}, u32[]{:S(2)}) copy-start(f32[256,256]{1,0:T(8,128)} %get-tuple-element.34) | copy-start | bytes 786436
  156.6 37.9 %all-to-all-start = ((f32[8,128,256]{2,1,0:T(8,128)}), f32[8,128,256]{2,1,0:T(8,128)S(1)}, u32[]{:S(2)}, u32[]{:S(2)}) async-start(f32[8,128,256]{2,1,0:T(8,128)} %bitcast.70), calls=%async_computation | async-start | bytes 2097152 | tf_op jit(solution)/shard_map/all_to_all | solution.py:381
  194.5 1.0 copy-start.4
Sparse Core Ops, SparseCore 0:
  9.8 47.4 all-gather.1
  105.1 77.6 all-reduce.2

commit v4 on v3

--- a/solution.py
+++ b/solution.py
@@ -122,12 +122,28 @@
     return jnp.concatenate(came, 0)
 
 
-def gather_table(piece, core):
+def summed_over_cols(value):
+    for dim, bit in (("z", 1), ("y", 1), ("y", 2)):
+        pairs = []
+        for j in range(128):
+            at = place(j)
+            at[dim] ^= bit
+            pairs.append((j, device(at)))
+        other = lax.ppermute(value, AXES, pairs)
+        value = value + other
+    return value
+
+
+def gather_tables(piece, second, core):
     half = piece.shape[1] // 2
     mine = lax.dynamic_slice_in_dim(piece, core * half, half, 1)
     other = lax.dynamic_slice_in_dim(piece, (1 - core) * half, half, 1)
-    came = across(other)
-    unit = jnp.where(core == 0, jnp.stack([mine, came]), jnp.stack([came, mine]))
+    came = across(jnp.stack([other, second]))
+    here = jnp.stack([mine, second])
+    both = jnp.where(core == 0, jnp.stack([here, came]), jnp.stack([came, here]))
+    unit = both[:, 0]
+    close = ring(both[:, 1][None], ("x", "x"))
+    remote = shifted(close, ("z", "z"), 2)
     near = ring(unit[None], ("x", "y"))
     plane = ring(near[None], ("y", "z"))
     last = ("z", "x")
@@ -136,14 +152,44 @@
     far0 = shifted(left[:2], last, 1)
     far1 = shifted(right[2:], last, -1)
     own = [x.reshape(-1, *unit.shape) for x in (plane, left, right, far0, far1)]
-    return own, [across(x) for x in own]
+    return own, [across(x) for x in own], close, remote
+
+
+def spot(there, here):
+    ahead = (there - here) & 3
+    return jnp.where(ahead == 3, 1, jnp.where(ahead == 0, 0, ahead + 1))
+
+
+def pick_kernel(table, close_ref, remote_ref, index_ref, picked_ref, gram_ref, rows):
+    half = rows.shape[0] // 2
+    z_hi = table[4]
+    near = jnp.concatenate([close_ref[table[x]].reshape(32, -1) for x in range(4)], 0)
+    far = jnp.concatenate([remote_ref[table[x]].reshape(32, -1) for x in range(4)], 0)
+    rows[pl.ds(pl.multiple_of(z_hi * half, half), half), :] = near
+    rows[pl.ds(pl.multiple_of((1 - z_hi) * half, half), half), :] = far
+    r = rows[...]
+    gram_ref[...] = dot(r, r, NT)
+    at = lax.broadcasted_iota(jnp.int32, (r.shape[1], index_ref.shape[1]), 0)
+    hot = (at == index_ref[...]).astype(F32).astype(BF)
+    picked_ref[...] = dot(r, hot, NN).T.astype(BF)
+
+
+def pick(table, close, remote, index):
+    n, rows = index.shape[1], close.shape[-1]
+    return pl.pallas_call(
+        pick_kernel,
+        in_specs=[pl.BlockSpec(memory_space=pltpu.SMEM)]
+        + [pl.BlockSpec(memory_space=pltpu.VMEM)] * 3,
+        out_specs=[pl.BlockSpec(memory_space=pltpu.VMEM)] * 2,
+        out_shape=[jax.ShapeDtypeStruct((n, 256), BF), jax.ShapeDtypeStruct((256, 256), F32)],
+        scratch_shapes=[pltpu.VMEM((256, rows), BF)],
+        cost_estimate=pl.CostEstimate(
+            flops=2_000_000_000, bytes_accessed=2_000_000, transcendentals=0
+        ),
+    )(table, close, remote, index)
 
 
 def piece_table(row_at, col_at, order):
-    def spot(there, here):
-        ahead = (there - here) & 3
-        return jnp.where(ahead == 3, 1, jnp.where(ahead == 0, 0, ahead + 1))
-
     y, z_lo, z_hi, x = jnp.meshgrid(
         jnp.arange(4), jnp.arange(2), jnp.arange(2), jnp.arange(4), indexing="ij"
     )
@@ -352,13 +398,15 @@
     range_rows = second_factor.shape[0]
     slab = range_rows * n_cols // n_rows
 
-    second_range = lax.all_gather(second_factor, "rows", axis=1, tiled=True)
     core = row_at & 1
-    own, swapped = gather_table(third_factor.T, core)
-
-    contract = (((0,), (0,)), ((), ()))
-    local_gram = dot(second_range, second_range, contract)
-    gram_second = lax.psum(local_gram, "cols")
+    own, swapped, close, remote = gather_tables(third_factor.T, second_factor.T, core)
+    spots = jnp.concatenate(
+        [spot(jnp.arange(4, dtype=jnp.int32), row_at >> 1), (row_at >> 3)[None]]
+    )
+    picked, local_gram = pick(
+        spots, close, remote, (block_second - col_at * range_rows)[None, :]
+    )
+    gram_second = summed_over_cols(local_gram)
 
     lane = jnp.arange(width, dtype=jnp.int32)
     slot = jnp.arange(nblk, dtype=jnp.int32)
@@ -367,7 +415,6 @@
     head, rest = build(
         (block_third // LO).astype(F32), (block_third % LO).astype(F32), values
     )
-    picked = second_range[block_second - col_at * range_rows]
     owner = (block_owner - row_at * slab)[None, :]
     fold = product(piece_table(row_at, col_at, core), head, rest, own, (), slab)
     part, gram_third = product(

time: 231 us -> 225 us (0.974)
  starting transfers between devices: 22.7 us -> 38.1 us
  between operations: 14.9 us -> 1.58 us
  waiting for transfers between devices: 44.5 us -> 34.8 us
  Pallas kernels: 99.4 us -> 103 us
  other arithmetic: 8.53 us -> 12.1 us
  matrix products: 2.83 us -> 0 us
    psum x1 -> x0, waiting for transfers between devices: 22.4 us -> none  [per_device(): gram_second = lax.psum(local_gram, 'cols')]
    ppermute x16 -> x20, starting transfers between devices: 18.9 us -> 28.7 us  [shifted(): return lax.ppermute(value, AXES, pairs)]
    ppermute x0 -> x3, starting transfers between devices: none -> 5.71 us  [summed_over_cols(): other = lax.ppermute(value, AXES, pairs)]
    all_to_all x1, waiting for transfers between devices: 0.01 us -> 5.37 us  [per_device(): spread = lax.all_to_all(spread, 'cols', 0, 0, tiled=True)]
    ppermute x0 -> x3, waiting for transfers between devices: none -> 4.49 us  [summed_over_cols(): other = lax.ppermute(value, AXES, pairs)]
    pallas_call x0 -> x1, Pallas kernels: none -> 3.1 us  [pick(): pl.pallas_call(pick_kernel, in_specs=[pl.BlockSpec(memory_space=pltpu.SME...]
    dot_general x1 -> x0, matrix products: 2.83 us -> none  [dot(): return lax.dot_general(a, b, dims, preferred_element_type=F32)]
    ppermute x16 -> x20, waiting for transfers between devices: 22.1 us -> 24.9 us  [shifted(): return lax.ppermute(value, AXES, pairs)]
  transfers between devices with their start and end apart: 19 -> 24, of which waited for: 10 -> 7; matrix products, arithmetic and copies ran while one was open for 9% -> 7% of each run, Pallas kernels for 42% -> 45%
where the time goes in v4:
time: 225 us; the launch traced here: 224 us
  Pallas kernels  103 us (46%)
  starting transfers between devices  38.1 us (17%)
  waiting for transfers between devices  34.8 us (15%)
  blocking collectives  23.5 us (10%)
  other arithmetic  12.1 us (5%)
  local copies, waits for them, and re-layouts  10.7 us (5%)
    pallas_call x4, Pallas kernels, build(): made = call(hi, lo, v, *made)  44.3 us
    pallas_call x2, Pallas kernels, product(): pl.pallas_call(second_kernel if more else first_kernel, grid_spec=pltpu.P...  43.2 us
    ppermute x20, starting transfers between devices, shifted(): return lax.ppermute(value, AXES, pairs)  28.7 us
    ppermute x20, waiting for transfers between devices, shifted(): return lax.ppermute(value, AXES, pairs)  24.9 us
    all_to_all x1, blocking collectives, per_device(): moved = lax.all_to_all(solved, 'rows', 0, 0, tiled=True)  14.7 us
    pallas_call x1, Pallas kernels, inverse(): pl.pallas_call(inverse_kernel, out_shape=[jax.ShapeDtypeStruct((n, n), F3...  9.79 us
    all_to_all x1, blocking collectives, per_device(): moved = lax.all_to_all(moved, 'cols', 0, 0, tiled=True)  8.79 us
    ppermute x3, starting transfers between devices, summed_over_cols(): other = lax.ppermute(value, AXES, pairs)  5.71 us
  transfers between devices with their start and end apart: 24, of which 7 were waited for; matrix products, arithmetic and copies ran while one was open for 7% of the time, Pallas kernels for 45%

profile of v4, /device:TPU:0, one launch (start us, length us, event | category | flops | bytes accessed | tf_op | source)
XLA Modules:
  0.0 223.7 jit_solution(4451471518397494361)
XLA Ops:
  0.0 0.9 dynamic-slice_bitcast_fusion.1
  0.9 0.9 fusion.17
  1.8 2.0 fusion.12
  4.5 1.8 fusion.18.v_ref
  6.3 11.1 %shard_map.83 = (bf16[128,512,256]{2,1,0:T(8,128)(2,1)}, bf16[128,512,256]{2,1,0:T(8,128)(2,1)}) custom-call(f32[512,128]{1,0:T(8,128)} %get-tuple-element.72.hi_ref, f32[512,128]{1,0:T(8,128)} %get-tuple-element.71.lo_ref, f32[512,128]{1,0:T(8,128)} %fusion.18.v_ref), custom_call_target="tpu_custom_call" | custom-call | flops 10000000000 | bytes 16777216 | tf_op jit(solution)/shard_map/pallas_call | solution.py:87
  17.5 3.2 %collective-permute-start.10 = (bf16[1,2,16,2048]{3,2,1,0:T(8,128)(2,1)S(1)}, bf16[1,2,16,2048]{3,2,1,0:T(8,128)(2,1)S(1)}, u32[]{:S(2)}, u32[]{:S(2)}) collective-permute-start(bf16[1,2,16,2048]{3,2,1,0:T(8,128)(2,1)S(1)} %get-tuple-element.70), channel_id=1, source_target_pairs={{0,32},{1,33},{2,34},{3,35},{4,36},{5,37},{6,38},{7,39},{8,12},{9,... | collective-permute-start | bytes 393224 | tf_op jit(solution)/shard_map/ppermute | solution.py:111
  20.7 1.1 collective-permute-start.9
  21.8 0.9 collective-permute-start.8
  22.7 11.0 %shard_map.84 = (bf16[128,512,256]{2,1,0:T(8,128)(2,1)}, bf16[128,512,256]{2,1,0:T(8,128)(2,1)}) custom-call(f32[512,128]{1,0:T(8,128)} %get-tuple-element.72.hi_ref, f32[512,128]{1,0:T(8,128)} %get-tuple-element.71.lo_ref, f32[512,128]{1,0:T(8,128)} %fusion.18.v_ref, ...), custom_call_target="tpu_custom_call", output_to_operand_aliasing={{0}: (3, {}), {1}: (4, {})} | custom-call | flops 10000000000 | bytes 16777216 | tf_op jit(solution)/shard_map/pallas_call | solution.py:87
  33.8 3.3 %collective-permute-start.13 = (bf16[1,4,2,16,2048]{4,3,2,1,0:T(8,128)(2,1)S(1)}, bf16[1,4,2,16,2048]{4,3,2,1,0:T(8,128)(2,1)S(1)}, u32[]{:S(2)}, u32[]{:S(2)}) collective-permute-start(bf16[1,4,2,16,2048]{4,3,2,1,0:T(8,128)(2,1)S(1)} %maximum_bitcast_fusion), channel_id=1, source_target_pairs={{0,4},{1,5},{2,6},{3,7},{4,0},{5,1},{6,2},{7,3},{8,72},{9,73},{10,... | collective-permute-start | bytes 1572872 | tf_op jit(solution)/shard_map/ppermute | solution.py:111
  37.1 1.1 collective-permute-start.12
  38.2 1.0 collective-permute-start.11
  39.1 11.1 %shard_map.85 = (bf16[128,512,256]{2,1,0:T(8,128)(2,1)}, bf16[128,512,256]{2,1,0:T(8,128)(2,1)}) custom-call(f32[512,128]{1,0:T(8,128)} %get-tuple-element.72.hi_ref, f32[512,128]{1,0:T(8,128)} %get-tuple-element.71.lo_ref, f32[512,128]{1,0:T(8,128)} %fusion.18.v_ref, ...), custom_call_target="tpu_custom_call", output_to_operand_aliasing={{0}: (3, {}), {1}: (4, {})} | custom-call | flops 10000000000 | bytes 16777216 | tf_op jit(solution)/shard_map/pallas_call | solution.py:87
  50.6 0.8 copy-done.5
  51.4 1.5 pad_maximum_fusion.1
  52.9 2.0 collective-permute-start.15
  54.9 2.2 collective-permute-start.17
  57.7 2.6 %collective-permute-start.2 = (bf16[1,2,16,2048]{3,2,1,0:T(8,128)(2,1)S(1)}, bf16[1,2,16,2048]{3,2,1,0:T(8,128)(2,1)S(1)}, u32[]{:S(2)}, u32[]{:S(2)}) collective-permute-start(bf16[1,2,16,2048]{3,2,1,0:T(8,128)(2,1)S(1)} %get-tuple-element.69), channel_id=1, source_target_pairs={{0,48},{1,49},{2,50},{3,51},{4,52},{5,53},{6,54},{7,55},{8,56},{9,... | collective-permute-start | bytes 393224 | tf_op jit(solution)/shard_map/ppermute | solution.py:111
  60.4 4.6 %collective-permute-done.3 = bf16[1,2,16,2048]{3,2,1,0:T(8,128)(2,1)S(1)} collective-permute-done((bf16[1,2,16,2048]{3,2,1,0:T(8,128)(2,1)S(1)}, bf16[1,2,16,2048]{3,2,1,0:T(8,128)(2,1)S(1)}, u32[]{:S(2)}, u32[]{:S(2)}) %collective-permute-start.3) | collective-permute-done | bytes 131104 | tf_op jit(solution)/shard_map/ppermute | solution.py:111
  65.0 2.5 %collective-permute-done.2 = bf16[1,2,16,2048]{3,2,1,0:T(8,128)(2,1)S(1)} collective-permute-done((bf16[1,2,16,2048]{3,2,1,0:T(8,128)(2,1)S(1)}, bf16[1,2,16,2048]{3,2,1,0:T(8,128)(2,1)S(1)}, u32[]{:S(2)}, u32[]{:S(2)}) %collective-permute-start.2) | collective-permute-done | bytes 131104 | tf_op jit(solution)/shard_map/ppermute | solution.py:111
  68.0 1.9 collective-permute-start.4
  71.1 17.0 %collective-permute-done.4.remote_ref = bf16[4,2,16,2048]{3,2,1,0:T(8,128)(2,1)S(1)} collective-permute-done((bf16[4,2,16,2048]{3,2,1,0:T(8,128)(2,1)S(1)}, bf16[4,2,16,2048]{3,2,1,0:T(8,128)(2,1)S(1)}, u32[]{:S(2)}, u32[]{:S(2)}) %collective-permute-start.4) | collective-permute-done | bytes 524320 | tf_op jit(solution)/shard_map/ppermute | solution.py:111
  88.1 0.8 copy-done.10
  88.9 3.1 %shard_map.82 = (bf16[512,256]{1,0:T(8,128)(2,1)}, f32[256,256]{1,0:T(8,128)}) custom-call(s32[5]{0:T(128)} %pad_add_fusion.2.table, bf16[4,2,16,2048]{3,2,1,0:T(8,128)(2,1)} %copy-done.4, bf16[4,2,16,2048]{3,2,1,0:T(8,128)(2,1)} %copy-done.10, s32[1,512]{1,0:T(1,128)} %bitcast.90), custom_call_target="tpu_custom_call" | custom-call | flops 2000000000 | bytes 2000000 | tf_op jit(solution)/shard_map/pallas_call | solution.py:179
  92.0 1.4 collective-permute-start.5
  94.1 4.5 %collective-permute-done.5 = f32[256,256]{1,0:T(8,128)S(1)} collective-permute-done((f32[256,256]{1,0:T(8,128)}, f32[256,256]{1,0:T(8,128)S(1)}, u32[]{:S(2)}, u32[]{:S(2)}) %collective-permute-start.5) | collective-permute-done | bytes 262176 | tf_op jit(solution)/shard_map/ppermute | solution.py:132
  98.6 1.0 add.112
  99.6 1.3 collective-permute-start.6
  102.0 2.3 %slice.92 = bf16[2,4,2,16,2048]{4,3,2,1,0:T(8,128)(2,1)} slice(bf16[4,4,2,16,2048]{4,3,2,1,0:T(8,128)(2,1)} %collective-permute-done.15), slice={[0:2], [0:4], [0:2], [0:16], [0:2048]} | slice | bytes 2097152 | tf_op jit(solution)/shard_map/slice | solution.py:152
  104.3 1.5 collective-permute-start.19
  105.9 2.3 %slice.93 = bf16[2,4,2,16,2048]{4,3,2,1,0:T(8,128)(2,1)} slice(bf16[4,4,2,16,2048]{4,3,2,1,0:T(8,128)(2,1)} %collective-permute-done.17), slice={[2:4], [0:4], [0:2], [0:16], [0:2048]} | slice | bytes 2097152 | tf_op jit(solution)/shard_map/slice | solution.py:153
  108.2 1.7 collective-permute-start.21
  109.9 0.6 pad_add_fusion.1.table
  110.5 4.5 %collective-permute-start.14 = (bf16[16,2,16,2048]{3,2,1,0:T(8,128)(2,1)S(1)}, bf16[16,2,16,2048]{3,2,1,0:T(8,128)(2,1)}, u32[]{:S(2)}, u32[]{:S(2)}) collective-permute-start(bf16[16,2,16,2048]{3,2,1,0:T(8,128)(2,1)S(1)} %bitcast.79), channel_id=1, source_target_pairs={{0,8},{1,9},{2,10},{3,11},{4,12},{5,13},{6,14},{7,15},{8,0},{9,1},... | collective-permute-start | bytes 6291464 | tf_op jit(solution)/shard_map/ppermute | solution.py:111
  115.0 0.7 copy-done.6
  116.3 11.0 %shard_map.86 = (bf16[128,512,256]{2,1,0:T(8,128)(2,1)}, bf16[128,512,256]{2,1,0:T(8,128)(2,1)}) custom-call(f32[512,128]{1,0:T(8,128)} %get-tuple-element.72.hi_ref, f32[512,128]{1,0:T(8,128)} %get-tuple-element.71.lo_ref, f32[512,128]{1,0:T(8,128)} %fusion.18.v_ref, ...), custom_call_target="tpu_custom_call", output_to_operand_aliasing={{0}: (3, {}), {1}: (4, {})} | custom-call | flops 10000000000 | bytes 16777216 | tf_op jit(solution)/shard_map/pallas_call | solution.py:87
  127.3 1.7 add.113
  130.0 21.0 %shard_map.87 = (f32[512,256]{1,0:T(8,128)}, f32[256,256]{1,0:T(8,128)}) custom-call(s32[129]{0:T(256)} %pad_add_fusion.1.table, bf16[128,512,256]{2,1,0:T(8,128)(2,1)} %get-tuple-element.33.head_ref, bf16[128,512,256]{2,1,0:T(8,128)(2,1)} %get-tuple-element.34.rest_ref, bf16[16,2,16,2048]{3,2,1,0:T(8,128)(2,1)} %bitcast.80, ...), custom_call_target="tpu_custom_call" | custom-call | flops 15000000512 | bytes 50000000 | tf_op jit(solution)/shard_map/pallas_call | solution.py:285
  151.0 3.0 %collective-permute-start.7 = (f32[256,256]{1,0:T(8,128)S(1)}, f32[256,256]{1,0:T(8,128)S(1)}, u32[]{:S(2)}, u32[]{:S(2)}) collective-permute-start(f32[256,256]{1,0:T(8,128)S(1)} %copy-done.3), channel_id=1, source_target_pairs={{0,4},{1,5},{2,6},{3,7},{4,0},{5,1},{6,2},{7,3},{8,12},{9,13},{10,... | collective-permute-start | bytes 786440 | tf_op jit(solution)/shard_map/ppermute | solution.py:132
  154.1 22.2 %shard_map.88 = (f32[1024,256]{1,0:T(8,128)}, f32[256,256]{1,0:T(8,128)}) custom-call(s32[129]{0:T(256)} %pad_add_fusion.table, bf16[128,512,256]{2,1,0:T(8,128)(2,1)} %get-tuple-element.33.head_ref, bf16[128,512,256]{2,1,0:T(8,128)(2,1)} %get-tuple-element.34.rest_ref, bf16[16,2,16,2048]{3,2,1,0:T(8,128)(2,1)} %collective-permute-done.14.p0, ...), custom_call_target="tpu_custom_call" | custom-call | flops 15000000512 | bytes 50000000 | tf_op jit(solution)/shard_map/pallas_call | solution.py:285
  176.3 3.7 %all-to-all-start = ((f32[8,128,256]{2,1,0:T(8,128)}), f32[8,128,256]{2,1,0:T(8,128)S(1)}, u32[]{:S(2)}, u32[]{:S(2)}) async-start(f32[8,128,256]{2,1,0:T(8,128)} %bitcast.83), calls=%async_computation | async-start | bytes 2097152 | tf_op jit(solution)/shard_map/all_to_all | solution.py:428
  180.0 9.8 %shard_map.89 = (f32[256,256]{1,0:T(8,128)S(1)}, s32[1]{0:T(128)}) custom-call(f32[256,256]{1,0:T(8,128)S(1)} %multiply_multiply_fusion.gram_ref), custom_call_target="tpu_custom_call" | custom-call | flops 5000000000 | bytes 600000 | tf_op jit(solution)/shard_map/pallas_call | solution.py:345
  190.8 5.4 %all-to-all-done.spread_ref = f32[8,128,256]{2,1,0:T(8,128)S(1)} async-done(((f32[8,128,256]{2,1,0:T(8,128)}), f32[8,128,256]{2,1,0:T(8,128)S(1)}, u32[]{:S(2)}, u32[]{:S(2)}) %all-to-all-start) | async-done | bytes 1048608 | tf_op jit(solution)/shard_map/all_to_all | solution.py:428
  196.1 1.0 copy-done.2
  197.2 2.3 %shard_map.90 = f32[16,16,128]{2,1,0:T(8,128)} custom-call(f32[256,256]{1,0:T(8,128)S(1)} %get-tuple-element.137.inverse_ref, f32[8,128,256]{2,1,0:T(8,128)} %copy-done.2), custom_call_target="tpu_custom_call" | custom-call | flops 500000000 | bytes 1500000 | tf_op jit(solution)/shard_map/pallas_call | solution.py:374
  199.4 14.7 %all_to_all.15 = f32[16,16,128]{2,1,0:T(8,128)S(1)} all-to-all(f32[16,16,128]{2,1,0:T(8,128)} %shard_map.90), channel_id=1, replica_groups=mesh['rows'=16,'cols'=8] {'rows'}, dimensions={0} | all-to-all | bytes 262144 | tf_op jit(solution)/shard_map/all_to_all | solution.py:430
  214.1 8.8 %all_to_all.16 = f32[8,2,16,128]{3,2,1,0:T(8,128)S(1)} all-to-all(f32[8,2,16,128]{3,2,1,0:T(8,128)S(1)} %bitcast.84), channel_id=1, replica_groups=mesh['rows'=16,'cols'=8] {'cols'}, dimensions={0} | all-to-all | bytes 262144 | tf_op jit(solution)/shard_map/all_to_all | solution.py:433
  223.0 0.7 copy.21
  (72 shorter events, 6.7 us)
Async XLA Ops:
  1.8 15.7 %collective-permute-start = (bf16[2,16,2048]{2,1,0:T(8,128)(2,1)S(1)}, bf16[2,16,2048]{2,1,0:T(8,128)(2,1)S(1)}, u32[]{:S(2)}, u32[]{:S(2)}) collective-permute-start(bf16[2,16,2048]{2,1,0:T(8,128)(2,1)S(1)} %get-tuple-element.76), channel_id=1, source_target_pairs={{0,8},{1,9},{2,10},{3,11},{4,12},{5,13},{6,14},{7,15},{8,0},{9,1},... | collective-permute-start | bytes 393224 | tf_op jit(solution)/shard_map/ppermute | solution.py:111
  17.5 16.3 %collective-permute-start.10 = (bf16[1,2,16,2048]{3,2,1,0:T(8,128)(2,1)S(1)}, bf16[1,2,16,2048]{3,2,1,0:T(8,128)(2,1)S(1)}, u32[]{:S(2)}, u32[]{:S(2)}) collective-permute-start(bf16[1,2,16,2048]{3,2,1,0:T(8,128)(2,1)S(1)} %get-tuple-element.70), channel_id=1, source_target_pairs={{0,32},{1,33},{2,34},{3,35},{4,36},{5,37},{6,38},{7,39},{8,12},{9,... | collective-permute-start | bytes 393224 | tf_op jit(solution)/shard_map/ppermute | solution.py:111
  20.7 13.0 %collective-permute-start.9 = (bf16[1,2,16,2048]{3,2,1,0:T(8,128)(2,1)S(1)}, bf16[1,2,16,2048]{3,2,1,0:T(8,128)(2,1)S(1)}, u32[]{:S(2)}, u32[]{:S(2)}) collective-permute-start(bf16[1,2,16,2048]{3,2,1,0:T(8,128)(2,1)S(1)} %get-tuple-element.70), channel_id=1, source_target_pairs={{0,48},{1,49},{2,50},{3,51},{4,52},{5,53},{6,54},{7,55},{8,14},{9,... | collective-permute-start | bytes 393224 | tf_op jit(solution)/shard_map/ppermute | solution.py:111
  21.8 11.9 %collective-permute-start.8 = (bf16[1,2,16,2048]{3,2,1,0:T(8,128)(2,1)S(1)}, bf16[1,2,16,2048]{3,2,1,0:T(8,128)(2,1)S(1)}, u32[]{:S(2)}, u32[]{:S(2)}) collective-permute-start(bf16[1,2,16,2048]{3,2,1,0:T(8,128)(2,1)S(1)} %get-tuple-element.70), channel_id=1, source_target_pairs={{0,16},{1,17},{2,18},{3,19},{4,20},{5,21},{6,22},{7,23},{8,10},{9,... | collective-permute-start | bytes 393224 | tf_op jit(solution)/shard_map/ppermute | solution.py:111
  33.8 16.5 %collective-permute-start.13 = (bf16[1,4,2,16,2048]{4,3,2,1,0:T(8,128)(2,1)S(1)}, bf16[1,4,2,16,2048]{4,3,2,1,0:T(8,128)(2,1)S(1)}, u32[]{:S(2)}, u32[]{:S(2)}) collective-permute-start(bf16[1,4,2,16,2048]{4,3,2,1,0:T(8,128)(2,1)S(1)} %maximum_bitcast_fusion), channel_id=1, source_target_pairs={{0,4},{1,5},{2,6},{3,7},{4,0},{5,1},{6,2},{7,3},{8,72},{9,73},{10,... | collective-permute-start | bytes 1572872 | tf_op jit(solution)/shard_map/ppermute | solution.py:111
  37.1 13.5 %collective-permute-start.12 = (bf16[1,4,2,16,2048]{4,3,2,1,0:T(8,128)(2,1)S(1)}, bf16[1,4,2,16,2048]{4,3,2,1,0:T(8,128)(2,1)S(1)}, u32[]{:S(2)}, u32[]{:S(2)}) collective-permute-start(bf16[1,4,2,16,2048]{4,3,2,1,0:T(8,128)(2,1)S(1)} %maximum_bitcast_fusion), channel_id=1, source_target_pairs={{0,6},{1,7},{2,0},{3,1},{4,2},{5,3},{6,4},{7,5},{8,73},{9,8},{10,7... | collective-permute-start | bytes 1572872 | tf_op jit(solution)/shard_map/ppermute | solution.py:111
  38.2 13.3 %collective-permute-start.11 = (bf16[1,4,2,16,2048]{4,3,2,1,0:T(8,128)(2,1)S(1)}, bf16[1,4,2,16,2048]{4,3,2,1,0:T(8,128)(2,1)}, u32[]{:S(2)}, u32[]{:S(2)}) collective-permute-start(bf16[1,4,2,16,2048]{4,3,2,1,0:T(8,128)(2,1)S(1)} %maximum_bitcast_fusion), channel_id=1, source_target_pairs={{0,2},{1,3},{2,4},{3,5},{4,6},{5,7},{6,0},{7,1},{8,9},{9,72},{10,1... | collective-permute-start | bytes 1572872 | tf_op jit(solution)/shard_map/ppermute | solution.py:111
  50.3 20.2 %copy-start.8 = (s32[512]{0:T(512)S(1)}, s32[512]{0:T(512)}, u32[]{:S(2)}) copy-start(s32[512]{0:T(512)} %param.13) | copy-start | bytes 6148
  50.6 0.8 copy-start.5
  52.9 57.6 %copy-start = (bf16[4,4,2,16,2048]{4,3,2,1,0:T(8,128)(2,1)}, bf16[4,4,2,16,2048]{4,3,2,1,0:T(8,128)(2,1)S(1)}, u32[]{:S(2)}) copy-start(bf16[4,4,2,16,2048]{4,3,2,1,0:T(8,128)(2,1)S(1)} %pad_maximum_fusion.1) | copy-start | bytes 6291460
  52.9 49.1 %collective-permute-start.15 = (bf16[4,4,2,16,2048]{4,3,2,1,0:T(8,128)(2,1)S(1)}, bf16[4,4,2,16,2048]{4,3,2,1,0:T(8,128)(2,1)}, u32[]{:S(2)}, u32[]{:S(2)}) collective-permute-start(bf16[4,4,2,16,2048]{4,3,2,1,0:T(8,128)(2,1)S(1)} %pad_maximum_fusion.1), channel_id=1, source_target_pairs={{0,1},{1,64},{2,3},{3,66},{4,5},{5,68},{6,7},{7,70},{8,24},{9,25},... | collective-permute-start | bytes 6291464 | tf_op jit(solution)/shard_map/ppermute | solution.py:111
  54.9 51.0 %collective-permute-start.17 = (bf16[4,4,2,16,2048]{4,3,2,1,0:T(8,128)(2,1)S(1)}, bf16[4,4,2,16,2048]{4,3,2,1,0:T(8,128)(2,1)}, u32[]{:S(2)}, u32[]{:S(2)}) collective-permute-start(bf16[4,4,2,16,2048]{4,3,2,1,0:T(8,128)(2,1)S(1)} %pad_maximum_fusion.1), channel_id=1, source_target_pairs={{0,65},{1,0},{2,67},{3,2},{4,69},{5,4},{6,71},{7,6},{8,56},{9,57},... | collective-permute-start | bytes 6291464 | tf_op jit(solution)/shard_map/ppermute | solution.py:111
  57.1 7.9 %collective-permute-start.3 = (bf16[1,2,16,2048]{3,2,1,0:T(8,128)(2,1)S(1)}, bf16[1,2,16,2048]{3,2,1,0:T(8,128)(2,1)S(1)}, u32[]{:S(2)}, u32[]{:S(2)}) collective-permute-start(bf16[1,2,16,2048]{3,2,1,0:T(8,128)(2,1)S(1)} %get-tuple-element.69), channel_id=1, source_target_pairs={{0,32},{1,33},{2,34},{3,35},{4,36},{5,37},{6,38},{7,39},{8,40},{9,... | collective-permute-start | bytes 393224 | tf_op jit(solution)/shard_map/ppermute | solution.py:111
  57.7 9.7 %collective-permute-start.2 = (bf16[1,2,16,2048]{3,2,1,0:T(8,128)(2,1)S(1)}, bf16[1,2,16,2048]{3,2,1,0:T(8,128)(2,1)S(1)}, u32[]{:S(2)}, u32[]{:S(2)}) collective-permute-start(bf16[1,2,16,2048]{3,2,1,0:T(8,128)(2,1)S(1)} %get-tuple-element.69), channel_id=1, source_target_pairs={{0,48},{1,49},{2,50},{3,51},{4,52},{5,53},{6,54},{7,55},{8,56},{9,... | collective-permute-start | bytes 393224 | tf_op jit(solution)/shard_map/ppermute | solution.py:111
  60.4 7.6 %collective-permute-start.1 = (bf16[1,2,16,2048]{3,2,1,0:T(8,128)(2,1)S(1)}, bf16[1,2,16,2048]{3,2,1,0:T(8,128)(2,1)S(1)}, u32[]{:S(2)}, u32[]{:S(2)}) collective-permute-start(bf16[1,2,16,2048]{3,2,1,0:T(8,128)(2,1)S(1)} %get-tuple-element.69), channel_id=1, source_target_pairs={{0,16},{1,17},{2,18},{3,19},{4,20},{5,21},{6,22},{7,23},{8,24},{9,... | collective-permute-start | bytes 393224 | tf_op jit(solution)/shard_map/ppermute | solution.py:111
  68.0 20.9 %copy-start.4 = (bf16[4,2,16,2048]{3,2,1,0:T(8,128)(2,1)}, bf16[4,2,16,2048]{3,2,1,0:T(8,128)(2,1)S(1)}, u32[]{:S(2)}) copy-start(bf16[4,2,16,2048]{3,2,1,0:T(8,128)(2,1)S(1)} %pad_maximum_fusion.2.close_ref) | copy-start | bytes 1572868
  68.0 20.1 %collective-permute-start.4 = (bf16[4,2,16,2048]{3,2,1,0:T(8,128)(2,1)S(1)}, bf16[4,2,16,2048]{3,2,1,0:T(8,128)(2,1)S(1)}, u32[]{:S(2)}, u32[]{:S(2)}) collective-permute-start(bf16[4,2,16,2048]{3,2,1,0:T(8,128)(2,1)S(1)} %pad_maximum_fusion.2.close_ref), channel_id=1, source_target_pairs={{0,64},{1,65},{2,66},{3,67},{4,68},{5,69},{6,70},{7,71},{8,72},{9,... | collective-permute-start | bytes 1572872 | tf_op jit(solution)/shard_map/ppermute | solution.py:111
  88.1 0.8 copy-start.10
  88.9 11.9 %copy-start.9 = (s32[512]{0:T(512)S(1)}, s32[512]{0:T(512)}, u32[]{:S(2)}) copy-start(s32[512]{0:T(512)} %param.12) | copy-start | bytes 6148
  92.0 6.6 %collective-permute-start.5 = (f32[256,256]{1,0:T(8,128)}, f32[256,256]{1,0:T(8,128)S(1)}, u32[]{:S(2)}, u32[]{:S(2)}) collective-permute-start(f32[256,256]{1,0:T(8,128)} %get-tuple-element.26), channel_id=1, source_target_pairs={{0,1},{1,0},{2,3},{3,2},{4,5},{5,4},{6,7},{7,6},{8,9},{9,8},{10,11... | collective-permute-start | bytes 786440 | tf_op jit(solution)/shard_map/ppermute | solution.py:132
  99.6 15.5 %collective-permute-start.6 = (f32[256,256]{1,0:T(8,128)S(1)}, f32[256,256]{1,0:T(8,128)S(1)}, u32[]{:S(2)}, u32[]{:S(2)}) collective-permute-start(f32[256,256]{1,0:T(8,128)S(1)} %add.112), channel_id=1, source_target_pairs={{0,2},{1,3},{2,0},{3,1},{4,6},{5,7},{6,4},{7,5},{8,10},{9,11},{10,... | collective-permute-start | bytes 786440 | tf_op jit(solution)/shard_map/ppermute | solution.py:132
  104.3 24.6 %collective-permute-start.19 = (bf16[2,4,2,16,2048]{4,3,2,1,0:T(8,128)(2,1)}, bf16[2,4,2,16,2048]{4,3,2,1,0:T(8,128)(2,1)S(1)}, u32[]{:S(2)}, u32[]{:S(2)}) collective-permute-start(bf16[2,4,2,16,2048]{4,3,2,1,0:T(8,128)(2,1)} %slice.92), channel_id=1, source_target_pairs={{0,1},{1,64},{2,3},{3,66},{4,5},{5,68},{6,7},{7,70},{8,24},{9,25},... | collective-permute-start | bytes 3145736 | tf_op jit(solution)/shard_map/ppermute | solution.py:111
  108.2 20.8 %collective-permute-start.21 = (bf16[2,4,2,16,2048]{4,3,2,1,0:T(8,128)(2,1)}, bf16[2,4,2,16,2048]{4,3,2,1,0:T(8,128)(2,1)}, u32[]{:S(2)}, u32[]{:S(2)}) collective-permute-start(bf16[2,4,2,16,2048]{4,3,2,1,0:T(8,128)(2,1)} %slice.93), channel_id=1, source_target_pairs={{0,65},{1,0},{2,67},{3,2},{4,69},{5,4},{6,71},{7,6},{8,56},{9,57},... | collective-permute-start | bytes 3145736 | tf_op jit(solution)/shard_map/ppermute | solution.py:111
  110.5 40.5 %collective-permute-start.14 = (bf16[16,2,16,2048]{3,2,1,0:T(8,128)(2,1)S(1)}, bf16[16,2,16,2048]{3,2,1,0:T(8,128)(2,1)}, u32[]{:S(2)}, u32[]{:S(2)}) collective-permute-start(bf16[16,2,16,2048]{3,2,1,0:T(8,128)(2,1)S(1)} %bitcast.79), channel_id=1, source_target_pairs={{0,8},{1,9},{2,10},{3,11},{4,12},{5,13},{6,14},{7,15},{8,0},{9,1},... | collective-permute-start | bytes 6291464 | tf_op jit(solution)/shard_map/ppermute | solution.py:111
  115.0 39.0 %collective-permute-start.16 = (bf16[16,2,16,2048]{3,2,1,0:T(8,128)(2,1)}, bf16[16,2,16,2048]{3,2,1,0:T(8,128)(2,1)}, u32[]{:S(2)}, u32[]{:S(2)}) collective-permute-start(bf16[16,2,16,2048]{3,2,1,0:T(8,128)(2,1)} %bitcast.22.p1), channel_id=1, source_target_pairs={{0,8},{1,9},{2,10},{3,11},{4,12},{5,13},{6,14},{7,15},{8,0},{9,1},... | collective-permute-start | bytes 6291464 | tf_op jit(solution)/shard_map/ppermute | solution.py:111
  115.0 0.7 copy-start.6
  115.7 38.3 %collective-permute-start.18 = (bf16[16,2,16,2048]{3,2,1,0:T(8,128)(2,1)}, bf16[16,2,16,2048]{3,2,1,0:T(8,128)(2,1)}, u32[]{:S(2)}, u32[]{:S(2)}) collective-permute-start(bf16[16,2,16,2048]{3,2,1,0:T(8,128)(2,1)} %bitcast.23.p2), channel_id=1, source_target_pairs={{0,8},{1,9},{2,10},{3,11},{4,12},{5,13},{6,14},{7,15},{8,0},{9,1},... | collective-permute-start | bytes 6291464 | tf_op jit(solution)/shard_map/ppermute | solution.py:111
  129.0 1.0 copy-start.1
  129.0 25.1 %collective-permute-start.20 = (bf16[8,2,16,2048]{3,2,1,0:T(8,128)(2,1)S(1)}, bf16[8,2,16,2048]{3,2,1,0:T(8,128)(2,1)}, u32[]{:S(2)}, u32[]{:S(2)}) collective-permute-start(bf16[8,2,16,2048]{3,2,1,0:T(8,128)(2,1)S(1)} %bitcast.81), channel_id=1, source_target_pairs={{0,8},{1,9},{2,10},{3,11},{4,12},{5,13},{6,14},{7,15},{8,0},{9,1},... | collective-permute-start | bytes 3145736 | tf_op jit(solution)/shard_map/ppermute | solution.py:111
  129.0 25.1 %collective-permute-start.22 = (bf16[8,2,16,2048]{3,2,1,0:T(8,128)(2,1)}, bf16[8,2,16,2048]{3,2,1,0:T(8,128)(2,1)}, u32[]{:S(2)}, u32[]{:S(2)}) collective-permute-start(bf16[8,2,16,2048]{3,2,1,0:T(8,128)(2,1)} %bitcast.25.p4), channel_id=1, source_target_pairs={{0,8},{1,9},{2,10},{3,11},{4,12},{5,13},{6,14},{7,15},{8,0},{9,1},... | collective-permute-start | bytes 3145736 | tf_op jit(solution)/shard_map/ppermute | solution.py:111
  130.0 21.0 %copy-start.3 = (f32[256,256]{1,0:T(8,128)S(1)}, f32[256,256]{1,0:T(8,128)}, u32[]{:S(2)}) copy-start(f32[256,256]{1,0:T(8,128)} %add.113) | copy-start | bytes 786436
  151.0 28.9 %collective-permute-start.7 = (f32[256,256]{1,0:T(8,128)S(1)}, f32[256,256]{1,0:T(8,128)S(1)}, u32[]{:S(2)}, u32[]{:S(2)}) collective-permute-start(f32[256,256]{1,0:T(8,128)S(1)} %copy-done.3), channel_id=1, source_target_pairs={{0,4},{1,5},{2,6},{3,7},{4,0},{5,1},{6,2},{7,3},{8,12},{9,13},{10,... | collective-permute-start | bytes 786440 | tf_op jit(solution)/shard_map/ppermute | solution.py:132
  176.2 3.7 %copy-start.7 = (f32[256,256]{1,0:T(8,128)S(1)}, f32[256,256]{1,0:T(8,128)}, u32[]{:S(2)}) copy-start(f32[256,256]{1,0:T(8,128)} %get-tuple-element.38) | copy-start | bytes 786436
  176.3 19.9 %all-to-all-start = ((f32[8,128,256]{2,1,0:T(8,128)}), f32[8,128,256]{2,1,0:T(8,128)S(1)}, u32[]{:S(2)}, u32[]{:S(2)}) async-start(f32[8,128,256]{2,1,0:T(8,128)} %bitcast.83), calls=%async_computation | async-start | bytes 2097152 | tf_op jit(solution)/shard_map/all_to_all | solution.py:428
  196.1 1.0 copy-start.2

commit v5 on v4

--- a/solution.py
+++ b/solution.py
@@ -1,3 +1,5 @@
+import functools
+
 import jax
 import jax.numpy as jnp
 from jax import lax
@@ -14,7 +16,8 @@
 LO = 256
 HI = 128
 NB = 16
-PITCH = 24
+PITCH = 140
+GROUP = 64
 PARTS = 4
 STEP = 8
 TOLERANCE = 3e-4
@@ -31,61 +34,197 @@
     return head, (x - head.astype(F32)).astype(BF)
 
 
-def build_kernel(hi_ref, lo_ref, v_ref, head_ref, rest_ref, left, right):
+def prepare_kernel(
+    live_ref, third_ref, value_ref, length_ref, hi_ref, lo_ref, v_ref, list_ref, count_ref, again
+):
+    step = pl.program_id(0)
+    n, width = third_ref.shape
+    third = third_ref[...]
+    lane = lax.broadcasted_iota(jnp.int32, (n, width), 1)
+    block = lax.broadcasted_iota(jnp.int32, (n, width), 0) + step * n
+    live = (lane < length_ref[...]) & (block < live_ref[0])
+    hi_ref[...] = (third >> 8).astype(F32)
+    lo_ref[...] = (third & (LO - 1)).astype(F32)
+    v_ref[...] = jnp.where(live, value_ref[...].astype(F32), 0.0)
+    marked = jnp.where(live, third, -1 - lane)
+    same = jnp.zeros((n, width), jnp.bool_)
+    for shift in range(1, width // 2 + 1):
+        same = same | (marked == pltpu.roll(marked, shift, 1))
+    found = jnp.max(jnp.where(same, 1.0, 0.0), 1, keepdims=True)
+    again[pl.ds(pl.multiple_of(step * n, n), n), :] = jnp.broadcast_to(found, (n, width))
+
+    @pl.when(step == pl.num_programs(0) - 1)
+    def _():
+        total = again.shape[0]
+        flags = again[...]
+        row = lax.broadcasted_iota(jnp.int32, (total, total), 0)
+        col = lax.broadcasted_iota(jnp.int32, (total, total), 1)
+        earlier = jnp.where(col < row, 1.0, 0.0).astype(BF)
+        ahead = dot(earlier, flags.astype(BF), NN)
+        wide = jnp.concatenate([ahead] * (total // width), 1)
+        on = jnp.concatenate([flags] * (total // width), 1)
+        mine = (on > 0.5) & (wide == col.astype(F32))
+        picked = jnp.sum(jnp.where(mine, row.astype(F32), 0.0), 0, keepdims=True)
+        list_ref[...] = picked.astype(jnp.int32)
+        count_ref[0] = jnp.sum(flags[:, :1]).astype(jnp.int32)
+
+
+def prepare(third, values, length, live):
+    n, width = third.shape
+    rows = 128
+    spec = pl.BlockSpec((rows, width), lambda i: (i, 0))
+    shape = jax.ShapeDtypeStruct((n, width), F32)
+    return pl.pallas_call(
+        prepare_kernel,
+        grid=(n // rows,),
+        in_specs=[
+            pl.BlockSpec(memory_space=pltpu.SMEM),
+            spec,
+            spec,
+            pl.BlockSpec((rows, 1), lambda i: (i, 0)),
+        ],
+        out_specs=[spec] * 3
+        + [pl.BlockSpec((1, n), lambda i: (0, 0)), pl.BlockSpec(memory_space=pltpu.SMEM)],
+        out_shape=[shape] * 3
+        + [jax.ShapeDtypeStruct((1, n), jnp.int32), jax.ShapeDtypeStruct((1,), jnp.int32)],
+        scratch_shapes=[pltpu.VMEM((n, width), F32)],
+        cost_estimate=pl.CostEstimate(
+            flops=3_000_000_000, bytes_accessed=1_000_000, transcendentals=0
+        ),
+    )(live, third, values, length[:, None])
+
+
+def spread_blocks(rows_of, left, right):
     base = lax.broadcasted_iota(jnp.int32, (16, 128), 0)
     iota = [(base + 16 * j).astype(F32).astype(BF) for j in range(LO // 16)]
     one = jnp.ones((16, 128), BF)
     zero = jnp.zeros((16, 128), BF)
     for b in range(NB):
-        hi, lo, v = (
-            jnp.broadcast_to(ref[b : b + 1, :], (16, 128)).astype(BF)
-            for ref in (hi_ref, lo_ref, v_ref)
-        )
+        hi, lo, v = (jnp.broadcast_to(row, (16, 128)).astype(BF) for row in rows_of(b))
         a = jnp.concatenate([jnp.where(hi == iota[j], v, zero) for j in range(HI // 16)], 0)
         c = jnp.concatenate([jnp.where(lo == iota[j], one, zero) for j in range(LO // 16)], 0)
         s = dot(a, c, NT)
-        left[pl.ds(b, HI, stride=PITCH), :] = s[:, :128]
-        right[pl.ds(b, HI, stride=PITCH), :] = s[:, 128:]
-
-    def split(i, carry):
-        for u in range(4):
-            h = i * 4 + u
-            at = pl.multiple_of(h * PITCH, 8)
-            x = jnp.concatenate([left[pl.ds(at, NB), :], right[pl.ds(at, NB), :]], 1)
-            head_ref[h], rest_ref[h] = halves(x)
-        return carry
-
-    lax.fori_loop(0, HI // 4, split, 0)
-
-
-def build_more_kernel(hi_ref, lo_ref, v_ref, head_in, rest_in, *refs):
-    build_kernel(hi_ref, lo_ref, v_ref, *refs)
+        left[b * PITCH : b * PITCH + HI, :] = s[:, :128]
+        right[b * PITCH : b * PITCH + HI, :] = s[:, 128:]
+
+
+def write_blocks(left, right, buf, out_ref, at, sem, value_of):
+    quarter = HI // 4
+    for q in range(4):
+
+        def some(i, carry, q=q):
+            for u in range(16):
+                h = q * quarter + i * 16 + u
+                blocks = pl.ds(h, NB, stride=PITCH)
+                buf[h] = value_of(jnp.concatenate([left[blocks, :], right[blocks, :]], 1))
+            return carry
+
+        lax.fori_loop(0, quarter // 16, some, 0)
+        rows = pl.ds(q * quarter, quarter)
+        pltpu.make_async_copy(buf.at[rows], out_ref.at[rows, pl.ds(at, NB), :], sem).start()
+
+
+def written(buf, out_ref, sem):
+    return pltpu.make_async_copy(buf, out_ref.at[:, pl.ds(0, NB), :], sem)
+
+
+def build_kernel(first, hi_ref, lo_ref, v_ref, *refs):
+    head_ref, left, right, buf, sem = refs[-5:]
+    step = pl.program_id(0)
+    slot = lax.rem(step, 2)
+    spread_blocks(
+        lambda b: [ref[b : b + 1, :] for ref in (hi_ref, lo_ref, v_ref)], left, right
+    )
+
+    @pl.when(step >= 2)
+    def _():
+        written(buf.at[slot], head_ref, sem.at[slot]).wait()
+
+    at = pl.multiple_of((first + step) * NB, NB)
+    write_blocks(
+        left, right, buf.at[slot], head_ref, at, sem.at[slot], lambda x: x.astype(BF)
+    )
+
+    @pl.when(step == pl.num_programs(0) - 1)
+    def _():
+        for i in range(2):
+            written(buf.at[i], head_ref, sem.at[i]).wait()
 
 
 def build(hi, lo, v):
     n = hi.shape[0]
     steps = n // NB // PARTS
-    shape = jax.ShapeDtypeStruct((HI, n, LO), BF)
     made = ()
     for part in range(PARTS):
-        spec = pl.BlockSpec((NB, 128), lambda i, at=part * steps: (at + i, 0))
-        out = pl.BlockSpec((HI, NB, LO), lambda i, at=part * steps: (0, at + i, 0))
+        first = part * steps
+        spec = pl.BlockSpec((NB, 128), lambda i, first=first: (first + i, 0))
         call = pl.pallas_call(
-            build_more_kernel if made else build_kernel,
+            functools.partial(build_kernel, first),
             grid=(steps,),
             in_specs=[spec] * 3 + [pl.BlockSpec(memory_space=pl.ANY)] * len(made),
-            out_specs=[out, out],
-            out_shape=[shape, shape],
-            scratch_shapes=[pltpu.VMEM((HI * PITCH, 128), F32)] * 2,
-            input_output_aliases={3 + i: i for i in range(len(made))},
+            out_specs=pl.BlockSpec(memory_space=pl.ANY),
+            out_shape=jax.ShapeDtypeStruct((HI, n, LO), BF),
+            scratch_shapes=[pltpu.VMEM((NB * PITCH, 128), F32)] * 2
+            + [pltpu.VMEM((2, HI, NB, LO), BF), pltpu.SemaphoreType.DMA((2,))],
+            input_output_aliases={3: 0} if made else {},
             cost_estimate=pl.CostEstimate(
-                flops=40_000_000_000 // PARTS,
-                bytes_accessed=n * HI * LO * 4 // PARTS,
+                flops=30_000_000_000 // PARTS,
+                bytes_accessed=n * HI * LO * 2 // PARTS,
                 transcendentals=0,
             ),
         )
-        made = call(hi, lo, v, *made)
-    return made
+        made = (call(hi, lo, v, *made),)
+    return made[0]
+
+
+def groups_of(count):
+    return (count + GROUP - 1) // GROUP
+
+
+def rest_kernel(count_ref, list_ref, hi_ref, lo_ref, v_ref, rest_ref, left, right, buf, sem):
+    count = count_ref[0]
+
+    def some(i, carry):
+        def rows_of(b):
+            slot = i * NB + b
+            block = list_ref[0, slot]
+            on = jnp.where(slot < count, 1.0, 0.0).astype(F32)
+            hi, lo, v = (ref[pl.ds(block, 1), :] for ref in (hi_ref, lo_ref, v_ref))
+            return hi, lo, v * on
+
+        spread_blocks(rows_of, left, right)
+
+        @pl.when(i > 0)
+        def _():
+            written(buf, rest_ref, sem).wait()
+
+        at = pl.multiple_of(i * NB, NB)
+        write_blocks(
+            left, right, buf, rest_ref, at, sem, lambda x: (x - x.astype(BF).astype(F32)).astype(BF)
+        )
+        return carry
+
+    lax.fori_loop(0, groups_of(count) * (GROUP // NB), some, 0)
+
+    @pl.when(count > 0)
+    def _():
+        written(buf, rest_ref, sem).wait()
+
+
+def build_rest(count, listed, hi, lo, v):
+    n = hi.shape[0]
+    return pl.pallas_call(
+        rest_kernel,
+        in_specs=[pl.BlockSpec(memory_space=pltpu.SMEM)] * 2
+        + [pl.BlockSpec(memory_space=pltpu.VMEM)] * 3,
+        out_specs=pl.BlockSpec(memory_space=pl.ANY),
+        out_shape=jax.ShapeDtypeStruct((HI, n, LO), BF),
+        scratch_shapes=[pltpu.VMEM((NB * PITCH, 128), F32)] * 2
+        + [pltpu.VMEM((HI, NB, LO), BF), pltpu.SemaphoreType.DMA],
+        cost_estimate=pl.CostEstimate(
+            flops=6_000_000_000, bytes_accessed=6_000_000, transcendentals=0
+        ),
+    )(count, listed, hi, lo, v)
 
 
 def place(i):
@@ -205,7 +344,7 @@
     return jnp.concatenate([array.ravel(), index.ravel(), order[None]]).astype(jnp.int32)
 
 
-def fetch(table, pieces, buf, sem, step, slot):
+def fetch(table, count, rest, pieces, buf, rest_buf, sem, rest_sem, step, slot):
     n = buf.shape[1]
     for p in range(n):
         array = table[step * n + p]
@@ -216,86 +355,138 @@
             def _(ref=ref, p=p):
                 pltpu.make_async_copy(ref.at[index], buf.at[slot, p], sem.at[slot]).start()
 
-
-def accumulate(table, head_ref, rest_ref, pieces, fold_ref, gram_ref, buf, sem, begin):
+    @pl.when(count > 0)
+    def _():
+        rest_copy(table, rest, rest_buf, rest_sem, step, slot, 0).start()
+
+
+def rest_copy(table, rest, rest_buf, rest_sem, step, slot, group):
+    first = pl.multiple_of((2 * step + table[128]) * STEP, STEP)
+    at = pl.multiple_of(group * GROUP, GROUP)
+    return pltpu.make_async_copy(
+        rest.at[pl.ds(first, STEP), pl.ds(at, GROUP), :], rest_buf.at[slot], rest_sem.at[slot]
+    )
+
+
+def accumulate(table, count_ref, head_ref, rest, pieces, sums, bufs, begin):
+    fold_ref, gram_ref, extra_ref = sums
+    buf, rest_buf, sem, rest_sem = bufs
     step = pl.program_id(0)
     slot = lax.rem(step, 2)
+    count = count_ref[0]
 
     @pl.when(step == 0)
     def _():
         begin()
-        fetch(table, pieces, buf, sem, 0, 0)
+        fetch(table, count, rest, pieces, *bufs, 0, 0)
+
+        @pl.when(count == 0)
+        def _():
+            rest_buf[...] = jnp.zeros_like(rest_buf)
 
     @pl.when(step + 1 < pl.num_programs(0))
     def _():
-        fetch(table, pieces, buf, sem, step + 1, 1 - slot)
+        fetch(table, count, rest, pieces, *bufs, step + 1, 1 - slot)
 
     pltpu.make_async_copy(pieces[0].at[pl.ds(0, buf.shape[1])], buf.at[slot], sem.at[slot]).wait()
+
+    @pl.when(count > 0)
+    def _():
+        rest_copy(table, rest, rest_buf, rest_sem, step, slot, 0).wait()
+
+    def listed(at):
+        return jnp.concatenate([rest_buf[at, i] for i in range(STEP)], 1)
+
     t = buf[slot].reshape(256, STEP * LO)
     head = jnp.concatenate([head_ref[i] for i in range(STEP)], 1)
-    rest = jnp.concatenate([rest_ref[i] for i in range(STEP)], 1)
-    fold_ref[...] += dot(head, t, NT) + dot(rest, t, NT)
-    gram_ref[...] += dot(t, t, NT)
-
-
-def first_kernel(table, head_ref, rest_ref, p0, p1, p2, p3, p4, fold_ref, gram_ref, buf, sem):
+    fold_ref[...] += dot(head, t, NT)
+    both = dot(jnp.concatenate([t, listed(slot)], 0), t, NT)
+    gram_ref[...] += both[:256]
+    extra_ref[:GROUP] += both[256:]
+
+    def more(group, carry):
+        copy = rest_copy(table, rest, rest_buf, rest_sem, step, slot, group)
+        copy.start()
+        copy.wait()
+        at = pl.multiple_of(group * GROUP, GROUP)
+        extra_ref[pl.ds(at, GROUP), :] += dot(listed(slot), buf[slot].reshape(256, STEP * LO), NT)
+        return carry
+
+    lax.fori_loop(1, groups_of(count), more, 0)
+
+
+def first_kernel(
+    table, count_ref, head_ref, rest, p0, p1, p2, p3, p4, fold_ref, gram_ref, extra_ref, *bufs
+):
+    sums = (fold_ref, gram_ref, extra_ref)
+
     def begin():
-        fold_ref[...] = jnp.zeros_like(fold_ref)
-        gram_ref[...] = jnp.zeros_like(gram_ref)
-
-    accumulate(
-        table, head_ref, rest_ref, (p0, p1, p2, p3, p4), fold_ref, gram_ref, buf, sem, begin
-    )
+        for ref in sums:
+            ref[...] = jnp.zeros_like(ref)
+
+    accumulate(table, count_ref, head_ref, rest, (p0, p1, p2, p3, p4), sums, bufs, begin)
 
 
 def second_kernel(
-    table, head_ref, rest_ref, p0, p1, p2, p3, p4,
-    fold_in, gram_in, second_ref, owner_ref, part_ref, gram_ref, acc, buf, sem,
+    table, count_ref, head_ref, rest, p0, p1, p2, p3, p4, fold_in, gram_in, extra_in,
+    second_ref, owner_ref, list_ref, part_ref, gram_ref, fold_ref, extra_ref, *bufs,
 ):
     def begin():
-        acc[...] = fold_in[...]
+        fold_ref[...] = fold_in[...]
         gram_ref[...] = gram_in[...]
-
-    accumulate(table, head_ref, rest_ref, (p0, p1, p2, p3, p4), acc, gram_ref, buf, sem, begin)
+        extra_ref[...] = extra_in[...]
+
+    sums = (fold_ref, gram_ref, extra_ref)
+    accumulate(table, count_ref, head_ref, rest, (p0, p1, p2, p3, p4), sums, bufs, begin)
 
     @pl.when(pl.program_id(0) == pl.num_programs(0) - 1)
     def _():
-        head, rest = halves(second_ref[...].astype(F32) * acc[...])
         n = owner_ref.shape[1]
+        block = lax.broadcasted_iota(jnp.int32, (n, n), 0)
+        place = lax.broadcasted_iota(jnp.int32, (n, n), 1)
+        own = (block == list_ref[...]) & (place < count_ref[0])
+        own = jnp.where(own, 1.0, 0.0).astype(BF)
+        head, rest = halves(extra_ref[...])
+        fold = fold_ref[...] + (dot(own, head, NN) + dot(own, rest, NN))
+        head, rest = halves(second_ref[...].astype(F32) * fold)
         slot = lax.broadcasted_iota(jnp.int32, (part_ref.shape[0], n), 0)
         hot = (slot == owner_ref[...]).astype(F32).astype(BF)
         part_ref[...] = dot(hot, head, NN) + dot(hot, rest, NN)
 
 
-def product(table, head, rest, pieces, more, slab):
+def product(table, count, head, rest, pieces, more, slab):
     n = head.shape[1]
     steps = HI // STEP // 2
-    s_spec = pl.BlockSpec((STEP, n, LO), lambda i, table: (2 * i + table[128], 0, 0))
     any_spec = pl.BlockSpec(memory_space=pl.ANY)
-    whole = lambda x: pl.BlockSpec(x.shape, lambda i, table: (0, 0))
-    rows = slab if more else n
-    out = [jax.ShapeDtypeStruct((rows, 256), F32), jax.ShapeDtypeStruct((256, 256), F32)]
-    shape = pieces[0].shape
+    whole = lambda x: pl.BlockSpec(x.shape, lambda i, *scalars: (0, 0))
+    sums = [jax.ShapeDtypeStruct((rows, 256), F32) for rows in (n, 256, n)]
+    out = [jax.ShapeDtypeStruct((slab, 256), F32), sums[1]] if more else sums
     scratch = [
-        pltpu.VMEM((2, 8, *shape[1:]), BF),
+        pltpu.VMEM((2, 8, *pieces[0].shape[1:]), BF),
+        pltpu.VMEM((2, STEP, GROUP, LO), BF),
+        pltpu.SemaphoreType.DMA((2,)),
         pltpu.SemaphoreType.DMA((2,)),
     ]
     if more:
-        scratch = [pltpu.VMEM((n, 256), F32)] + scratch
+        scratch = [pltpu.VMEM((n, 256), F32)] * 2 + scratch
     return pl.pallas_call(
         second_kernel if more else first_kernel,
         grid_spec=pltpu.PrefetchScalarGridSpec(
-            num_scalar_prefetch=1,
+            num_scalar_prefetch=2,
             grid=(steps,),
-            in_specs=[s_spec, s_spec] + [any_spec] * 5 + [whole(x) for x in more],
+            in_specs=[
+                pl.BlockSpec((STEP, n, LO), lambda i, table, count: (2 * i + table[128], 0, 0))
+            ]
+            + [any_spec] * 6
+            + [whole(x) for x in more],
             out_specs=[whole(x) for x in out],
             scratch_shapes=scratch,
         ),
         out_shape=out,
         cost_estimate=pl.CostEstimate(
-            flops=15_000_000_000, bytes_accessed=50_000_000, transcendentals=0
-        ),
-    )(table, head, rest, *pieces, *more)
+            flops=15_000_000_000, bytes_accessed=30_000_000, transcendentals=0
+        ),
+    )(table, count, head, rest, *pieces, *more)
 
 
 def exact(a, b, dims):
@@ -394,7 +585,6 @@
     n_cols = lax.axis_size("cols")
     row_at = lax.axis_index("rows")
     col_at = lax.axis_index("cols")
-    nblk, width = block_values.shape
     range_rows = second_factor.shape[0]
     slab = range_rows * n_cols // n_rows
 
@@ -408,17 +598,19 @@
     )
     gram_second = summed_over_cols(local_gram)
 
-    lane = jnp.arange(width, dtype=jnp.int32)
-    slot = jnp.arange(nblk, dtype=jnp.int32)
-    live = (lane[None, :] < block_length[:, None]) & (slot < live_blocks[0])[:, None]
-    values = jnp.where(live, block_values, jnp.zeros((), BF)).astype(F32)
-    head, rest = build(
-        (block_third // LO).astype(F32), (block_third % LO).astype(F32), values
-    )
+    hi, lo, v, listed, count = prepare(block_third, block_values, block_length, live_blocks)
+    head = build(hi, lo, v)
+    rest = build_rest(count, listed, hi, lo, v)
     owner = (block_owner - row_at * slab)[None, :]
-    fold = product(piece_table(row_at, col_at, core), head, rest, own, (), slab)
+    sums = product(piece_table(row_at, col_at, core), count, head, rest, own, (), slab)
     part, gram_third = product(
-        piece_table(row_at, col_at, 1 - core), head, rest, swapped, (*fold, picked, owner), slab
+        piece_table(row_at, col_at, 1 - core),
+        count,
+        head,
+        rest,
+        swapped,
+        (*sums, picked, owner, listed),
+        slab,
     )
 
     gram = (gram_second / (range_rows * n_cols)) * (

time: 225 us -> 205 us (0.911)
  waiting for transfers between devices: 34.8 us -> 21.5 us
  Pallas kernels: 103 us -> 94.2 us
  starting transfers between devices: 38.1 us -> 45.9 us
  other arithmetic: 12.1 us -> 7.46 us
    ppermute x20, waiting for transfers between devices: 24.9 us -> 16.1 us  [shifted(): return lax.ppermute(value, AXES, pairs)]
    ppermute x20, starting transfers between devices: 28.7 us -> 36.5 us  [shifted(): return lax.ppermute(value, AXES, pairs)]
    pallas_call x2, Pallas kernels: 43.2 us -> 36.1 us  [product(): pl.pallas_call(second_kernel if more else first_kernel, grid_spec=pltpu.P...]
    ppermute x3, waiting for transfers between devices: 4.49 us -> 0.01 us  [summed_over_cols(): other = lax.ppermute(value, AXES, pairs)]
    convert_element_type x2 -> x0, other arithmetic: 3.82 us -> none  [the longest x1 2 us: per_device(): (block_third % LO).astype(F32)]
    unnamed x23 -> x21, local copies, waits for them, and re-layouts: 4.57 us -> 3.04 us
    pallas_call x4 -> x6, Pallas kernels: 44.3 us -> 43 us  [the longest x4 28.5 us: build(): made = (call(hi, lo, v, *made),)]
  transfers between devices with their start and end apart: 24 -> 24, of which waited for: 7 -> 6; matrix products, arithmetic and copies ran while one was open for 7% -> 6% of each run, Pallas kernels for 45% -> 45%
where the time goes in v5:
time: 205 us; the launch traced here: 203 us
  Pallas kernels  94.2 us (46%)
  starting transfers between devices  45.9 us (22%)
  waiting for transfers between devices  21.5 us (10%)
  blocking collectives  21.4 us (10%)
  local copies, waits for them, and re-layouts  10.8 us (5%)
  other arithmetic  7.46 us (4%)
    ppermute x20, starting transfers between devices, shifted(): return lax.ppermute(value, AXES, pairs)  36.5 us
    pallas_call x2, Pallas kernels, product(): pl.pallas_call(second_kernel if more else first_kernel, grid_spec=pltpu.P...  36.1 us
    pallas_call x4, Pallas kernels, build(): made = (call(hi, lo, v, *made),)  28.5 us
    ppermute x20, waiting for transfers between devices, shifted(): return lax.ppermute(value, AXES, pairs)  16.1 us
    all_to_all x1, blocking collectives, per_device(): moved = lax.all_to_all(solved, 'rows', 0, 0, tiled=True)  12.6 us
    pallas_call x1, Pallas kernels, inverse(): pl.pallas_call(inverse_kernel, out_shape=[jax.ShapeDtypeStruct((n, n), F3...  9.79 us
    all_to_all x1, blocking collectives, per_device(): moved = lax.all_to_all(moved, 'cols', 0, 0, tiled=True)  8.79 us
    pallas_call x1, Pallas kernels, prepare(): pl.pallas_call(prepare_kernel, grid=(n // rows,), in_specs=[pl.BlockSpec(...  8.11 us
  transfers between devices with their start and end apart: 24, of which 6 were waited for; matrix products, arithmetic and copies ran while one was open for 6% of the time, Pallas kernels for 45%

profile of v5, /device:TPU:0, one launch (start us, length us, event | category | flops | bytes accessed | tf_op | source)
XLA Modules:
  0.0 203.2 jit_solution(782730220327253662)
XLA Ops:
  0.0 0.9 dynamic-slice_bitcast_fusion.1
  0.9 0.9 fusion.11
  2.0 1.5 copy.16.length_ref
  4.2 8.1 %shard_map.83 = (f32[512,128]{1,0:T(8,128)}, f32[512,128]{1,0:T(8,128)}, f32[512,128]{1,0:T(8,128)}, s32[1,512]{1,0:T(1,128)}, s32[1]{0:T(128)}) custom-call(s32[1]{0:T(128)S(6)} %copy.39.live_ref, s32[512,128]{1,0:T(8,128)} %third_ref.1, bf16[512,128]{1,0:T(8,128)(2,1)} %value_ref.1, s32[512,1]{1,0:T(8,128)} %copy.16.length_ref), custom_call_target="tpu_custom_call" | custom-call | flops 3000000000 | bytes 1000000 | tf_op jit(solution)/shard_map/pallas_call | solution.py:77
  12.3 7.1 %shard_map.84.refs_0_ = bf16[128,512,256]{2,1,0:T(8,128)(2,1)} custom-call(f32[512,128]{1,0:T(8,128)} %get-tuple-element.26.hi_ref, f32[512,128]{1,0:T(8,128)} %get-tuple-element.27.lo_ref, f32[512,128]{1,0:T(8,128)} %get-tuple-element.28.v_ref), custom_call_target="tpu_custom_call" | custom-call | flops 7500000256 | bytes 8388608 | tf_op jit(solution)/shard_map/pallas_call | solution.py:176
  19.6 3.2 %collective-permute-start.10 = (bf16[1,2,16,2048]{3,2,1,0:T(8,128)(2,1)S(1)}, bf16[1,2,16,2048]{3,2,1,0:T(8,128)(2,1)S(1)}, u32[]{:S(2)}, u32[]{:S(2)}) collective-permute-start(bf16[1,2,16,2048]{3,2,1,0:T(8,128)(2,1)S(1)} %get-tuple-element.66), channel_id=1, source_target_pairs={{0,32},{1,33},{2,34},{3,35},{4,36},{5,37},{6,38},{7,39},{8,12},{9,... | collective-permute-start | bytes 393224 | tf_op jit(solution)/shard_map/ppermute | solution.py:250
  23.4 2.6 %collective-permute-start.9 = (bf16[1,2,16,2048]{3,2,1,0:T(8,128)(2,1)S(1)}, bf16[1,2,16,2048]{3,2,1,0:T(8,128)(2,1)S(1)}, u32[]{:S(2)}, u32[]{:S(2)}) collective-permute-start(bf16[1,2,16,2048]{3,2,1,0:T(8,128)(2,1)S(1)} %get-tuple-element.66), channel_id=1, source_target_pairs={{0,48},{1,49},{2,50},{3,51},{4,52},{5,53},{6,54},{7,55},{8,14},{9,... | collective-permute-start | bytes 393224 | tf_op jit(solution)/shard_map/ppermute | solution.py:250
  26.6 2.4 %collective-permute-done.8 = bf16[1,2,16,2048]{3,2,1,0:T(8,128)(2,1)S(1)} collective-permute-done((bf16[1,2,16,2048]{3,2,1,0:T(8,128)(2,1)S(1)}, bf16[1,2,16,2048]{3,2,1,0:T(8,128)(2,1)S(1)}, u32[]{:S(2)}, u32[]{:S(2)}) %collective-permute-start.8) | collective-permute-done | bytes 131104 | tf_op jit(solution)/shard_map/ppermute | solution.py:250
  29.0 1.7 collective-permute-start.11
  30.7 1.6 collective-permute-start.12
  32.3 2.0 collective-permute-start.13
  34.3 7.1 %shard_map.85.refs_0_ = bf16[128,512,256]{2,1,0:T(8,128)(2,1)} custom-call(f32[512,128]{1,0:T(8,128)} %get-tuple-element.26.hi_ref, f32[512,128]{1,0:T(8,128)} %get-tuple-element.27.lo_ref, f32[512,128]{1,0:T(8,128)} %get-tuple-element.28.v_ref, bf16[128,512,256]{2,1,0:T(8,128)(2,1)} %shard_map.84.refs_0_), custom_call_target="tpu_custom_call", output_to_operand_aliasing={{}: (3, {})} | custom-call | flops 7500000256 | bytes 8388608 | tf_op jit(solution)/shard_map/pallas_call | solution.py:176
  41.5 0.8 copy-done.5
  42.3 4.1 %collective-permute-done.13 = bf16[1,4,2,16,2048]{4,3,2,1,0:T(8,128)(2,1)} collective-permute-done((bf16[1,4,2,16,2048]{4,3,2,1,0:T(8,128)(2,1)S(1)}, bf16[1,4,2,16,2048]{4,3,2,1,0:T(8,128)(2,1)}, u32[]{:S(2)}, u32[]{:S(2)}) %collective-permute-start.13) | collective-permute-done | bytes 524320 | tf_op jit(solution)/shard_map/ppermute | solution.py:250
  46.5 1.5 pad_maximum_fusion.1
  47.9 2.0 collective-permute-start.15
  49.9 2.2 %collective-permute-start.17 = (bf16[4,4,2,16,2048]{4,3,2,1,0:T(8,128)(2,1)S(1)}, bf16[4,4,2,16,2048]{4,3,2,1,0:T(8,128)(2,1)}, u32[]{:S(2)}, u32[]{:S(2)}) collective-permute-start(bf16[4,4,2,16,2048]{4,3,2,1,0:T(8,128)(2,1)S(1)} %pad_maximum_fusion.1), channel_id=1, source_target_pairs={{0,65},{1,0},{2,67},{3,2},{4,69},{5,4},{6,71},{7,6},{8,56},{9,57},... | collective-permute-start | bytes 6291464 | tf_op jit(solution)/shard_map/ppermute | solution.py:250
  52.1 7.1 %shard_map.86.refs_0_ = bf16[128,512,256]{2,1,0:T(8,128)(2,1)} custom-call(f32[512,128]{1,0:T(8,128)} %get-tuple-element.26.hi_ref, f32[512,128]{1,0:T(8,128)} %get-tuple-element.27.lo_ref, f32[512,128]{1,0:T(8,128)} %get-tuple-element.28.v_ref, bf16[128,512,256]{2,1,0:T(8,128)(2,1)} %shard_map.85.refs_0_), custom_call_target="tpu_custom_call", output_to_operand_aliasing={{}: (3, {})} | custom-call | flops 7500000256 | bytes 8388608 | tf_op jit(solution)/shard_map/pallas_call | solution.py:176
  59.5 3.1 %collective-permute-start.2 = (bf16[1,2,16,2048]{3,2,1,0:T(8,128)(2,1)S(1)}, bf16[1,2,16,2048]{3,2,1,0:T(8,128)(2,1)S(1)}, u32[]{:S(2)}, u32[]{:S(2)}) collective-permute-start(bf16[1,2,16,2048]{3,2,1,0:T(8,128)(2,1)S(1)} %get-tuple-element.65), channel_id=1, source_target_pairs={{0,48},{1,49},{2,50},{3,51},{4,52},{5,53},{6,54},{7,55},{8,56},{9,... | collective-permute-start | bytes 393224 | tf_op jit(solution)/shard_map/ppermute | solution.py:250
  62.6 1.4 collective-permute-start.3
  64.5 0.6 pad_add_fusion.2.table
  65.2 1.7 collective-permute-done.1
  66.9 4.3 %collective-permute-done.3 = bf16[1,2,16,2048]{3,2,1,0:T(8,128)(2,1)S(1)} collective-permute-done((bf16[1,2,16,2048]{3,2,1,0:T(8,128)(2,1)S(1)}, bf16[1,2,16,2048]{3,2,1,0:T(8,128)(2,1)S(1)}, u32[]{:S(2)}, u32[]{:S(2)}) %collective-permute-start.3) | collective-permute-done | bytes 131104 | tf_op jit(solution)/shard_map/ppermute | solution.py:250
  71.2 1.9 collective-permute-start.4
  73.1 6.5 %shard_map.88.rest = bf16[128,512,256]{2,1,0:T(8,128)(2,1)} custom-call(s32[1]{0:T(128)} %get-tuple-element.25.count_ref, s32[1,512]{1,0:T(1,128)} %get-tuple-element.29.list_ref, f32[512,128]{1,0:T(8,128)} %get-tuple-element.26.hi_ref, f32[512,128]{1,0:T(8,128)} %get-tuple-element.27.lo_ref, f32[512,128]{1,0:T(8,128)} %get-tuple-element.28.v_ref), custom_call_target="tpu_custom_call" | custom-call | flops 6000000000 | bytes 6000000 | tf_op jit(solution)/shard_map/pallas_call | solution.py:216
  79.6 3.6 %collective-permute-done.4.remote_ref = bf16[4,2,16,2048]{3,2,1,0:T(8,128)(2,1)} collective-permute-done((bf16[4,2,16,2048]{3,2,1,0:T(8,128)(2,1)S(1)}, bf16[4,2,16,2048]{3,2,1,0:T(8,128)(2,1)}, u32[]{:S(2)}, u32[]{:S(2)}) %collective-permute-start.4) | collective-permute-done | bytes 524320 | tf_op jit(solution)/shard_map/ppermute | solution.py:250
  83.2 3.1 %shard_map.82 = (bf16[512,256]{1,0:T(8,128)(2,1)}, f32[256,256]{1,0:T(8,128)}) custom-call(s32[5]{0:T(128)} %pad_add_fusion.2.table, bf16[4,2,16,2048]{3,2,1,0:T(8,128)(2,1)} %copy-done.4, bf16[4,2,16,2048]{3,2,1,0:T(8,128)(2,1)} %collective-permute-done.4.remote_ref, s32[1,512]{1,0:T(1,128)} %bitcast.90), custom_call_target="tpu_custom_call" | custom-call | flops 2000000000 | bytes 2000000 | tf_op jit(solution)/shard_map/pallas_call | solution.py:318
  86.3 1.4 collective-permute-start.5
  87.7 2.4 %slice.92 = bf16[2,4,2,16,2048]{4,3,2,1,0:T(8,128)(2,1)} slice(bf16[4,4,2,16,2048]{4,3,2,1,0:T(8,128)(2,1)} %collective-permute-done.15), slice={[0:2], [0:4], [0:2], [0:16], [0:2048]} | slice | bytes 2097152 | tf_op jit(solution)/shard_map/slice | solution.py:291
  90.7 2.3 %slice.93 = bf16[2,4,2,16,2048]{4,3,2,1,0:T(8,128)(2,1)} slice(bf16[4,4,2,16,2048]{4,3,2,1,0:T(8,128)(2,1)} %collective-permute-done.17), slice={[2:4], [0:4], [0:2], [0:16], [0:2048]} | slice | bytes 2097152 | tf_op jit(solution)/shard_map/slice | solution.py:292
  93.0 2.6 %collective-permute-start.21 = (bf16[2,4,2,16,2048]{4,3,2,1,0:T(8,128)(2,1)}, bf16[2,4,2,16,2048]{4,3,2,1,0:T(8,128)(2,1)}, u32[]{:S(2)}, u32[]{:S(2)}) collective-permute-start(bf16[2,4,2,16,2048]{4,3,2,1,0:T(8,128)(2,1)} %slice.93), channel_id=1, source_target_pairs={{0,65},{1,0},{2,67},{3,2},{4,69},{5,4},{6,71},{7,6},{8,56},{9,57},... | collective-permute-start | bytes 3145736 | tf_op jit(solution)/shard_map/ppermute | solution.py:250
  95.6 0.6 pad_add_fusion.1.table
  96.3 1.5 collective-permute-start.6
  99.0 5.7 %collective-permute-start.14 = (bf16[16,2,16,2048]{3,2,1,0:T(8,128)(2,1)S(1)}, bf16[16,2,16,2048]{3,2,1,0:T(8,128)(2,1)}, u32[]{:S(2)}, u32[]{:S(2)}) collective-permute-start(bf16[16,2,16,2048]{3,2,1,0:T(8,128)(2,1)S(1)} %bitcast.78), channel_id=1, source_target_pairs={{0,8},{1,9},{2,10},{3,11},{4,12},{5,13},{6,14},{7,15},{8,0},{9,1},... | collective-permute-start | bytes 6291464 | tf_op jit(solution)/shard_map/ppermute | solution.py:250
  104.7 4.4 %collective-permute-start.18 = (bf16[16,2,16,2048]{3,2,1,0:T(8,128)(2,1)}, bf16[16,2,16,2048]{3,2,1,0:T(8,128)(2,1)}, u32[]{:S(2)}, u32[]{:S(2)}) collective-permute-start(bf16[16,2,16,2048]{3,2,1,0:T(8,128)(2,1)} %bitcast.23.p2), channel_id=1, source_target_pairs={{0,8},{1,9},{2,10},{3,11},{4,12},{5,13},{6,14},{7,15},{8,0},{9,1},... | collective-permute-start | bytes 6291464 | tf_op jit(solution)/shard_map/ppermute | solution.py:250
  109.1 7.1 %shard_map.87.head_ref = bf16[128,512,256]{2,1,0:T(8,128)(2,1)} custom-call(f32[512,128]{1,0:T(8,128)} %get-tuple-element.26.hi_ref, f32[512,128]{1,0:T(8,128)} %get-tuple-element.27.lo_ref, f32[512,128]{1,0:T(8,128)} %get-tuple-element.28.v_ref, bf16[128,512,256]{2,1,0:T(8,128)(2,1)} %shard_map.86.refs_0_), custom_call_target="tpu_custom_call", output_to_operand_aliasing={{}: (3, {})} | custom-call | flops 7500000256 | bytes 8388608 | tf_op jit(solution)/shard_map/pallas_call | solution.py:176
  116.3 1.7 add.106
  119.0 17.0 %shard_map.89 = (f32[512,256]{1,0:T(8,128)}, f32[256,256]{1,0:T(8,128)}, f32[512,256]{1,0:T(8,128)}) custom-call(s32[129]{0:T(256)} %pad_add_fusion.1.table, s32[1]{0:T(128)} %get-tuple-element.25.count_ref, bf16[128,512,256]{2,1,0:T(8,128)(2,1)} %shard_map.87.head_ref, bf16[128,512,256]{2,1,0:T(8,128)(2,1)} %shard_map.88.rest, ...), custom_call_target="tpu_custom_call" | custom-call | flops 15000000512 | bytes 30000000 | tf_op jit(solution)/shard_map/pallas_call | solution.py:472
  136.0 2.8 %collective-permute-start.7 = (f32[256,256]{1,0:T(8,128)S(1)}, f32[256,256]{1,0:T(8,128)S(1)}, u32[]{:S(2)}, u32[]{:S(2)}) collective-permute-start(f32[256,256]{1,0:T(8,128)S(1)} %copy-done.3), channel_id=1, source_target_pairs={{0,4},{1,5},{2,6},{3,7},{4,0},{5,1},{6,2},{7,3},{8,12},{9,13},{10,... | collective-permute-start | bytes 786440 | tf_op jit(solution)/shard_map/ppermute | solution.py:271
  138.8 19.1 %shard_map.90 = (f32[1024,256]{1,0:T(8,128)}, f32[256,256]{1,0:T(8,128)}) custom-call(s32[129]{0:T(256)} %pad_add_fusion.table, s32[1]{0:T(128)} %get-tuple-element.25.count_ref, bf16[128,512,256]{2,1,0:T(8,128)(2,1)} %shard_map.87.head_ref, bf16[128,512,256]{2,1,0:T(8,128)(2,1)} %shard_map.88.rest, bf16[16,2,16,2048]{3,2,1,0:T(8,128)(2,1)} %collective-permute-done.14.p0, ...), custom_call_target="tpu_custom_call" | custom-call | flops 15000000512 | bytes 30000000 | tf_op jit(solution)/shard_map/pallas_call | solution.py:472
  157.9 3.7 %all-to-all-start = ((f32[8,128,256]{2,1,0:T(8,128)}), f32[8,128,256]{2,1,0:T(8,128)S(1)}, u32[]{:S(2)}, u32[]{:S(2)}) async-start(f32[8,128,256]{2,1,0:T(8,128)} %bitcast.82), calls=%async_computation | async-start | bytes 2097152 | tf_op jit(solution)/shard_map/all_to_all | solution.py:620
  161.7 9.8 %shard_map.91 = (f32[256,256]{1,0:T(8,128)S(1)}, s32[1]{0:T(128)}) custom-call(f32[256,256]{1,0:T(8,128)S(1)} %multiply_multiply_fusion.gram_ref), custom_call_target="tpu_custom_call" | custom-call | flops 5000000000 | bytes 600000 | tf_op jit(solution)/shard_map/pallas_call | solution.py:536
  172.4 5.3 %all-to-all-done.spread_ref = f32[8,128,256]{2,1,0:T(8,128)S(1)} async-done(((f32[8,128,256]{2,1,0:T(8,128)}), f32[8,128,256]{2,1,0:T(8,128)S(1)}, u32[]{:S(2)}, u32[]{:S(2)}) %all-to-all-start) | async-done | bytes 1048608 | tf_op jit(solution)/shard_map/all_to_all | solution.py:620
  177.8 1.0 copy-done.2
  178.8 2.3 %shard_map.92 = f32[16,16,128]{2,1,0:T(8,128)} custom-call(f32[256,256]{1,0:T(8,128)S(1)} %get-tuple-element.131.inverse_ref, f32[8,128,256]{2,1,0:T(8,128)} %copy-done.2), custom_call_target="tpu_custom_call" | custom-call | flops 500000000 | bytes 1500000 | tf_op jit(solution)/shard_map/pallas_call | solution.py:565
  181.0 12.6 %all_to_all.15 = f32[16,16,128]{2,1,0:T(8,128)S(1)} all-to-all(f32[16,16,128]{2,1,0:T(8,128)} %shard_map.92), channel_id=1, replica_groups=mesh['rows'=16,'cols'=8] {'rows'}, dimensions={0} | all-to-all | bytes 262144 | tf_op jit(solution)/shard_map/all_to_all | solution.py:622
  193.6 8.8 %all_to_all.16 = f32[8,2,16,128]{3,2,1,0:T(8,128)S(1)} all-to-all(f32[8,2,16,128]{3,2,1,0:T(8,128)S(1)} %bitcast.83), channel_id=1, replica_groups=mesh['rows'=16,'cols'=8] {'cols'}, dimensions={0} | all-to-all | bytes 262144 | tf_op jit(solution)/shard_map/all_to_all | solution.py:625
  202.5 0.7 copy.22
  (70 shorter events, 5.8 us)
Async XLA Ops:
  1.8 17.7 %collective-permute-start = (bf16[2,16,2048]{2,1,0:T(8,128)(2,1)S(1)}, bf16[2,16,2048]{2,1,0:T(8,128)(2,1)S(1)}, u32[]{:S(2)}, u32[]{:S(2)}) collective-permute-start(bf16[2,16,2048]{2,1,0:T(8,128)(2,1)S(1)} %get-tuple-element.70), channel_id=1, source_target_pairs={{0,8},{1,9},{2,10},{3,11},{4,12},{5,13},{6,14},{7,15},{8,0},{9,1},... | collective-permute-start | bytes 393224 | tf_op jit(solution)/shard_map/ppermute | solution.py:250
  12.3 13.7 %copy-start.8 = (s32[512]{0:T(512)S(1)}, s32[512]{0:T(512)}, u32[]{:S(2)}) copy-start(s32[512]{0:T(512)} %param.13) | copy-start | bytes 6148
  19.6 7.0 %collective-permute-start.10 = (bf16[1,2,16,2048]{3,2,1,0:T(8,128)(2,1)S(1)}, bf16[1,2,16,2048]{3,2,1,0:T(8,128)(2,1)S(1)}, u32[]{:S(2)}, u32[]{:S(2)}) collective-permute-start(bf16[1,2,16,2048]{3,2,1,0:T(8,128)(2,1)S(1)} %get-tuple-element.66), channel_id=1, source_target_pairs={{0,32},{1,33},{2,34},{3,35},{4,36},{5,37},{6,38},{7,39},{8,12},{9,... | collective-permute-start | bytes 393224 | tf_op jit(solution)/shard_map/ppermute | solution.py:250
  22.8 6.2 %collective-permute-start.8 = (bf16[1,2,16,2048]{3,2,1,0:T(8,128)(2,1)S(1)}, bf16[1,2,16,2048]{3,2,1,0:T(8,128)(2,1)S(1)}, u32[]{:S(2)}, u32[]{:S(2)}) collective-permute-start(bf16[1,2,16,2048]{3,2,1,0:T(8,128)(2,1)S(1)} %get-tuple-element.66), channel_id=1, source_target_pairs={{0,16},{1,17},{2,18},{3,19},{4,20},{5,21},{6,22},{7,23},{8,10},{9,... | collective-permute-start | bytes 393224 | tf_op jit(solution)/shard_map/ppermute | solution.py:250
  23.4 5.6 %collective-permute-start.9 = (bf16[1,2,16,2048]{3,2,1,0:T(8,128)(2,1)S(1)}, bf16[1,2,16,2048]{3,2,1,0:T(8,128)(2,1)S(1)}, u32[]{:S(2)}, u32[]{:S(2)}) collective-permute-start(bf16[1,2,16,2048]{3,2,1,0:T(8,128)(2,1)S(1)} %get-tuple-element.66), channel_id=1, source_target_pairs={{0,48},{1,49},{2,50},{3,51},{4,52},{5,53},{6,54},{7,55},{8,14},{9,... | collective-permute-start | bytes 393224 | tf_op jit(solution)/shard_map/ppermute | solution.py:250
  29.0 12.5 %collective-permute-start.11 = (bf16[1,4,2,16,2048]{4,3,2,1,0:T(8,128)(2,1)S(1)}, bf16[1,4,2,16,2048]{4,3,2,1,0:T(8,128)(2,1)S(1)}, u32[]{:S(2)}, u32[]{:S(2)}) collective-permute-start(bf16[1,4,2,16,2048]{4,3,2,1,0:T(8,128)(2,1)S(1)} %maximum_bitcast_fusion), channel_id=1, source_target_pairs={{0,2},{1,3},{2,4},{3,5},{4,6},{5,7},{6,0},{7,1},{8,9},{9,72},{10,1... | collective-permute-start | bytes 1572872 | tf_op jit(solution)/shard_map/ppermute | solution.py:250
  30.7 10.8 %collective-permute-start.12 = (bf16[1,4,2,16,2048]{4,3,2,1,0:T(8,128)(2,1)S(1)}, bf16[1,4,2,16,2048]{4,3,2,1,0:T(8,128)(2,1)S(1)}, u32[]{:S(2)}, u32[]{:S(2)}) collective-permute-start(bf16[1,4,2,16,2048]{4,3,2,1,0:T(8,128)(2,1)S(1)} %maximum_bitcast_fusion), channel_id=1, source_target_pairs={{0,6},{1,7},{2,0},{3,1},{4,2},{5,3},{6,4},{7,5},{8,73},{9,8},{10,7... | collective-permute-start | bytes 1572872 | tf_op jit(solution)/shard_map/ppermute | solution.py:250
  32.3 14.1 %collective-permute-start.13 = (bf16[1,4,2,16,2048]{4,3,2,1,0:T(8,128)(2,1)S(1)}, bf16[1,4,2,16,2048]{4,3,2,1,0:T(8,128)(2,1)}, u32[]{:S(2)}, u32[]{:S(2)}) collective-permute-start(bf16[1,4,2,16,2048]{4,3,2,1,0:T(8,128)(2,1)S(1)} %maximum_bitcast_fusion), channel_id=1, source_target_pairs={{0,4},{1,5},{2,6},{3,7},{4,0},{5,1},{6,2},{7,3},{8,72},{9,73},{10,... | collective-permute-start | bytes 1572872 | tf_op jit(solution)/shard_map/ppermute | solution.py:250
  41.5 0.8 copy-start.5
  47.9 51.1 %copy-start = (bf16[4,4,2,16,2048]{4,3,2,1,0:T(8,128)(2,1)}, bf16[4,4,2,16,2048]{4,3,2,1,0:T(8,128)(2,1)S(1)}, u32[]{:S(2)}) copy-start(bf16[4,4,2,16,2048]{4,3,2,1,0:T(8,128)(2,1)S(1)} %pad_maximum_fusion.1) | copy-start | bytes 6291460
  47.9 39.8 %collective-permute-start.15 = (bf16[4,4,2,16,2048]{4,3,2,1,0:T(8,128)(2,1)S(1)}, bf16[4,4,2,16,2048]{4,3,2,1,0:T(8,128)(2,1)}, u32[]{:S(2)}, u32[]{:S(2)}) collective-permute-start(bf16[4,4,2,16,2048]{4,3,2,1,0:T(8,128)(2,1)S(1)} %pad_maximum_fusion.1), channel_id=1, source_target_pairs={{0,1},{1,64},{2,3},{3,66},{4,5},{5,68},{6,7},{7,70},{8,24},{9,25},... | collective-permute-start | bytes 6291464 | tf_op jit(solution)/shard_map/ppermute | solution.py:250
  49.9 40.8 %collective-permute-start.17 = (bf16[4,4,2,16,2048]{4,3,2,1,0:T(8,128)(2,1)S(1)}, bf16[4,4,2,16,2048]{4,3,2,1,0:T(8,128)(2,1)}, u32[]{:S(2)}, u32[]{:S(2)}) collective-permute-start(bf16[4,4,2,16,2048]{4,3,2,1,0:T(8,128)(2,1)S(1)} %pad_maximum_fusion.1), channel_id=1, source_target_pairs={{0,65},{1,0},{2,67},{3,2},{4,69},{5,4},{6,71},{7,6},{8,56},{9,57},... | collective-permute-start | bytes 6291464 | tf_op jit(solution)/shard_map/ppermute | solution.py:250
  59.2 7.7 %collective-permute-start.1 = (bf16[1,2,16,2048]{3,2,1,0:T(8,128)(2,1)S(1)}, bf16[1,2,16,2048]{3,2,1,0:T(8,128)(2,1)S(1)}, u32[]{:S(2)}, u32[]{:S(2)}) collective-permute-start(bf16[1,2,16,2048]{3,2,1,0:T(8,128)(2,1)S(1)} %get-tuple-element.65), channel_id=1, source_target_pairs={{0,16},{1,17},{2,18},{3,19},{4,20},{5,21},{6,22},{7,23},{8,24},{9,... | collective-permute-start | bytes 393224 | tf_op jit(solution)/shard_map/ppermute | solution.py:250
  59.5 7.4 %collective-permute-start.2 = (bf16[1,2,16,2048]{3,2,1,0:T(8,128)(2,1)S(1)}, bf16[1,2,16,2048]{3,2,1,0:T(8,128)(2,1)S(1)}, u32[]{:S(2)}, u32[]{:S(2)}) collective-permute-start(bf16[1,2,16,2048]{3,2,1,0:T(8,128)(2,1)S(1)} %get-tuple-element.65), channel_id=1, source_target_pairs={{0,48},{1,49},{2,50},{3,51},{4,52},{5,53},{6,54},{7,55},{8,56},{9,... | collective-permute-start | bytes 393224 | tf_op jit(solution)/shard_map/ppermute | solution.py:250
  62.6 8.5 %collective-permute-start.3 = (bf16[1,2,16,2048]{3,2,1,0:T(8,128)(2,1)S(1)}, bf16[1,2,16,2048]{3,2,1,0:T(8,128)(2,1)S(1)}, u32[]{:S(2)}, u32[]{:S(2)}) collective-permute-start(bf16[1,2,16,2048]{3,2,1,0:T(8,128)(2,1)S(1)} %get-tuple-element.65), channel_id=1, source_target_pairs={{0,32},{1,33},{2,34},{3,35},{4,36},{5,37},{6,38},{7,39},{8,40},{9,... | collective-permute-start | bytes 393224 | tf_op jit(solution)/shard_map/ppermute | solution.py:250
  71.2 8.4 %copy-start.4 = (bf16[4,2,16,2048]{3,2,1,0:T(8,128)(2,1)}, bf16[4,2,16,2048]{3,2,1,0:T(8,128)(2,1)S(1)}, u32[]{:S(2)}) copy-start(bf16[4,2,16,2048]{3,2,1,0:T(8,128)(2,1)S(1)} %pad_maximum_fusion.2.close_ref) | copy-start | bytes 1572868
  71.2 12.0 %collective-permute-start.4 = (bf16[4,2,16,2048]{3,2,1,0:T(8,128)(2,1)S(1)}, bf16[4,2,16,2048]{3,2,1,0:T(8,128)(2,1)}, u32[]{:S(2)}, u32[]{:S(2)}) collective-permute-start(bf16[4,2,16,2048]{3,2,1,0:T(8,128)(2,1)S(1)} %pad_maximum_fusion.2.close_ref), channel_id=1, source_target_pairs={{0,64},{1,65},{2,66},{3,67},{4,68},{5,69},{6,70},{7,71},{8,72},{9,... | collective-permute-start | bytes 1572872 | tf_op jit(solution)/shard_map/ppermute | solution.py:250
  86.3 10.0 %collective-permute-start.5 = (f32[256,256]{1,0:T(8,128)}, f32[256,256]{1,0:T(8,128)S(1)}, u32[]{:S(2)}, u32[]{:S(2)}) collective-permute-start(f32[256,256]{1,0:T(8,128)} %get-tuple-element.24), channel_id=1, source_target_pairs={{0,1},{1,0},{2,3},{3,2},{4,5},{5,4},{6,7},{7,6},{8,9},{9,8},{10,11... | collective-permute-start | bytes 786440 | tf_op jit(solution)/shard_map/ppermute | solution.py:271
  87.7 8.6 %copy-start.6 = (f32[256,256]{1,0:T(8,128)S(1)}, f32[256,256]{1,0:T(8,128)}, u32[]{:S(2)}) copy-start(f32[256,256]{1,0:T(8,128)} %get-tuple-element.24) | copy-start | bytes 786436
  87.7 10.7 %copy-start.9 = (s32[512]{0:T(512)S(1)}, s32[512]{0:T(512)}, u32[]{:S(2)}) copy-start(s32[512]{0:T(512)} %param.12) | copy-start | bytes 6148
  90.1 27.9 %collective-permute-start.19 = (bf16[2,4,2,16,2048]{4,3,2,1,0:T(8,128)(2,1)}, bf16[2,4,2,16,2048]{4,3,2,1,0:T(8,128)(2,1)S(1)}, u32[]{:S(2)}, u32[]{:S(2)}) collective-permute-start(bf16[2,4,2,16,2048]{4,3,2,1,0:T(8,128)(2,1)} %slice.92), channel_id=1, source_target_pairs={{0,1},{1,64},{2,3},{3,66},{4,5},{5,68},{6,7},{7,70},{8,24},{9,25},... | collective-permute-start | bytes 3145736 | tf_op jit(solution)/shard_map/ppermute | solution.py:250
  93.0 25.0 %collective-permute-start.21 = (bf16[2,4,2,16,2048]{4,3,2,1,0:T(8,128)(2,1)}, bf16[2,4,2,16,2048]{4,3,2,1,0:T(8,128)(2,1)}, u32[]{:S(2)}, u32[]{:S(2)}) collective-permute-start(bf16[2,4,2,16,2048]{4,3,2,1,0:T(8,128)(2,1)} %slice.93), channel_id=1, source_target_pairs={{0,65},{1,0},{2,67},{3,2},{4,69},{5,4},{6,71},{7,6},{8,56},{9,57},... | collective-permute-start | bytes 3145736 | tf_op jit(solution)/shard_map/ppermute | solution.py:250
  96.3 8.4 %collective-permute-start.6 = (f32[256,256]{1,0:T(8,128)S(1)}, f32[256,256]{1,0:T(8,128)}, u32[]{:S(2)}, u32[]{:S(2)}) collective-permute-start(f32[256,256]{1,0:T(8,128)S(1)} %add.105), channel_id=1, source_target_pairs={{0,2},{1,3},{2,0},{3,1},{4,6},{5,7},{6,4},{7,5},{8,10},{9,11},{10,... | collective-permute-start | bytes 786440 | tf_op jit(solution)/shard_map/ppermute | solution.py:271
  99.0 36.9 %collective-permute-start.14 = (bf16[16,2,16,2048]{3,2,1,0:T(8,128)(2,1)S(1)}, bf16[16,2,16,2048]{3,2,1,0:T(8,128)(2,1)}, u32[]{:S(2)}, u32[]{:S(2)}) collective-permute-start(bf16[16,2,16,2048]{3,2,1,0:T(8,128)(2,1)S(1)} %bitcast.78), channel_id=1, source_target_pairs={{0,8},{1,9},{2,10},{3,11},{4,12},{5,13},{6,14},{7,15},{8,0},{9,1},... | collective-permute-start | bytes 6291464 | tf_op jit(solution)/shard_map/ppermute | solution.py:250
  104.7 34.1 %collective-permute-start.16 = (bf16[16,2,16,2048]{3,2,1,0:T(8,128)(2,1)}, bf16[16,2,16,2048]{3,2,1,0:T(8,128)(2,1)}, u32[]{:S(2)}, u32[]{:S(2)}) collective-permute-start(bf16[16,2,16,2048]{3,2,1,0:T(8,128)(2,1)} %bitcast.22.p1), channel_id=1, source_target_pairs={{0,8},{1,9},{2,10},{3,11},{4,12},{5,13},{6,14},{7,15},{8,0},{9,1},... | collective-permute-start | bytes 6291464 | tf_op jit(solution)/shard_map/ppermute | solution.py:250
  104.7 34.1 %collective-permute-start.18 = (bf16[16,2,16,2048]{3,2,1,0:T(8,128)(2,1)}, bf16[16,2,16,2048]{3,2,1,0:T(8,128)(2,1)}, u32[]{:S(2)}, u32[]{:S(2)}) collective-permute-start(bf16[16,2,16,2048]{3,2,1,0:T(8,128)(2,1)} %bitcast.23.p2), channel_id=1, source_target_pairs={{0,8},{1,9},{2,10},{3,11},{4,12},{5,13},{6,14},{7,15},{8,0},{9,1},... | collective-permute-start | bytes 6291464 | tf_op jit(solution)/shard_map/ppermute | solution.py:250
  118.0 1.0 copy-start.1
  118.0 20.8 %collective-permute-start.20 = (bf16[8,2,16,2048]{3,2,1,0:T(8,128)(2,1)S(1)}, bf16[8,2,16,2048]{3,2,1,0:T(8,128)(2,1)}, u32[]{:S(2)}, u32[]{:S(2)}) collective-permute-start(bf16[8,2,16,2048]{3,2,1,0:T(8,128)(2,1)S(1)} %bitcast.80), channel_id=1, source_target_pairs={{0,8},{1,9},{2,10},{3,11},{4,12},{5,13},{6,14},{7,15},{8,0},{9,1},... | collective-permute-start | bytes 3145736 | tf_op jit(solution)/shard_map/ppermute | solution.py:250
  118.0 18.0 %copy-start.3 = (f32[256,256]{1,0:T(8,128)S(1)}, f32[256,256]{1,0:T(8,128)}, u32[]{:S(2)}) copy-start(f32[256,256]{1,0:T(8,128)} %add.106) | copy-start | bytes 786436
  118.0 20.8 %collective-permute-start.22 = (bf16[8,2,16,2048]{3,2,1,0:T(8,128)(2,1)}, bf16[8,2,16,2048]{3,2,1,0:T(8,128)(2,1)}, u32[]{:S(2)}, u32[]{:S(2)}) collective-permute-start(bf16[8,2,16,2048]{3,2,1,0:T(8,128)(2,1)} %bitcast.25.p4), channel_id=1, source_target_pairs={{0,8},{1,9},{2,10},{3,11},{4,12},{5,13},{6,14},{7,15},{8,0},{9,1},... | collective-permute-start | bytes 3145736 | tf_op jit(solution)/shard_map/ppermute | solution.py:250
  136.0 25.6 %collective-permute-start.7 = (f32[256,256]{1,0:T(8,128)S(1)}, f32[256,256]{1,0:T(8,128)S(1)}, u32[]{:S(2)}, u32[]{:S(2)}) collective-permute-start(f32[256,256]{1,0:T(8,128)S(1)} %copy-done.3), channel_id=1, source_target_pairs={{0,4},{1,5},{2,6},{3,7},{4,0},{5,1},{6,2},{7,3},{8,12},{9,13},{10,... | collective-permute-start | bytes 786440 | tf_op jit(solution)/shard_map/ppermute | solution.py:271
  157.9 3.7 %copy-start.7 = (f32[256,256]{1,0:T(8,128)S(1)}, f32[256,256]{1,0:T(8,128)}, u32[]{:S(2)}) copy-start(f32[256,256]{1,0:T(8,128)} %get-tuple-element.34) | copy-start | bytes 786436
  157.9 19.9 %all-to-all-start = ((f32[8,128,256]{2,1,0:T(8,128)}), f32[8,128,256]{2,1,0:T(8,128)S(1)}, u32[]{:S(2)}, u32[]{:S(2)}) async-start(f32[8,128,256]{2,1,0:T(8,128)} %bitcast.82), calls=%async_computation | async-start | bytes 2097152 | tf_op jit(solution)/shard_map/all_to_all | solution.py:620
  177.8 1.0 copy-start.2

commit v6 on v5

--- a/solution.py
+++ b/solution.py
@@ -42,15 +42,22 @@
     third = third_ref[...]
     lane = lax.broadcasted_iota(jnp.int32, (n, width), 1)
     block = lax.broadcasted_iota(jnp.int32, (n, width), 0) + step * n
-    live = (lane < length_ref[...]) & (block < live_ref[0])
+    across = lax.broadcasted_iota(jnp.int32, (n, width), 0) == lane
+    length = jnp.sum(jnp.where(across, length_ref[...].astype(F32), 0.0), 1, keepdims=True)
+    live = (lane.astype(F32) < length) & (block < live_ref[0])
     hi_ref[...] = (third >> 8).astype(F32)
     lo_ref[...] = (third & (LO - 1)).astype(F32)
     v_ref[...] = jnp.where(live, value_ref[...].astype(F32), 0.0)
-    marked = jnp.where(live, third, -1 - lane)
-    same = jnp.zeros((n, width), jnp.bool_)
+    marked = jnp.where(live, third, (1 << 15) + lane)
+    pair = marked[: n // 2] | (marked[n // 2 :] << 16)
+    low = jnp.zeros_like(pair)
+    high = jnp.zeros_like(pair)
     for shift in range(1, width // 2 + 1):
-        same = same | (marked == pltpu.roll(marked, shift, 1))
-    found = jnp.max(jnp.where(same, 1.0, 0.0), 1, keepdims=True)
+        differ = pair ^ pltpu.roll(pair, shift, 1)
+        low = low | ((differ & 0xFFFF) - 1)
+        high = high | (lax.shift_right_logical(differ, 16) - 1)
+    same = jnp.concatenate([jnp.where(x < 0, 1.0, 0.0) for x in (low, high)], 0)
+    found = jnp.max(same, 1, keepdims=True)
     again[pl.ds(pl.multiple_of(step * n, n), n), :] = jnp.broadcast_to(found, (n, width))
 
     @pl.when(step == pl.num_programs(0) - 1)
@@ -81,7 +88,7 @@
             pl.BlockSpec(memory_space=pltpu.SMEM),
             spec,
             spec,
-            pl.BlockSpec((rows, 1), lambda i: (i, 0)),
+            pl.BlockSpec((1, rows), lambda i: (0, i)),
         ],
         out_specs=[spec] * 3
         + [pl.BlockSpec((1, n), lambda i: (0, 0)), pl.BlockSpec(memory_space=pltpu.SMEM)],
@@ -91,7 +98,7 @@
         cost_estimate=pl.CostEstimate(
             flops=3_000_000_000, bytes_accessed=1_000_000, transcendentals=0
         ),
-    )(live, third, values, length[:, None])
+    )(live, third, values, length[None, :])
 
 
 def spread_blocks(rows_of, left, right):
@@ -309,7 +316,7 @@
     r = rows[...]
     gram_ref[...] = dot(r, r, NT)
     at = lax.broadcasted_iota(jnp.int32, (r.shape[1], index_ref.shape[1]), 0)
-    hot = (at == index_ref[...]).astype(F32).astype(BF)
+    hot = (at == index_ref[...] - table[5]).astype(F32).astype(BF)
     picked_ref[...] = dot(r, hot, NN).T.astype(BF)
 
 
@@ -328,7 +335,7 @@
     )(table, close, remote, index)
 
 
-def piece_table(row_at, col_at, order):
+def piece_table(row_at, col_at, order, slab):
     y, z_lo, z_hi, x = jnp.meshgrid(
         jnp.arange(4), jnp.arange(2), jnp.arange(2), jnp.arange(4), indexing="ij"
     )
@@ -341,7 +348,8 @@
     late = (third == 3) & (second >= 2)
     array = third + late
     index = (second - 2 * late) * 4 + first
-    return jnp.concatenate([array.ravel(), index.ravel(), order[None]]).astype(jnp.int32)
+    last = jnp.stack([order, row_at * slab])
+    return jnp.concatenate([array.ravel(), index.ravel(), last]).astype(jnp.int32)
 
 
 def fetch(table, count, rest, pieces, buf, rest_buf, sem, rest_sem, step, slot):
@@ -450,7 +458,7 @@
         fold = fold_ref[...] + (dot(own, head, NN) + dot(own, rest, NN))
         head, rest = halves(second_ref[...].astype(F32) * fold)
         slot = lax.broadcasted_iota(jnp.int32, (part_ref.shape[0], n), 0)
-        hot = (slot == owner_ref[...]).astype(F32).astype(BF)
+        hot = (slot == owner_ref[...] - table[129]).astype(F32).astype(BF)
         part_ref[...] = dot(hot, head, NN) + dot(hot, rest, NN)
 
 
@@ -591,20 +599,21 @@
     core = row_at & 1
     own, swapped, close, remote = gather_tables(third_factor.T, second_factor.T, core)
     spots = jnp.concatenate(
-        [spot(jnp.arange(4, dtype=jnp.int32), row_at >> 1), (row_at >> 3)[None]]
-    )
-    picked, local_gram = pick(
-        spots, close, remote, (block_second - col_at * range_rows)[None, :]
-    )
+        [
+            spot(jnp.arange(4, dtype=jnp.int32), row_at >> 1),
+            jnp.stack([row_at >> 3, col_at * range_rows]),
+        ]
+    )
+    picked, local_gram = pick(spots, close, remote, block_second[None, :])
     gram_second = summed_over_cols(local_gram)
 
     hi, lo, v, listed, count = prepare(block_third, block_values, block_length, live_blocks)
     head = build(hi, lo, v)
     rest = build_rest(count, listed, hi, lo, v)
-    owner = (block_owner - row_at * slab)[None, :]
-    sums = product(piece_table(row_at, col_at, core), count, head, rest, own, (), slab)
+    owner = block_owner[None, :]
+    sums = product(piece_table(row_at, col_at, core, slab), count, head, rest, own, (), slab)
     part, gram_third = product(
-        piece_table(row_at, col_at, 1 - core),
+        piece_table(row_at, col_at, 1 - core, slab),
         count,
         head,
         rest,

time: 205 us -> 206 us (level)
  waiting for transfers between devices: 21.5 us -> 27 us
  Pallas kernels: 94.2 us -> 91.3 us
  starting transfers between devices: 45.9 us -> 43.7 us
    ppermute x3, waiting for transfers between devices: 0.01 us -> 4.5 us  [summed_over_cols(): other = lax.ppermute(value, AXES, pairs)]
    ppermute x20, starting transfers between devices: 36.5 us -> 32.5 us  [shifted(): return lax.ppermute(value, AXES, pairs)]
    pallas_call x1, Pallas kernels: 8.11 us -> 5.31 us  [prepare(): pl.pallas_call(prepare_kernel, grid=(n // rows,), in_specs=[pl.BlockSpec(...]
  transfers between devices with their start and end apart: 24 -> 24, of which waited for: 6 -> 8; matrix products, arithmetic and copies ran while one was open for 6% -> 5% of each run, Pallas kernels for 45% -> 44%
where the time goes in v6:
time: 206 us; the launch traced here: 204 us
  Pallas kernels  91.3 us (44%)
  starting transfers between devices  43.7 us (21%)
  waiting for transfers between devices  27 us (13%)
  blocking collectives  23.2 us (11%)
  local copies, waits for them, and re-layouts  9.45 us (5%)
  other arithmetic  7.23 us (4%)
    pallas_call x2, Pallas kernels, product(): pl.pallas_call(second_kernel if more else first_kernel, grid_spec=pltpu.P...  36 us
    ppermute x20, starting transfers between devices, shifted(): return lax.ppermute(value, AXES, pairs)  32.5 us
    pallas_call x4, Pallas kernels, build(): made = (call(hi, lo, v, *made),)  28.4 us
    ppermute x20, waiting for transfers between devices, shifted(): return lax.ppermute(value, AXES, pairs)  17.3 us
    all_to_all x1, blocking collectives, per_device(): moved = lax.all_to_all(solved, 'rows', 0, 0, tiled=True)  14.4 us
    pallas_call x1, Pallas kernels, inverse(): pl.pallas_call(inverse_kernel, out_shape=[jax.ShapeDtypeStruct((n, n), F3...  9.79 us
    all_to_all x1, blocking collectives, per_device(): moved = lax.all_to_all(moved, 'cols', 0, 0, tiled=True)  8.79 us
    ppermute x3, starting transfers between devices, summed_over_cols(): other = lax.ppermute(value, AXES, pairs)  7.4 us
  transfers between devices with their start and end apart: 24, of which 8 were waited for; matrix products, arithmetic and copies ran while one was open for 5% of the time, Pallas kernels for 44%

profile of v6, /device:TPU:0, one launch (start us, length us, event | category | flops | bytes accessed | tf_op | source)
XLA Modules:
  0.0 203.8 jit_solution(14382293727916207406)
XLA Ops:
  0.0 0.9 dynamic-slice_bitcast_fusion.1
  0.9 0.9 fusion.11
  2.5 5.3 %shard_map.83 = (f32[512,128]{1,0:T(8,128)}, f32[512,128]{1,0:T(8,128)}, f32[512,128]{1,0:T(8,128)}, s32[1,512]{1,0:T(1,128)}, s32[1]{0:T(128)}) custom-call(s32[1]{0:T(128)S(6)} %copy.35.live_ref, s32[512,128]{1,0:T(8,128)} %third_ref.1, bf16[512,128]{1,0:T(8,128)(2,1)} %value_ref.1, s32[1,512]{1,0:T(1,128)} %bitcast.91), custom_call_target="tpu_custom_call" | custom-call | flops 3000000000 | bytes 1000000 | tf_op jit(solution)/shard_map/pallas_call | solution.py:84
  7.8 7.1 %shard_map.84.refs_0_ = bf16[128,512,256]{2,1,0:T(8,128)(2,1)} custom-call(f32[512,128]{1,0:T(8,128)} %get-tuple-element.26.hi_ref, f32[512,128]{1,0:T(8,128)} %get-tuple-element.27.lo_ref, f32[512,128]{1,0:T(8,128)} %get-tuple-element.28.v_ref), custom_call_target="tpu_custom_call" | custom-call | flops 7500000256 | bytes 8388608 | tf_op jit(solution)/shard_map/pallas_call | solution.py:183
  15.1 3.2 %collective-permute-start.10 = (bf16[1,2,16,2048]{3,2,1,0:T(8,128)(2,1)S(1)}, bf16[1,2,16,2048]{3,2,1,0:T(8,128)(2,1)S(1)}, u32[]{:S(2)}, u32[]{:S(2)}) collective-permute-start(bf16[1,2,16,2048]{3,2,1,0:T(8,128)(2,1)S(1)} %get-tuple-element.66), channel_id=1, source_target_pairs={{0,32},{1,33},{2,34},{3,35},{4,36},{5,37},{6,38},{7,39},{8,12},{9,... | collective-permute-start | bytes 393224 | tf_op jit(solution)/shard_map/ppermute | solution.py:257
  18.9 2.7 %collective-permute-start.9 = (bf16[1,2,16,2048]{3,2,1,0:T(8,128)(2,1)S(1)}, bf16[1,2,16,2048]{3,2,1,0:T(8,128)(2,1)S(1)}, u32[]{:S(2)}, u32[]{:S(2)}) collective-permute-start(bf16[1,2,16,2048]{3,2,1,0:T(8,128)(2,1)S(1)} %get-tuple-element.66), channel_id=1, source_target_pairs={{0,48},{1,49},{2,50},{3,51},{4,52},{5,53},{6,54},{7,55},{8,14},{9,... | collective-permute-start | bytes 393224 | tf_op jit(solution)/shard_map/ppermute | solution.py:257
  21.6 2.9 %collective-permute-done.8 = bf16[1,2,16,2048]{3,2,1,0:T(8,128)(2,1)S(1)} collective-permute-done((bf16[1,2,16,2048]{3,2,1,0:T(8,128)(2,1)S(1)}, bf16[1,2,16,2048]{3,2,1,0:T(8,128)(2,1)S(1)}, u32[]{:S(2)}, u32[]{:S(2)}) %collective-permute-start.8) | collective-permute-done | bytes 131104 | tf_op jit(solution)/shard_map/ppermute | solution.py:257
  24.5 1.7 collective-permute-start.11
  26.2 1.6 collective-permute-start.12
  27.9 2.0 collective-permute-start.13
  29.8 7.1 %shard_map.85.refs_0_ = bf16[128,512,256]{2,1,0:T(8,128)(2,1)} custom-call(f32[512,128]{1,0:T(8,128)} %get-tuple-element.26.hi_ref, f32[512,128]{1,0:T(8,128)} %get-tuple-element.27.lo_ref, f32[512,128]{1,0:T(8,128)} %get-tuple-element.28.v_ref, bf16[128,512,256]{2,1,0:T(8,128)(2,1)} %shard_map.84.refs_0_), custom_call_target="tpu_custom_call", output_to_operand_aliasing={{}: (3, {})} | custom-call | flops 7500000256 | bytes 8388608 | tf_op jit(solution)/shard_map/pallas_call | solution.py:183
  37.0 0.8 copy-done.5
  37.8 4.2 %collective-permute-done.13 = bf16[1,4,2,16,2048]{4,3,2,1,0:T(8,128)(2,1)} collective-permute-done((bf16[1,4,2,16,2048]{4,3,2,1,0:T(8,128)(2,1)S(1)}, bf16[1,4,2,16,2048]{4,3,2,1,0:T(8,128)(2,1)}, u32[]{:S(2)}, u32[]{:S(2)}) %collective-permute-start.13) | collective-permute-done | bytes 524320 | tf_op jit(solution)/shard_map/ppermute | solution.py:257
  42.0 1.5 pad_maximum_fusion.1
  43.5 2.0 collective-permute-start.15
  45.4 2.2 %collective-permute-start.17 = (bf16[4,4,2,16,2048]{4,3,2,1,0:T(8,128)(2,1)S(1)}, bf16[4,4,2,16,2048]{4,3,2,1,0:T(8,128)(2,1)}, u32[]{:S(2)}, u32[]{:S(2)}) collective-permute-start(bf16[4,4,2,16,2048]{4,3,2,1,0:T(8,128)(2,1)S(1)} %pad_maximum_fusion.1), channel_id=1, source_target_pairs={{0,65},{1,0},{2,67},{3,2},{4,69},{5,4},{6,71},{7,6},{8,56},{9,57},... | collective-permute-start | bytes 6291464 | tf_op jit(solution)/shard_map/ppermute | solution.py:257
  47.6 7.1 %shard_map.86.refs_0_ = bf16[128,512,256]{2,1,0:T(8,128)(2,1)} custom-call(f32[512,128]{1,0:T(8,128)} %get-tuple-element.26.hi_ref, f32[512,128]{1,0:T(8,128)} %get-tuple-element.27.lo_ref, f32[512,128]{1,0:T(8,128)} %get-tuple-element.28.v_ref, bf16[128,512,256]{2,1,0:T(8,128)(2,1)} %shard_map.85.refs_0_), custom_call_target="tpu_custom_call", output_to_operand_aliasing={{}: (3, {})} | custom-call | flops 7500000256 | bytes 8388608 | tf_op jit(solution)/shard_map/pallas_call | solution.py:183
  55.1 3.1 %collective-permute-start.2 = (bf16[1,2,16,2048]{3,2,1,0:T(8,128)(2,1)S(1)}, bf16[1,2,16,2048]{3,2,1,0:T(8,128)(2,1)S(1)}, u32[]{:S(2)}, u32[]{:S(2)}) collective-permute-start(bf16[1,2,16,2048]{3,2,1,0:T(8,128)(2,1)S(1)} %get-tuple-element.65), channel_id=1, source_target_pairs={{0,48},{1,49},{2,50},{3,51},{4,52},{5,53},{6,54},{7,55},{8,56},{9,... | collective-permute-start | bytes 393224 | tf_op jit(solution)/shard_map/ppermute | solution.py:257
  58.1 1.4 collective-permute-start.3
  60.1 2.3 %collective-permute-done.1 = bf16[1,2,16,2048]{3,2,1,0:T(8,128)(2,1)S(1)} collective-permute-done((bf16[1,2,16,2048]{3,2,1,0:T(8,128)(2,1)S(1)}, bf16[1,2,16,2048]{3,2,1,0:T(8,128)(2,1)S(1)}, u32[]{:S(2)}, u32[]{:S(2)}) %collective-permute-start.1) | collective-permute-done | bytes 131104 | tf_op jit(solution)/shard_map/ppermute | solution.py:257
  62.4 4.3 %collective-permute-done.3 = bf16[1,2,16,2048]{3,2,1,0:T(8,128)(2,1)S(1)} collective-permute-done((bf16[1,2,16,2048]{3,2,1,0:T(8,128)(2,1)S(1)}, bf16[1,2,16,2048]{3,2,1,0:T(8,128)(2,1)S(1)}, u32[]{:S(2)}, u32[]{:S(2)}) %collective-permute-start.3) | collective-permute-done | bytes 131104 | tf_op jit(solution)/shard_map/ppermute | solution.py:257
  66.8 1.9 collective-permute-start.4
  68.6 6.4 %shard_map.88.rest = bf16[128,512,256]{2,1,0:T(8,128)(2,1)} custom-call(s32[1]{0:T(128)} %get-tuple-element.25.count_ref, s32[1,512]{1,0:T(1,128)} %get-tuple-element.29.list_ref, f32[512,128]{1,0:T(8,128)} %get-tuple-element.26.hi_ref, f32[512,128]{1,0:T(8,128)} %get-tuple-element.27.lo_ref, f32[512,128]{1,0:T(8,128)} %get-tuple-element.28.v_ref), custom_call_target="tpu_custom_call" | custom-call | flops 6000000000 | bytes 6000000 | tf_op jit(solution)/shard_map/pallas_call | solution.py:223
  75.1 3.6 %collective-permute-done.4.remote_ref = bf16[4,2,16,2048]{3,2,1,0:T(8,128)(2,1)S(1)} collective-permute-done((bf16[4,2,16,2048]{3,2,1,0:T(8,128)(2,1)S(1)}, bf16[4,2,16,2048]{3,2,1,0:T(8,128)(2,1)S(1)}, u32[]{:S(2)}, u32[]{:S(2)}) %collective-permute-start.4) | collective-permute-done | bytes 524320 | tf_op jit(solution)/shard_map/ppermute | solution.py:257
  78.6 0.8 copy-done.7
  79.4 3.1 %shard_map.82 = (bf16[512,256]{1,0:T(8,128)(2,1)}, f32[256,256]{1,0:T(8,128)}) custom-call(s32[6]{0:T(128)} %pad_add_fusion.2.table, bf16[4,2,16,2048]{3,2,1,0:T(8,128)(2,1)} %copy-done.4, bf16[4,2,16,2048]{3,2,1,0:T(8,128)(2,1)} %copy-done.7, s32[1,512]{1,0:T(1,128)} %bitcast.92), custom_call_target="tpu_custom_call" | custom-call | flops 2000000000 | bytes 2000000 | tf_op jit(solution)/shard_map/pallas_call | solution.py:325
  82.5 1.4 collective-permute-start.5
  84.6 4.5 %collective-permute-done.5 = f32[256,256]{1,0:T(8,128)S(1)} collective-permute-done((f32[256,256]{1,0:T(8,128)}, f32[256,256]{1,0:T(8,128)S(1)}, u32[]{:S(2)}, u32[]{:S(2)}) %collective-permute-start.5) | collective-permute-done | bytes 262176 | tf_op jit(solution)/shard_map/ppermute | solution.py:278
  89.1 1.0 add.105
  90.0 1.5 collective-permute-start.6
  91.6 2.3 %slice.92 = bf16[2,4,2,16,2048]{4,3,2,1,0:T(8,128)(2,1)} slice(bf16[4,4,2,16,2048]{4,3,2,1,0:T(8,128)(2,1)} %collective-permute-done.15), slice={[0:2], [0:4], [0:2], [0:16], [0:2048]} | slice | bytes 2097152 | tf_op jit(solution)/shard_map/slice | solution.py:298
  93.9 1.4 collective-permute-start.19
  95.3 2.3 %slice.93 = bf16[2,4,2,16,2048]{4,3,2,1,0:T(8,128)(2,1)} slice(bf16[4,4,2,16,2048]{4,3,2,1,0:T(8,128)(2,1)} %collective-permute-done.17), slice={[2:4], [0:4], [0:2], [0:16], [0:2048]} | slice | bytes 2097152 | tf_op jit(solution)/shard_map/slice | solution.py:299
  97.6 1.8 collective-permute-start.21
  100.7 4.5 %collective-permute-start.14 = (bf16[16,2,16,2048]{3,2,1,0:T(8,128)(2,1)S(1)}, bf16[16,2,16,2048]{3,2,1,0:T(8,128)(2,1)}, u32[]{:S(2)}, u32[]{:S(2)}) collective-permute-start(bf16[16,2,16,2048]{3,2,1,0:T(8,128)(2,1)S(1)} %bitcast.80), channel_id=1, source_target_pairs={{0,8},{1,9},{2,10},{3,11},{4,12},{5,13},{6,14},{7,15},{8,0},{9,1},... | collective-permute-start | bytes 6291464 | tf_op jit(solution)/shard_map/ppermute | solution.py:257
  105.8 7.1 %shard_map.87.head_ref = bf16[128,512,256]{2,1,0:T(8,128)(2,1)} custom-call(f32[512,128]{1,0:T(8,128)} %get-tuple-element.26.hi_ref, f32[512,128]{1,0:T(8,128)} %get-tuple-element.27.lo_ref, f32[512,128]{1,0:T(8,128)} %get-tuple-element.28.v_ref, bf16[128,512,256]{2,1,0:T(8,128)(2,1)} %shard_map.86.refs_0_), custom_call_target="tpu_custom_call", output_to_operand_aliasing={{}: (3, {})} | custom-call | flops 7500000256 | bytes 8388608 | tf_op jit(solution)/shard_map/pallas_call | solution.py:183
  112.9 1.7 add.106
  114.6 1.5 collective-permute-start.22
  116.1 17.0 %shard_map.89 = (f32[512,256]{1,0:T(8,128)}, f32[256,256]{1,0:T(8,128)}, f32[512,256]{1,0:T(8,128)}) custom-call(s32[130]{0:T(256)} %pad_add_fusion.table, s32[1]{0:T(128)} %get-tuple-element.25.count_ref, bf16[128,512,256]{2,1,0:T(8,128)(2,1)} %shard_map.87.head_ref, bf16[128,512,256]{2,1,0:T(8,128)(2,1)} %shard_map.88.rest, ...), custom_call_target="tpu_custom_call" | custom-call | flops 15000000512 | bytes 30000000 | tf_op jit(solution)/shard_map/pallas_call | solution.py:480
  133.1 4.5 %collective-permute-start.7 = (f32[256,256]{1,0:T(8,128)S(1)}, f32[256,256]{1,0:T(8,128)S(1)}, u32[]{:S(2)}, u32[]{:S(2)}) collective-permute-start(f32[256,256]{1,0:T(8,128)S(1)} %copy-done.3), channel_id=1, source_target_pairs={{0,4},{1,5},{2,6},{3,7},{4,0},{5,1},{6,2},{7,3},{8,12},{9,13},{10,... | collective-permute-start | bytes 786440 | tf_op jit(solution)/shard_map/ppermute | solution.py:278
  137.6 19.1 %shard_map.90 = (f32[1024,256]{1,0:T(8,128)}, f32[256,256]{1,0:T(8,128)}) custom-call(s32[130]{0:T(256)} %pad_add_fusion.1.table, s32[1]{0:T(128)} %get-tuple-element.25.count_ref, bf16[128,512,256]{2,1,0:T(8,128)(2,1)} %shard_map.87.head_ref, bf16[128,512,256]{2,1,0:T(8,128)(2,1)} %shard_map.88.rest, bf16[16,2,16,2048]{3,2,1,0:T(8,128)(2,1)} %collective-permute-done.14.p0, ...), custom_call_target="tpu_custom_call" | custom-call | flops 15000000512 | bytes 30000000 | tf_op jit(solution)/shard_map/pallas_call | solution.py:480
  156.7 3.8 %all-to-all-start = ((f32[8,128,256]{2,1,0:T(8,128)}), f32[8,128,256]{2,1,0:T(8,128)S(1)}, u32[]{:S(2)}, u32[]{:S(2)}) async-start(f32[8,128,256]{2,1,0:T(8,128)} %bitcast.84), calls=%async_computation | async-start | bytes 2097152 | tf_op jit(solution)/shard_map/all_to_all | solution.py:629
  160.6 9.8 %shard_map.91 = (f32[256,256]{1,0:T(8,128)S(1)}, s32[1]{0:T(128)}) custom-call(f32[256,256]{1,0:T(8,128)S(1)} %multiply_multiply_fusion.gram_ref), custom_call_target="tpu_custom_call" | custom-call | flops 5000000000 | bytes 600000 | tf_op jit(solution)/shard_map/pallas_call | solution.py:544
  171.3 5.2 %all-to-all-done.spread_ref = f32[8,128,256]{2,1,0:T(8,128)S(1)} async-done(((f32[8,128,256]{2,1,0:T(8,128)}), f32[8,128,256]{2,1,0:T(8,128)S(1)}, u32[]{:S(2)}, u32[]{:S(2)}) %all-to-all-start) | async-done | bytes 1048608 | tf_op jit(solution)/shard_map/all_to_all | solution.py:629
  176.5 1.0 copy-done.2
  177.5 2.3 %shard_map.92 = f32[16,16,128]{2,1,0:T(8,128)} custom-call(f32[256,256]{1,0:T(8,128)S(1)} %get-tuple-element.131.inverse_ref, f32[8,128,256]{2,1,0:T(8,128)} %copy-done.2), custom_call_target="tpu_custom_call" | custom-call | flops 500000000 | bytes 1500000 | tf_op jit(solution)/shard_map/pallas_call | solution.py:573
  179.8 14.4 %all_to_all.15 = f32[16,16,128]{2,1,0:T(8,128)S(1)} all-to-all(f32[16,16,128]{2,1,0:T(8,128)} %shard_map.92), channel_id=1, replica_groups=mesh['rows'=16,'cols'=8] {'rows'}, dimensions={0} | all-to-all | bytes 262144 | tf_op jit(solution)/shard_map/all_to_all | solution.py:631
  194.2 8.8 %all_to_all.16 = f32[8,2,16,128]{3,2,1,0:T(8,128)S(1)} all-to-all(f32[8,2,16,128]{3,2,1,0:T(8,128)S(1)} %bitcast.85), channel_id=1, replica_groups=mesh['rows'=16,'cols'=8] {'cols'}, dimensions={0} | all-to-all | bytes 262144 | tf_op jit(solution)/shard_map/all_to_all | solution.py:634
  (63 shorter events, 5.5 us)
Async XLA Ops:
  1.8 13.2 %collective-permute-start = (bf16[2,16,2048]{2,1,0:T(8,128)(2,1)S(1)}, bf16[2,16,2048]{2,1,0:T(8,128)(2,1)S(1)}, u32[]{:S(2)}, u32[]{:S(2)}) collective-permute-start(bf16[2,16,2048]{2,1,0:T(8,128)(2,1)S(1)} %get-tuple-element.70), channel_id=1, source_target_pairs={{0,8},{1,9},{2,10},{3,11},{4,12},{5,13},{6,14},{7,15},{8,0},{9,1},... | collective-permute-start | bytes 393224 | tf_op jit(solution)/shard_map/ppermute | solution.py:257
  15.1 6.6 %collective-permute-start.10 = (bf16[1,2,16,2048]{3,2,1,0:T(8,128)(2,1)S(1)}, bf16[1,2,16,2048]{3,2,1,0:T(8,128)(2,1)S(1)}, u32[]{:S(2)}, u32[]{:S(2)}) collective-permute-start(bf16[1,2,16,2048]{3,2,1,0:T(8,128)(2,1)S(1)} %get-tuple-element.66), channel_id=1, source_target_pairs={{0,32},{1,33},{2,34},{3,35},{4,36},{5,37},{6,38},{7,39},{8,12},{9,... | collective-permute-start | bytes 393224 | tf_op jit(solution)/shard_map/ppermute | solution.py:257
  18.3 6.2 %collective-permute-start.8 = (bf16[1,2,16,2048]{3,2,1,0:T(8,128)(2,1)S(1)}, bf16[1,2,16,2048]{3,2,1,0:T(8,128)(2,1)S(1)}, u32[]{:S(2)}, u32[]{:S(2)}) collective-permute-start(bf16[1,2,16,2048]{3,2,1,0:T(8,128)(2,1)S(1)} %get-tuple-element.66), channel_id=1, source_target_pairs={{0,16},{1,17},{2,18},{3,19},{4,20},{5,21},{6,22},{7,23},{8,10},{9,... | collective-permute-start | bytes 393224 | tf_op jit(solution)/shard_map/ppermute | solution.py:257
  18.9 5.6 %collective-permute-start.9 = (bf16[1,2,16,2048]{3,2,1,0:T(8,128)(2,1)S(1)}, bf16[1,2,16,2048]{3,2,1,0:T(8,128)(2,1)S(1)}, u32[]{:S(2)}, u32[]{:S(2)}) collective-permute-start(bf16[1,2,16,2048]{3,2,1,0:T(8,128)(2,1)S(1)} %get-tuple-element.66), channel_id=1, source_target_pairs={{0,48},{1,49},{2,50},{3,51},{4,52},{5,53},{6,54},{7,55},{8,14},{9,... | collective-permute-start | bytes 393224 | tf_op jit(solution)/shard_map/ppermute | solution.py:257
  24.5 12.4 %collective-permute-start.11 = (bf16[1,4,2,16,2048]{4,3,2,1,0:T(8,128)(2,1)S(1)}, bf16[1,4,2,16,2048]{4,3,2,1,0:T(8,128)(2,1)S(1)}, u32[]{:S(2)}, u32[]{:S(2)}) collective-permute-start(bf16[1,4,2,16,2048]{4,3,2,1,0:T(8,128)(2,1)S(1)} %maximum_bitcast_fusion), channel_id=1, source_target_pairs={{0,2},{1,3},{2,4},{3,5},{4,6},{5,7},{6,0},{7,1},{8,9},{9,72},{10,1... | collective-permute-start | bytes 1572872 | tf_op jit(solution)/shard_map/ppermute | solution.py:257
  26.2 10.8 %collective-permute-start.12 = (bf16[1,4,2,16,2048]{4,3,2,1,0:T(8,128)(2,1)S(1)}, bf16[1,4,2,16,2048]{4,3,2,1,0:T(8,128)(2,1)S(1)}, u32[]{:S(2)}, u32[]{:S(2)}) collective-permute-start(bf16[1,4,2,16,2048]{4,3,2,1,0:T(8,128)(2,1)S(1)} %maximum_bitcast_fusion), channel_id=1, source_target_pairs={{0,6},{1,7},{2,0},{3,1},{4,2},{5,3},{6,4},{7,5},{8,73},{9,8},{10,7... | collective-permute-start | bytes 1572872 | tf_op jit(solution)/shard_map/ppermute | solution.py:257
  27.9 14.1 %collective-permute-start.13 = (bf16[1,4,2,16,2048]{4,3,2,1,0:T(8,128)(2,1)S(1)}, bf16[1,4,2,16,2048]{4,3,2,1,0:T(8,128)(2,1)}, u32[]{:S(2)}, u32[]{:S(2)}) collective-permute-start(bf16[1,4,2,16,2048]{4,3,2,1,0:T(8,128)(2,1)S(1)} %maximum_bitcast_fusion), channel_id=1, source_target_pairs={{0,4},{1,5},{2,6},{3,7},{4,0},{5,1},{6,2},{7,3},{8,72},{9,73},{10,... | collective-permute-start | bytes 1572872 | tf_op jit(solution)/shard_map/ppermute | solution.py:257
  37.0 0.8 copy-start.5
  43.4 57.3 %copy-start = (bf16[4,4,2,16,2048]{4,3,2,1,0:T(8,128)(2,1)}, bf16[4,4,2,16,2048]{4,3,2,1,0:T(8,128)(2,1)S(1)}, u32[]{:S(2)}) copy-start(bf16[4,4,2,16,2048]{4,3,2,1,0:T(8,128)(2,1)S(1)} %pad_maximum_fusion.1) | copy-start | bytes 6291460
  43.5 48.1 %collective-permute-start.15 = (bf16[4,4,2,16,2048]{4,3,2,1,0:T(8,128)(2,1)S(1)}, bf16[4,4,2,16,2048]{4,3,2,1,0:T(8,128)(2,1)}, u32[]{:S(2)}, u32[]{:S(2)}) collective-permute-start(bf16[4,4,2,16,2048]{4,3,2,1,0:T(8,128)(2,1)S(1)} %pad_maximum_fusion.1), channel_id=1, source_target_pairs={{0,1},{1,64},{2,3},{3,66},{4,5},{5,68},{6,7},{7,70},{8,24},{9,25},... | collective-permute-start | bytes 6291464 | tf_op jit(solution)/shard_map/ppermute | solution.py:257
  45.4 49.9 %collective-permute-start.17 = (bf16[4,4,2,16,2048]{4,3,2,1,0:T(8,128)(2,1)S(1)}, bf16[4,4,2,16,2048]{4,3,2,1,0:T(8,128)(2,1)}, u32[]{:S(2)}, u32[]{:S(2)}) collective-permute-start(bf16[4,4,2,16,2048]{4,3,2,1,0:T(8,128)(2,1)S(1)} %pad_maximum_fusion.1), channel_id=1, source_target_pairs={{0,65},{1,0},{2,67},{3,2},{4,69},{5,4},{6,71},{7,6},{8,56},{9,57},... | collective-permute-start | bytes 6291464 | tf_op jit(solution)/shard_map/ppermute | solution.py:257
  54.8 7.7 %collective-permute-start.1 = (bf16[1,2,16,2048]{3,2,1,0:T(8,128)(2,1)S(1)}, bf16[1,2,16,2048]{3,2,1,0:T(8,128)(2,1)S(1)}, u32[]{:S(2)}, u32[]{:S(2)}) collective-permute-start(bf16[1,2,16,2048]{3,2,1,0:T(8,128)(2,1)S(1)} %get-tuple-element.65), channel_id=1, source_target_pairs={{0,16},{1,17},{2,18},{3,19},{4,20},{5,21},{6,22},{7,23},{8,24},{9,... | collective-permute-start | bytes 393224 | tf_op jit(solution)/shard_map/ppermute | solution.py:257
  55.1 7.3 %collective-permute-start.2 = (bf16[1,2,16,2048]{3,2,1,0:T(8,128)(2,1)S(1)}, bf16[1,2,16,2048]{3,2,1,0:T(8,128)(2,1)S(1)}, u32[]{:S(2)}, u32[]{:S(2)}) collective-permute-start(bf16[1,2,16,2048]{3,2,1,0:T(8,128)(2,1)S(1)} %get-tuple-element.65), channel_id=1, source_target_pairs={{0,48},{1,49},{2,50},{3,51},{4,52},{5,53},{6,54},{7,55},{8,56},{9,... | collective-permute-start | bytes 393224 | tf_op jit(solution)/shard_map/ppermute | solution.py:257
  58.1 8.5 %collective-permute-start.3 = (bf16[1,2,16,2048]{3,2,1,0:T(8,128)(2,1)S(1)}, bf16[1,2,16,2048]{3,2,1,0:T(8,128)(2,1)S(1)}, u32[]{:S(2)}, u32[]{:S(2)}) collective-permute-start(bf16[1,2,16,2048]{3,2,1,0:T(8,128)(2,1)S(1)} %get-tuple-element.65), channel_id=1, source_target_pairs={{0,32},{1,33},{2,34},{3,35},{4,36},{5,37},{6,38},{7,39},{8,40},{9,... | collective-permute-start | bytes 393224 | tf_op jit(solution)/shard_map/ppermute | solution.py:257
  66.7 8.3 %copy-start.4 = (bf16[4,2,16,2048]{3,2,1,0:T(8,128)(2,1)}, bf16[4,2,16,2048]{3,2,1,0:T(8,128)(2,1)S(1)}, u32[]{:S(2)}) copy-start(bf16[4,2,16,2048]{3,2,1,0:T(8,128)(2,1)S(1)} %pad_maximum_fusion.2.close_ref) | copy-start | bytes 1572868
  66.8 11.9 %collective-permute-start.4 = (bf16[4,2,16,2048]{3,2,1,0:T(8,128)(2,1)S(1)}, bf16[4,2,16,2048]{3,2,1,0:T(8,128)(2,1)S(1)}, u32[]{:S(2)}, u32[]{:S(2)}) collective-permute-start(bf16[4,2,16,2048]{3,2,1,0:T(8,128)(2,1)S(1)} %pad_maximum_fusion.2.close_ref), channel_id=1, source_target_pairs={{0,64},{1,65},{2,66},{3,67},{4,68},{5,69},{6,70},{7,71},{8,72},{9,... | collective-permute-start | bytes 1572872 | tf_op jit(solution)/shard_map/ppermute | solution.py:257
  78.6 0.8 copy-start.7
  82.5 6.6 %collective-permute-start.5 = (f32[256,256]{1,0:T(8,128)}, f32[256,256]{1,0:T(8,128)S(1)}, u32[]{:S(2)}, u32[]{:S(2)}) collective-permute-start(f32[256,256]{1,0:T(8,128)} %get-tuple-element.24), channel_id=1, source_target_pairs={{0,1},{1,0},{2,3},{3,2},{4,5},{5,4},{6,7},{7,6},{8,9},{9,8},{10,11... | collective-permute-start | bytes 786440 | tf_op jit(solution)/shard_map/ppermute | solution.py:278
  90.0 15.2 %collective-permute-start.6 = (f32[256,256]{1,0:T(8,128)S(1)}, f32[256,256]{1,0:T(8,128)}, u32[]{:S(2)}, u32[]{:S(2)}) collective-permute-start(f32[256,256]{1,0:T(8,128)S(1)} %add.105), channel_id=1, source_target_pairs={{0,2},{1,3},{2,0},{3,1},{4,6},{5,7},{6,4},{7,5},{8,10},{9,11},{10,... | collective-permute-start | bytes 786440 | tf_op jit(solution)/shard_map/ppermute | solution.py:278
  93.9 20.7 %collective-permute-start.19 = (bf16[2,4,2,16,2048]{4,3,2,1,0:T(8,128)(2,1)}, bf16[2,4,2,16,2048]{4,3,2,1,0:T(8,128)(2,1)S(1)}, u32[]{:S(2)}, u32[]{:S(2)}) collective-permute-start(bf16[2,4,2,16,2048]{4,3,2,1,0:T(8,128)(2,1)} %slice.92), channel_id=1, source_target_pairs={{0,1},{1,64},{2,3},{3,66},{4,5},{5,68},{6,7},{7,70},{8,24},{9,25},... | collective-permute-start | bytes 3145736 | tf_op jit(solution)/shard_map/ppermute | solution.py:257
  97.6 17.0 %collective-permute-start.21 = (bf16[2,4,2,16,2048]{4,3,2,1,0:T(8,128)(2,1)}, bf16[2,4,2,16,2048]{4,3,2,1,0:T(8,128)(2,1)}, u32[]{:S(2)}, u32[]{:S(2)}) collective-permute-start(bf16[2,4,2,16,2048]{4,3,2,1,0:T(8,128)(2,1)} %slice.93), channel_id=1, source_target_pairs={{0,65},{1,0},{2,67},{3,2},{4,69},{5,4},{6,71},{7,6},{8,56},{9,57},... | collective-permute-start | bytes 3145736 | tf_op jit(solution)/shard_map/ppermute | solution.py:257
  100.7 32.4 %collective-permute-start.14 = (bf16[16,2,16,2048]{3,2,1,0:T(8,128)(2,1)S(1)}, bf16[16,2,16,2048]{3,2,1,0:T(8,128)(2,1)}, u32[]{:S(2)}, u32[]{:S(2)}) collective-permute-start(bf16[16,2,16,2048]{3,2,1,0:T(8,128)(2,1)S(1)} %bitcast.80), channel_id=1, source_target_pairs={{0,8},{1,9},{2,10},{3,11},{4,12},{5,13},{6,14},{7,15},{8,0},{9,1},... | collective-permute-start | bytes 6291464 | tf_op jit(solution)/shard_map/ppermute | solution.py:257
  105.2 32.3 %collective-permute-start.16 = (bf16[16,2,16,2048]{3,2,1,0:T(8,128)(2,1)}, bf16[16,2,16,2048]{3,2,1,0:T(8,128)(2,1)}, u32[]{:S(2)}, u32[]{:S(2)}) collective-permute-start(bf16[16,2,16,2048]{3,2,1,0:T(8,128)(2,1)} %bitcast.24.p1), channel_id=1, source_target_pairs={{0,8},{1,9},{2,10},{3,11},{4,12},{5,13},{6,14},{7,15},{8,0},{9,1},... | collective-permute-start | bytes 6291464 | tf_op jit(solution)/shard_map/ppermute | solution.py:257
  105.3 32.3 %collective-permute-start.18 = (bf16[16,2,16,2048]{3,2,1,0:T(8,128)(2,1)}, bf16[16,2,16,2048]{3,2,1,0:T(8,128)(2,1)}, u32[]{:S(2)}, u32[]{:S(2)}) collective-permute-start(bf16[16,2,16,2048]{3,2,1,0:T(8,128)(2,1)} %bitcast.25.p2), channel_id=1, source_target_pairs={{0,8},{1,9},{2,10},{3,11},{4,12},{5,13},{6,14},{7,15},{8,0},{9,1},... | collective-permute-start | bytes 6291464 | tf_op jit(solution)/shard_map/ppermute | solution.py:257
  114.5 1.6 copy-start.1
  114.6 23.0 %collective-permute-start.20 = (bf16[8,2,16,2048]{3,2,1,0:T(8,128)(2,1)S(1)}, bf16[8,2,16,2048]{3,2,1,0:T(8,128)(2,1)}, u32[]{:S(2)}, u32[]{:S(2)}) collective-permute-start(bf16[8,2,16,2048]{3,2,1,0:T(8,128)(2,1)S(1)} %bitcast.82), channel_id=1, source_target_pairs={{0,8},{1,9},{2,10},{3,11},{4,12},{5,13},{6,14},{7,15},{8,0},{9,1},... | collective-permute-start | bytes 3145736 | tf_op jit(solution)/shard_map/ppermute | solution.py:257
  114.6 18.5 %copy-start.3 = (f32[256,256]{1,0:T(8,128)S(1)}, f32[256,256]{1,0:T(8,128)}, u32[]{:S(2)}) copy-start(f32[256,256]{1,0:T(8,128)} %add.106) | copy-start | bytes 786436
  114.6 23.0 %collective-permute-start.22 = (bf16[8,2,16,2048]{3,2,1,0:T(8,128)(2,1)}, bf16[8,2,16,2048]{3,2,1,0:T(8,128)(2,1)}, u32[]{:S(2)}, u32[]{:S(2)}) collective-permute-start(bf16[8,2,16,2048]{3,2,1,0:T(8,128)(2,1)} %bitcast.27.p4), channel_id=1, source_target_pairs={{0,8},{1,9},{2,10},{3,11},{4,12},{5,13},{6,14},{7,15},{8,0},{9,1},... | collective-permute-start | bytes 3145736 | tf_op jit(solution)/shard_map/ppermute | solution.py:257
  133.1 27.4 %collective-permute-start.7 = (f32[256,256]{1,0:T(8,128)S(1)}, f32[256,256]{1,0:T(8,128)S(1)}, u32[]{:S(2)}, u32[]{:S(2)}) collective-permute-start(f32[256,256]{1,0:T(8,128)S(1)} %copy-done.3), channel_id=1, source_target_pairs={{0,4},{1,5},{2,6},{3,7},{4,0},{5,1},{6,2},{7,3},{8,12},{9,13},{10,... | collective-permute-start | bytes 786440 | tf_op jit(solution)/shard_map/ppermute | solution.py:278
  156.7 3.8 %copy-start.6 = (f32[256,256]{1,0:T(8,128)S(1)}, f32[256,256]{1,0:T(8,128)}, u32[]{:S(2)}) copy-start(f32[256,256]{1,0:T(8,128)} %get-tuple-element.34) | copy-start | bytes 786436
  156.7 19.8 %all-to-all-start = ((f32[8,128,256]{2,1,0:T(8,128)}), f32[8,128,256]{2,1,0:T(8,128)S(1)}, u32[]{:S(2)}, u32[]{:S(2)}) async-start(f32[8,128,256]{2,1,0:T(8,128)} %bitcast.84), calls=%async_computation | async-start | bytes 2097152 | tf_op jit(solution)/shard_map/all_to_all | solution.py:629
  176.5 1.0 copy-start.2

commit v7 on v6

--- a/solution.py
+++ b/solution.py
@@ -280,16 +280,12 @@
     return value
 
 
-def gather_tables(piece, second, core):
+def gather_table(piece, core):
     half = piece.shape[1] // 2
     mine = lax.dynamic_slice_in_dim(piece, core * half, half, 1)
     other = lax.dynamic_slice_in_dim(piece, (1 - core) * half, half, 1)
-    came = across(jnp.stack([other, second]))
-    here = jnp.stack([mine, second])
-    both = jnp.where(core == 0, jnp.stack([here, came]), jnp.stack([came, here]))
-    unit = both[:, 0]
-    close = ring(both[:, 1][None], ("x", "x"))
-    remote = shifted(close, ("z", "z"), 2)
+    came = across(other)
+    unit = jnp.where(core == 0, jnp.stack([mine, came]), jnp.stack([came, mine]))
     near = ring(unit[None], ("x", "y"))
     plane = ring(near[None], ("y", "z"))
     last = ("z", "x")
@@ -298,7 +294,7 @@
     far0 = shifted(left[:2], last, 1)
     far1 = shifted(right[2:], last, -1)
     own = [x.reshape(-1, *unit.shape) for x in (plane, left, right, far0, far1)]
-    return own, [across(x) for x in own], close, remote
+    return own, [across(x) for x in own]
 
 
 def spot(there, here):
@@ -306,33 +302,26 @@
     return jnp.where(ahead == 3, 1, jnp.where(ahead == 0, 0, ahead + 1))
 
 
-def pick_kernel(table, close_ref, remote_ref, index_ref, picked_ref, gram_ref, rows):
-    half = rows.shape[0] // 2
-    z_hi = table[4]
-    near = jnp.concatenate([close_ref[table[x]].reshape(32, -1) for x in range(4)], 0)
-    far = jnp.concatenate([remote_ref[table[x]].reshape(32, -1) for x in range(4)], 0)
-    rows[pl.ds(pl.multiple_of(z_hi * half, half), half), :] = near
-    rows[pl.ds(pl.multiple_of((1 - z_hi) * half, half), half), :] = far
-    r = rows[...]
+def pick_kernel(first_ref, range_ref, index_ref, picked_ref, gram_ref):
+    r = range_ref[...].reshape(256, range_ref.shape[2])
     gram_ref[...] = dot(r, r, NT)
     at = lax.broadcasted_iota(jnp.int32, (r.shape[1], index_ref.shape[1]), 0)
-    hot = (at == index_ref[...] - table[5]).astype(F32).astype(BF)
+    hot = (at == index_ref[...] - first_ref[0]).astype(F32).astype(BF)
     picked_ref[...] = dot(r, hot, NN).T.astype(BF)
 
 
-def pick(table, close, remote, index):
-    n, rows = index.shape[1], close.shape[-1]
+def pick(first, second_range, index):
+    n = index.shape[1]
     return pl.pallas_call(
         pick_kernel,
         in_specs=[pl.BlockSpec(memory_space=pltpu.SMEM)]
-        + [pl.BlockSpec(memory_space=pltpu.VMEM)] * 3,
+        + [pl.BlockSpec(memory_space=pltpu.VMEM)] * 2,
         out_specs=[pl.BlockSpec(memory_space=pltpu.VMEM)] * 2,
         out_shape=[jax.ShapeDtypeStruct((n, 256), BF), jax.ShapeDtypeStruct((256, 256), F32)],
-        scratch_shapes=[pltpu.VMEM((256, rows), BF)],
         cost_estimate=pl.CostEstimate(
             flops=2_000_000_000, bytes_accessed=2_000_000, transcendentals=0
         ),
-    )(table, close, remote, index)
+    )(first, second_range, index)
 
 
 def piece_table(row_at, col_at, order, slab):
@@ -597,14 +586,12 @@
     slab = range_rows * n_cols // n_rows
 
     core = row_at & 1
-    own, swapped, close, remote = gather_tables(third_factor.T, second_factor.T, core)
-    spots = jnp.concatenate(
-        [
-            spot(jnp.arange(4, dtype=jnp.int32), row_at >> 1),
-            jnp.stack([row_at >> 3, col_at * range_rows]),
-        ]
-    )
-    picked, local_gram = pick(spots, close, remote, block_second[None, :])
+    own, swapped = gather_table(third_factor.T, core)
+    second = jnp.broadcast_to(second_factor.T[None], (n_rows, *second_factor.T.shape))
+    second_range = lax.all_to_all(second, "rows", 0, 0, tiled=True)
+    picked, local_gram = pick(
+        (col_at * range_rows)[None], second_range, block_second[None, :]
+    )
     gram_second = summed_over_cols(local_gram)
 
     hi, lo, v, listed, count = prepare(block_third, block_values, block_length, live_blocks)

time: 206 us -> 197 us (0.956)
  starting transfers between devices: 43.7 us -> 34.8 us
  waiting for transfers between devices: 27 us -> 29.1 us
  blocking collectives: 23.2 us -> 21.1 us
    ppermute x20 -> x16, starting transfers between devices: 32.5 us -> 18.8 us  [shifted(): return lax.ppermute(value, AXES, pairs)]
    all_to_all x0 -> x1, starting transfers between devices: none -> 7.98 us  [per_device(): second_range = lax.all_to_all(second, 'rows', 0, 0, tiled=True)]
    ppermute x3, waiting for transfers between devices: 4.5 us -> 12 us  [summed_over_cols(): other = lax.ppermute(value, AXES, pairs)]
    ppermute x20 -> x16, waiting for transfers between devices: 17.3 us -> 10.8 us  [shifted(): return lax.ppermute(value, AXES, pairs)]
    ppermute x3, starting transfers between devices: 7.4 us -> 4.32 us  [summed_over_cols(): other = lax.ppermute(value, AXES, pairs)]
    all_to_all x1, blocking collectives: 14.4 us -> 12.4 us  [per_device(): moved = lax.all_to_all(solved, 'rows', 0, 0, tiled=True)]
  transfers between devices with their start and end apart: 24 -> 21, of which waited for: 8 -> 7; matrix products, arithmetic and copies ran while one was open for 5% -> 7% of each run, Pallas kernels for 44% -> 46%
where the time goes in v7:
time: 197 us; the launch traced here: 195 us
  Pallas kernels  91.5 us (46%)
  starting transfers between devices  34.8 us (18%)
  waiting for transfers between devices  29.1 us (15%)
  blocking collectives  21.1 us (11%)
  local copies, waits for them, and re-layouts  10.7 us (5%)
  other arithmetic  5.74 us (3%)
    pallas_call x2, Pallas kernels, product(): pl.pallas_call(second_kernel if more else first_kernel, grid_spec=pltpu.P...  36.2 us
    pallas_call x4, Pallas kernels, build(): made = (call(hi, lo, v, *made),)  28.5 us
    ppermute x16, starting transfers between devices, shifted(): return lax.ppermute(value, AXES, pairs)  18.8 us
    all_to_all x1, blocking collectives, per_device(): moved = lax.all_to_all(solved, 'rows', 0, 0, tiled=True)  12.4 us
    ppermute x3, waiting for transfers between devices, summed_over_cols(): other = lax.ppermute(value, AXES, pairs)  12 us
    ppermute x16, waiting for transfers between devices, shifted(): return lax.ppermute(value, AXES, pairs)  10.8 us
    pallas_call x1, Pallas kernels, inverse(): pl.pallas_call(inverse_kernel, out_shape=[jax.ShapeDtypeStruct((n, n), F3...  9.79 us
    all_to_all x1, blocking collectives, per_device(): moved = lax.all_to_all(moved, 'cols', 0, 0, tiled=True)  8.79 us
  transfers between devices with their start and end apart: 21, of which 7 were waited for; matrix products, arithmetic and copies ran while one was open for 7% of the time, Pallas kernels for 46%

profile of v7, /device:TPU:0, one launch (start us, length us, event | category | flops | bytes accessed | tf_op | source)
XLA Modules:
  0.0 194.9 jit_solution(3214924278946873842)
XLA Ops:
  0.0 0.9 dynamic-slice_bitcast_fusion.1
  1.0 2.0 %broadcast_in_dim.68 = bf16[16,16,2048]{2,1,0:T(8,128)(2,1)} broadcast(bf16[16,2048]{1,0:T(8,128)(2,1)} %bitcast.77), dimensions={1,2} | broadcast | bytes 1114112 | tf_op jit(solution)/shard_map/broadcast_in_dim | solution.py:590
  3.0 8.0 %all-to-all-start = ((bf16[16,16,2048]{2,1,0:T(8,128)(2,1)}), bf16[16,16,2048]{2,1,0:T(8,128)(2,1)}, u32[]{:S(2)}, u32[]{:S(2)}) async-start(bf16[16,16,2048]{2,1,0:T(8,128)(2,1)} %broadcast_in_dim.68), calls=%async_computation | async-start | bytes 2097152 | tf_op jit(solution)/shard_map/all_to_all | solution.py:591
  11.6 5.3 %shard_map.83 = (f32[512,128]{1,0:T(8,128)}, f32[512,128]{1,0:T(8,128)}, f32[512,128]{1,0:T(8,128)}, s32[1,512]{1,0:T(1,128)}, s32[1]{0:T(128)}) custom-call(s32[1]{0:T(128)S(6)} %copy.35.live_ref, s32[512,128]{1,0:T(8,128)} %third_ref.1, bf16[512,128]{1,0:T(8,128)(2,1)} %value_ref.1, s32[1,512]{1,0:T(1,128)} %bitcast.80), custom_call_target="tpu_custom_call" | custom-call | flops 3000000000 | bytes 1000000 | tf_op jit(solution)/shard_map/pallas_call | solution.py:84
  16.9 7.1 %shard_map.84.refs_0_ = bf16[128,512,256]{2,1,0:T(8,128)(2,1)} custom-call(f32[512,128]{1,0:T(8,128)} %get-tuple-element.26.hi_ref, f32[512,128]{1,0:T(8,128)} %get-tuple-element.27.lo_ref, f32[512,128]{1,0:T(8,128)} %get-tuple-element.28.v_ref), custom_call_target="tpu_custom_call" | custom-call | flops 7500000256 | bytes 8388608 | tf_op jit(solution)/shard_map/pallas_call | solution.py:183
  24.1 1.9 collective-permute-start.4
  26.0 1.4 collective-permute-start.5
  27.4 2.2 %collective-permute-start.6 = (bf16[1,2,16,2048]{3,2,1,0:T(8,128)(2,1)S(1)}, bf16[1,2,16,2048]{3,2,1,0:T(8,128)(2,1)S(1)}, u32[]{:S(2)}, u32[]{:S(2)}) collective-permute-start(bf16[1,2,16,2048]{3,2,1,0:T(8,128)(2,1)S(1)} %maximum_select_fusion), channel_id=1, source_target_pairs={{0,32},{1,33},{2,34},{3,35},{4,36},{5,37},{6,38},{7,39},{8,12},{9,... | collective-permute-start | bytes 393224 | tf_op jit(solution)/shard_map/ppermute | solution.py:257
  29.6 0.8 collective-permute-done.4
  30.3 0.7 collective-permute-done.5
  31.0 2.9 %collective-permute-done.6 = bf16[1,2,16,2048]{3,2,1,0:T(8,128)(2,1)S(1)} collective-permute-done((bf16[1,2,16,2048]{3,2,1,0:T(8,128)(2,1)S(1)}, bf16[1,2,16,2048]{3,2,1,0:T(8,128)(2,1)S(1)}, u32[]{:S(2)}, u32[]{:S(2)}) %collective-permute-start.6) | collective-permute-done | bytes 131104 | tf_op jit(solution)/shard_map/ppermute | solution.py:257
  33.9 1.6 collective-permute-start.7
  35.6 1.7 collective-permute-start.8
  37.2 2.0 %collective-permute-start.9 = (bf16[1,4,2,16,2048]{4,3,2,1,0:T(8,128)(2,1)S(1)}, bf16[1,4,2,16,2048]{4,3,2,1,0:T(8,128)(2,1)}, u32[]{:S(2)}, u32[]{:S(2)}) collective-permute-start(bf16[1,4,2,16,2048]{4,3,2,1,0:T(8,128)(2,1)S(1)} %maximum_bitcast_fusion), channel_id=1, source_target_pairs={{0,4},{1,5},{2,6},{3,7},{4,0},{5,1},{6,2},{7,3},{8,72},{9,73},{10,... | collective-permute-start | bytes 1572872 | tf_op jit(solution)/shard_map/ppermute | solution.py:257
  39.2 7.1 %shard_map.85.refs_0_ = bf16[128,512,256]{2,1,0:T(8,128)(2,1)} custom-call(f32[512,128]{1,0:T(8,128)} %get-tuple-element.26.hi_ref, f32[512,128]{1,0:T(8,128)} %get-tuple-element.27.lo_ref, f32[512,128]{1,0:T(8,128)} %get-tuple-element.28.v_ref, bf16[128,512,256]{2,1,0:T(8,128)(2,1)} %shard_map.84.refs_0_), custom_call_target="tpu_custom_call", output_to_operand_aliasing={{}: (3, {})} | custom-call | flops 7500000256 | bytes 8388608 | tf_op jit(solution)/shard_map/pallas_call | solution.py:183
  46.4 0.8 copy-done.4
  47.2 4.2 %collective-permute-done.9 = bf16[1,4,2,16,2048]{4,3,2,1,0:T(8,128)(2,1)} collective-permute-done((bf16[1,4,2,16,2048]{4,3,2,1,0:T(8,128)(2,1)S(1)}, bf16[1,4,2,16,2048]{4,3,2,1,0:T(8,128)(2,1)}, u32[]{:S(2)}, u32[]{:S(2)}) %collective-permute-start.9) | collective-permute-done | bytes 524320 | tf_op jit(solution)/shard_map/ppermute | solution.py:257
  51.3 1.5 pad_maximum_fusion.1
  52.8 1.1 collective-permute-start.11
  53.9 2.6 %collective-permute-start.13 = (bf16[4,4,2,16,2048]{4,3,2,1,0:T(8,128)(2,1)S(1)}, bf16[4,4,2,16,2048]{4,3,2,1,0:T(8,128)(2,1)}, u32[]{:S(2)}, u32[]{:S(2)}) collective-permute-start(bf16[4,4,2,16,2048]{4,3,2,1,0:T(8,128)(2,1)S(1)} %pad_maximum_fusion.1), channel_id=1, source_target_pairs={{0,65},{1,0},{2,67},{3,2},{4,69},{5,4},{6,71},{7,6},{8,56},{9,57},... | collective-permute-start | bytes 6291464 | tf_op jit(solution)/shard_map/ppermute | solution.py:257
  56.5 6.4 %shard_map.88.rest = bf16[128,512,256]{2,1,0:T(8,128)(2,1)} custom-call(s32[1]{0:T(128)} %get-tuple-element.25.count_ref, s32[1,512]{1,0:T(1,128)} %get-tuple-element.29.list_ref, f32[512,128]{1,0:T(8,128)} %get-tuple-element.26.hi_ref, f32[512,128]{1,0:T(8,128)} %get-tuple-element.27.lo_ref, f32[512,128]{1,0:T(8,128)} %get-tuple-element.28.v_ref), custom_call_target="tpu_custom_call" | custom-call | flops 6000000000 | bytes 6000000 | tf_op jit(solution)/shard_map/pallas_call | solution.py:223
  63.0 7.1 %shard_map.86.refs_0_ = bf16[128,512,256]{2,1,0:T(8,128)(2,1)} custom-call(f32[512,128]{1,0:T(8,128)} %get-tuple-element.26.hi_ref, f32[512,128]{1,0:T(8,128)} %get-tuple-element.27.lo_ref, f32[512,128]{1,0:T(8,128)} %get-tuple-element.28.v_ref, bf16[128,512,256]{2,1,0:T(8,128)(2,1)} %shard_map.85.refs_0_), custom_call_target="tpu_custom_call", output_to_operand_aliasing={{}: (3, {})} | custom-call | flops 7500000256 | bytes 8388608 | tf_op jit(solution)/shard_map/pallas_call | solution.py:183
  70.1 3.0 %shard_map.82 = (bf16[512,256]{1,0:T(8,128)(2,1)}, f32[256,256]{1,0:T(8,128)}) custom-call(s32[1]{0:T(128)} %bitcast.5.first_ref, bf16[16,16,2048]{2,1,0:T(8,128)(2,1)} %all-to-all-done.range_ref, s32[1,512]{1,0:T(1,128)} %bitcast.81), custom_call_target="tpu_custom_call" | custom-call | flops 2000000000 | bytes 2000000 | tf_op jit(solution)/shard_map/pallas_call | solution.py:315
  73.9 12.0 %collective-permute-done = f32[256,256]{1,0:T(8,128)S(1)} collective-permute-done((f32[256,256]{1,0:T(8,128)}, f32[256,256]{1,0:T(8,128)S(1)}, u32[]{:S(2)}, u32[]{:S(2)}) %collective-permute-start) | collective-permute-done | bytes 262176 | tf_op jit(solution)/shard_map/ppermute | solution.py:278
  85.9 1.0 add.101
  86.8 1.5 collective-permute-start.1
  88.3 2.4 %slice.82 = bf16[2,4,2,16,2048]{4,3,2,1,0:T(8,128)(2,1)} slice(bf16[4,4,2,16,2048]{4,3,2,1,0:T(8,128)(2,1)} %collective-permute-done.11), slice={[0:2], [0:4], [0:2], [0:16], [0:2048]} | slice | bytes 2097152 | tf_op jit(solution)/shard_map/slice | solution.py:294
  90.7 2.3 %slice.83 = bf16[2,4,2,16,2048]{4,3,2,1,0:T(8,128)(2,1)} slice(bf16[4,4,2,16,2048]{4,3,2,1,0:T(8,128)(2,1)} %collective-permute-done.13), slice={[2:4], [0:4], [0:2], [0:16], [0:2048]} | slice | bytes 2097152 | tf_op jit(solution)/shard_map/slice | solution.py:295
  93.0 3.2 %collective-permute-start.17 = (bf16[2,4,2,16,2048]{4,3,2,1,0:T(8,128)(2,1)}, bf16[2,4,2,16,2048]{4,3,2,1,0:T(8,128)(2,1)}, u32[]{:S(2)}, u32[]{:S(2)}) collective-permute-start(bf16[2,4,2,16,2048]{4,3,2,1,0:T(8,128)(2,1)} %slice.83), channel_id=1, source_target_pairs={{0,65},{1,0},{2,67},{3,2},{4,69},{5,4},{6,71},{7,6},{8,56},{9,57},... | collective-permute-start | bytes 3145736 | tf_op jit(solution)/shard_map/ppermute | solution.py:257
  96.3 0.7 pad_add_fusion.table
  96.9 0.6 pad_add_fusion.1.table
  97.6 0.5 collective-permute-start.12
  98.1 7.1 %shard_map.87.head_ref = bf16[128,512,256]{2,1,0:T(8,128)(2,1)} custom-call(f32[512,128]{1,0:T(8,128)} %get-tuple-element.26.hi_ref, f32[512,128]{1,0:T(8,128)} %get-tuple-element.27.lo_ref, f32[512,128]{1,0:T(8,128)} %get-tuple-element.28.v_ref, bf16[128,512,256]{2,1,0:T(8,128)(2,1)} %shard_map.86.refs_0_), custom_call_target="tpu_custom_call", output_to_operand_aliasing={{}: (3, {})} | custom-call | flops 7500000256 | bytes 8388608 | tf_op jit(solution)/shard_map/pallas_call | solution.py:183
  105.2 1.7 add.102
  107.0 0.5 collective-permute-start.16
  107.5 2.3 %collective-permute-done.17 = bf16[2,4,2,16,2048]{4,3,2,1,0:T(8,128)(2,1)} collective-permute-done((bf16[2,4,2,16,2048]{4,3,2,1,0:T(8,128)(2,1)}, bf16[2,4,2,16,2048]{4,3,2,1,0:T(8,128)(2,1)}, u32[]{:S(2)}, u32[]{:S(2)}) %collective-permute-start.17) | collective-permute-done | bytes 1048608 | tf_op jit(solution)/shard_map/ppermute | solution.py:257
  109.8 17.1 %shard_map.89 = (f32[512,256]{1,0:T(8,128)}, f32[256,256]{1,0:T(8,128)}, f32[512,256]{1,0:T(8,128)}) custom-call(s32[130]{0:T(256)} %pad_add_fusion.table, s32[1]{0:T(128)} %get-tuple-element.25.count_ref, bf16[128,512,256]{2,1,0:T(8,128)(2,1)} %shard_map.87.head_ref, bf16[128,512,256]{2,1,0:T(8,128)(2,1)} %shard_map.88.rest, ...), custom_call_target="tpu_custom_call" | custom-call | flops 15000000512 | bytes 30000000 | tf_op jit(solution)/shard_map/pallas_call | solution.py:469
  126.8 2.8 %collective-permute-start.2 = (f32[256,256]{1,0:T(8,128)S(1)}, f32[256,256]{1,0:T(8,128)S(1)}, u32[]{:S(2)}, u32[]{:S(2)}) collective-permute-start(f32[256,256]{1,0:T(8,128)S(1)} %copy-done.3), channel_id=1, source_target_pairs={{0,4},{1,5},{2,6},{3,7},{4,0},{5,1},{6,2},{7,3},{8,12},{9,13},{10,... | collective-permute-start | bytes 786440 | tf_op jit(solution)/shard_map/ppermute | solution.py:278
  129.7 19.2 %shard_map.90 = (f32[1024,256]{1,0:T(8,128)}, f32[256,256]{1,0:T(8,128)}) custom-call(s32[130]{0:T(256)} %pad_add_fusion.1.table, s32[1]{0:T(128)} %get-tuple-element.25.count_ref, bf16[128,512,256]{2,1,0:T(8,128)(2,1)} %shard_map.87.head_ref, bf16[128,512,256]{2,1,0:T(8,128)(2,1)} %shard_map.88.rest, bf16[16,2,16,2048]{3,2,1,0:T(8,128)(2,1)} %collective-permute-done.10.p0, ...), custom_call_target="tpu_custom_call" | custom-call | flops 15000000512 | bytes 30000000 | tf_op jit(solution)/shard_map/pallas_call | solution.py:469
  148.9 3.7 %all-to-all-start.1 = ((f32[8,128,256]{2,1,0:T(8,128)}), f32[8,128,256]{2,1,0:T(8,128)S(1)}, u32[]{:S(2)}, u32[]{:S(2)}) async-start(f32[8,128,256]{2,1,0:T(8,128)} %bitcast.73), calls=%async_computation.1 | async-start | bytes 2097152 | tf_op jit(solution)/shard_map/all_to_all | solution.py:616
  152.7 9.8 %shard_map.91 = (f32[256,256]{1,0:T(8,128)S(1)}, s32[1]{0:T(128)}) custom-call(f32[256,256]{1,0:T(8,128)S(1)} %multiply_multiply_fusion.gram_ref), custom_call_target="tpu_custom_call" | custom-call | flops 5000000000 | bytes 600000 | tf_op jit(solution)/shard_map/pallas_call | solution.py:533
  163.1 0.3 conditional.1
  163.4 6.3 %all-to-all-done.1.spread_ref = f32[8,128,256]{2,1,0:T(8,128)S(1)} async-done(((f32[8,128,256]{2,1,0:T(8,128)}), f32[8,128,256]{2,1,0:T(8,128)S(1)}, u32[]{:S(2)}, u32[]{:S(2)}) %all-to-all-start.1) | async-done | bytes 1048608 | tf_op jit(solution)/shard_map/all_to_all | solution.py:616
  169.7 1.0 copy-done.2
  170.7 2.3 %shard_map.92 = f32[16,16,128]{2,1,0:T(8,128)} custom-call(f32[256,256]{1,0:T(8,128)S(1)} %get-tuple-element.127.inverse_ref, f32[8,128,256]{2,1,0:T(8,128)} %copy-done.2), custom_call_target="tpu_custom_call" | custom-call | flops 500000000 | bytes 1500000 | tf_op jit(solution)/shard_map/pallas_call | solution.py:562
  172.9 12.4 %all_to_all.20 = f32[16,16,128]{2,1,0:T(8,128)S(1)} all-to-all(f32[16,16,128]{2,1,0:T(8,128)} %shard_map.92), channel_id=1, replica_groups=mesh['rows'=16,'cols'=8] {'rows'}, dimensions={0} | all-to-all | bytes 262144 | tf_op jit(solution)/shard_map/all_to_all | solution.py:618
  185.3 8.8 %all_to_all.21 = f32[8,2,16,128]{3,2,1,0:T(8,128)S(1)} all-to-all(f32[8,2,16,128]{3,2,1,0:T(8,128)S(1)} %bitcast.74), channel_id=1, replica_groups=mesh['rows'=16,'cols'=8] {'cols'}, dimensions={0} | all-to-all | bytes 262144 | tf_op jit(solution)/shard_map/all_to_all | solution.py:621
  194.2 0.7 copy.18
  (49 shorter events, 1.1 us)
Async XLA Ops:
  0.9 23.2 %collective-permute-start.3 = (bf16[16,2048]{1,0:T(8,128)(2,1)S(1)}, bf16[16,2048]{1,0:T(8,128)(2,1)S(1)}, u32[]{:S(2)}, u32[]{:S(2)}) collective-permute-start(bf16[16,2048]{1,0:T(8,128)(2,1)S(1)} %get-tuple-element.66), channel_id=1, source_target_pairs={{0,8},{1,9},{2,10},{3,11},{4,12},{5,13},{6,14},{7,15},{8,0},{9,1},... | collective-permute-start | bytes 196616 | tf_op jit(solution)/shard_map/ppermute | solution.py:257
  3.0 67.1 %all-to-all-start = ((bf16[16,16,2048]{2,1,0:T(8,128)(2,1)}), bf16[16,16,2048]{2,1,0:T(8,128)(2,1)}, u32[]{:S(2)}, u32[]{:S(2)}) async-start(bf16[16,16,2048]{2,1,0:T(8,128)(2,1)} %broadcast_in_dim.68), calls=%async_computation | async-start | bytes 2097152 | tf_op jit(solution)/shard_map/all_to_all | solution.py:591
  24.1 6.2 %collective-permute-start.4 = (bf16[1,2,16,2048]{3,2,1,0:T(8,128)(2,1)S(1)}, bf16[1,2,16,2048]{3,2,1,0:T(8,128)(2,1)S(1)}, u32[]{:S(2)}, u32[]{:S(2)}) collective-permute-start(bf16[1,2,16,2048]{3,2,1,0:T(8,128)(2,1)S(1)} %maximum_select_fusion), channel_id=1, source_target_pairs={{0,16},{1,17},{2,18},{3,19},{4,20},{5,21},{6,22},{7,23},{8,10},{9,... | collective-permute-start | bytes 393224 | tf_op jit(solution)/shard_map/ppermute | solution.py:257
  26.0 5.0 %collective-permute-start.5 = (bf16[1,2,16,2048]{3,2,1,0:T(8,128)(2,1)S(1)}, bf16[1,2,16,2048]{3,2,1,0:T(8,128)(2,1)S(1)}, u32[]{:S(2)}, u32[]{:S(2)}) collective-permute-start(bf16[1,2,16,2048]{3,2,1,0:T(8,128)(2,1)S(1)} %maximum_select_fusion), channel_id=1, source_target_pairs={{0,48},{1,49},{2,50},{3,51},{4,52},{5,53},{6,54},{7,55},{8,14},{9,... | collective-permute-start | bytes 393224 | tf_op jit(solution)/shard_map/ppermute | solution.py:257
  27.4 6.5 %collective-permute-start.6 = (bf16[1,2,16,2048]{3,2,1,0:T(8,128)(2,1)S(1)}, bf16[1,2,16,2048]{3,2,1,0:T(8,128)(2,1)S(1)}, u32[]{:S(2)}, u32[]{:S(2)}) collective-permute-start(bf16[1,2,16,2048]{3,2,1,0:T(8,128)(2,1)S(1)} %maximum_select_fusion), channel_id=1, source_target_pairs={{0,32},{1,33},{2,34},{3,35},{4,36},{5,37},{6,38},{7,39},{8,12},{9,... | collective-permute-start | bytes 393224 | tf_op jit(solution)/shard_map/ppermute | solution.py:257
  33.9 12.4 %collective-permute-start.7 = (bf16[1,4,2,16,2048]{4,3,2,1,0:T(8,128)(2,1)S(1)}, bf16[1,4,2,16,2048]{4,3,2,1,0:T(8,128)(2,1)S(1)}, u32[]{:S(2)}, u32[]{:S(2)}) collective-permute-start(bf16[1,4,2,16,2048]{4,3,2,1,0:T(8,128)(2,1)S(1)} %maximum_bitcast_fusion), channel_id=1, source_target_pairs={{0,2},{1,3},{2,4},{3,5},{4,6},{5,7},{6,0},{7,1},{8,9},{9,72},{10,1... | collective-permute-start | bytes 1572872 | tf_op jit(solution)/shard_map/ppermute | solution.py:257
  35.6 10.8 %collective-permute-start.8 = (bf16[1,4,2,16,2048]{4,3,2,1,0:T(8,128)(2,1)S(1)}, bf16[1,4,2,16,2048]{4,3,2,1,0:T(8,128)(2,1)S(1)}, u32[]{:S(2)}, u32[]{:S(2)}) collective-permute-start(bf16[1,4,2,16,2048]{4,3,2,1,0:T(8,128)(2,1)S(1)} %maximum_bitcast_fusion), channel_id=1, source_target_pairs={{0,6},{1,7},{2,0},{3,1},{4,2},{5,3},{6,4},{7,5},{8,73},{9,8},{10,7... | collective-permute-start | bytes 1572872 | tf_op jit(solution)/shard_map/ppermute | solution.py:257
  37.2 14.1 %collective-permute-start.9 = (bf16[1,4,2,16,2048]{4,3,2,1,0:T(8,128)(2,1)S(1)}, bf16[1,4,2,16,2048]{4,3,2,1,0:T(8,128)(2,1)}, u32[]{:S(2)}, u32[]{:S(2)}) collective-permute-start(bf16[1,4,2,16,2048]{4,3,2,1,0:T(8,128)(2,1)S(1)} %maximum_bitcast_fusion), channel_id=1, source_target_pairs={{0,4},{1,5},{2,6},{3,7},{4,0},{5,1},{6,2},{7,3},{8,72},{9,73},{10,... | collective-permute-start | bytes 1572872 | tf_op jit(solution)/shard_map/ppermute | solution.py:257
  46.4 0.8 copy-start.4
  52.8 44.8 %copy-start = (bf16[4,4,2,16,2048]{4,3,2,1,0:T(8,128)(2,1)}, bf16[4,4,2,16,2048]{4,3,2,1,0:T(8,128)(2,1)S(1)}, u32[]{:S(2)}) copy-start(bf16[4,4,2,16,2048]{4,3,2,1,0:T(8,128)(2,1)S(1)} %pad_maximum_fusion.1) | copy-start | bytes 6291460
  52.8 35.5 %collective-permute-start.11 = (bf16[4,4,2,16,2048]{4,3,2,1,0:T(8,128)(2,1)S(1)}, bf16[4,4,2,16,2048]{4,3,2,1,0:T(8,128)(2,1)}, u32[]{:S(2)}, u32[]{:S(2)}) collective-permute-start(bf16[4,4,2,16,2048]{4,3,2,1,0:T(8,128)(2,1)S(1)} %pad_maximum_fusion.1), channel_id=1, source_target_pairs={{0,1},{1,64},{2,3},{3,66},{4,5},{5,68},{6,7},{7,70},{8,24},{9,25},... | collective-permute-start | bytes 6291464 | tf_op jit(solution)/shard_map/ppermute | solution.py:257
  53.9 36.8 %collective-permute-start.13 = (bf16[4,4,2,16,2048]{4,3,2,1,0:T(8,128)(2,1)S(1)}, bf16[4,4,2,16,2048]{4,3,2,1,0:T(8,128)(2,1)}, u32[]{:S(2)}, u32[]{:S(2)}) collective-permute-start(bf16[4,4,2,16,2048]{4,3,2,1,0:T(8,128)(2,1)S(1)} %pad_maximum_fusion.1), channel_id=1, source_target_pairs={{0,65},{1,0},{2,67},{3,2},{4,69},{5,4},{6,71},{7,6},{8,56},{9,57},... | collective-permute-start | bytes 6291464 | tf_op jit(solution)/shard_map/ppermute | solution.py:257
  73.2 12.7 %collective-permute-start = (f32[256,256]{1,0:T(8,128)}, f32[256,256]{1,0:T(8,128)S(1)}, u32[]{:S(2)}, u32[]{:S(2)}) collective-permute-start(f32[256,256]{1,0:T(8,128)} %get-tuple-element.24), channel_id=1, source_target_pairs={{0,1},{1,0},{2,3},{3,2},{4,5},{5,4},{6,7},{7,6},{8,9},{9,8},{10,11... | collective-permute-start | bytes 786440 | tf_op jit(solution)/shard_map/ppermute | solution.py:278
  86.8 11.3 %collective-permute-start.1 = (f32[256,256]{1,0:T(8,128)S(1)}, f32[256,256]{1,0:T(8,128)}, u32[]{:S(2)}, u32[]{:S(2)}) collective-permute-start(f32[256,256]{1,0:T(8,128)S(1)} %add.101), channel_id=1, source_target_pairs={{0,2},{1,3},{2,0},{3,1},{4,6},{5,7},{6,4},{7,5},{8,10},{9,11},{10,... | collective-permute-start | bytes 786440 | tf_op jit(solution)/shard_map/ppermute | solution.py:278
  90.7 16.2 %collective-permute-start.15 = (bf16[2,4,2,16,2048]{4,3,2,1,0:T(8,128)(2,1)}, bf16[2,4,2,16,2048]{4,3,2,1,0:T(8,128)(2,1)S(1)}, u32[]{:S(2)}, u32[]{:S(2)}) collective-permute-start(bf16[2,4,2,16,2048]{4,3,2,1,0:T(8,128)(2,1)} %slice.82), channel_id=1, source_target_pairs={{0,1},{1,64},{2,3},{3,66},{4,5},{5,68},{6,7},{7,70},{8,24},{9,25},... | collective-permute-start | bytes 3145736 | tf_op jit(solution)/shard_map/ppermute | solution.py:257
  93.0 16.7 %collective-permute-start.17 = (bf16[2,4,2,16,2048]{4,3,2,1,0:T(8,128)(2,1)}, bf16[2,4,2,16,2048]{4,3,2,1,0:T(8,128)(2,1)}, u32[]{:S(2)}, u32[]{:S(2)}) collective-permute-start(bf16[2,4,2,16,2048]{4,3,2,1,0:T(8,128)(2,1)} %slice.83), channel_id=1, source_target_pairs={{0,65},{1,0},{2,67},{3,2},{4,69},{5,4},{6,71},{7,6},{8,56},{9,57},... | collective-permute-start | bytes 3145736 | tf_op jit(solution)/shard_map/ppermute | solution.py:257
  97.6 29.2 %collective-permute-start.10 = (bf16[16,2,16,2048]{3,2,1,0:T(8,128)(2,1)S(1)}, bf16[16,2,16,2048]{3,2,1,0:T(8,128)(2,1)}, u32[]{:S(2)}, u32[]{:S(2)}) collective-permute-start(bf16[16,2,16,2048]{3,2,1,0:T(8,128)(2,1)S(1)} %bitcast.69), channel_id=1, source_target_pairs={{0,8},{1,9},{2,10},{3,11},{4,12},{5,13},{6,14},{7,15},{8,0},{9,1},... | collective-permute-start | bytes 6291464 | tf_op jit(solution)/shard_map/ppermute | solution.py:257
  97.6 32.1 %collective-permute-start.12 = (bf16[16,2,16,2048]{3,2,1,0:T(8,128)(2,1)}, bf16[16,2,16,2048]{3,2,1,0:T(8,128)(2,1)}, u32[]{:S(2)}, u32[]{:S(2)}) collective-permute-start(bf16[16,2,16,2048]{3,2,1,0:T(8,128)(2,1)} %bitcast.18.p1), channel_id=1, source_target_pairs={{0,8},{1,9},{2,10},{3,11},{4,12},{5,13},{6,14},{7,15},{8,0},{9,1},... | collective-permute-start | bytes 6291464 | tf_op jit(solution)/shard_map/ppermute | solution.py:257
  98.1 31.6 %collective-permute-start.14 = (bf16[16,2,16,2048]{3,2,1,0:T(8,128)(2,1)}, bf16[16,2,16,2048]{3,2,1,0:T(8,128)(2,1)}, u32[]{:S(2)}, u32[]{:S(2)}) collective-permute-start(bf16[16,2,16,2048]{3,2,1,0:T(8,128)(2,1)} %bitcast.19.p2), channel_id=1, source_target_pairs={{0,8},{1,9},{2,10},{3,11},{4,12},{5,13},{6,14},{7,15},{8,0},{9,1},... | collective-permute-start | bytes 6291464 | tf_op jit(solution)/shard_map/ppermute | solution.py:257
  106.9 2.8 %copy-start.1 = (bf16[2,4,2,16,2048]{4,3,2,1,0:T(8,128)(2,1)}, bf16[2,4,2,16,2048]{4,3,2,1,0:T(8,128)(2,1)S(1)}, u32[]{:S(2)}) copy-start(bf16[2,4,2,16,2048]{4,3,2,1,0:T(8,128)(2,1)S(1)} %collective-permute-done.15) | copy-start | bytes 3145732
  107.0 22.7 %collective-permute-start.16 = (bf16[8,2,16,2048]{3,2,1,0:T(8,128)(2,1)S(1)}, bf16[8,2,16,2048]{3,2,1,0:T(8,128)(2,1)}, u32[]{:S(2)}, u32[]{:S(2)}) collective-permute-start(bf16[8,2,16,2048]{3,2,1,0:T(8,128)(2,1)S(1)} %bitcast.71), channel_id=1, source_target_pairs={{0,8},{1,9},{2,10},{3,11},{4,12},{5,13},{6,14},{7,15},{8,0},{9,1},... | collective-permute-start | bytes 3145736 | tf_op jit(solution)/shard_map/ppermute | solution.py:257
  109.8 17.1 %copy-start.3 = (f32[256,256]{1,0:T(8,128)S(1)}, f32[256,256]{1,0:T(8,128)}, u32[]{:S(2)}) copy-start(f32[256,256]{1,0:T(8,128)} %add.102) | copy-start | bytes 786436
  109.8 19.9 %collective-permute-start.18 = (bf16[8,2,16,2048]{3,2,1,0:T(8,128)(2,1)}, bf16[8,2,16,2048]{3,2,1,0:T(8,128)(2,1)}, u32[]{:S(2)}, u32[]{:S(2)}) collective-permute-start(bf16[8,2,16,2048]{3,2,1,0:T(8,128)(2,1)} %bitcast.21.p4), channel_id=1, source_target_pairs={{0,8},{1,9},{2,10},{3,11},{4,12},{5,13},{6,14},{7,15},{8,0},{9,1},... | collective-permute-start | bytes 3145736 | tf_op jit(solution)/shard_map/ppermute | solution.py:257
  126.8 25.7 %collective-permute-start.2 = (f32[256,256]{1,0:T(8,128)S(1)}, f32[256,256]{1,0:T(8,128)S(1)}, u32[]{:S(2)}, u32[]{:S(2)}) collective-permute-start(f32[256,256]{1,0:T(8,128)S(1)} %copy-done.3), channel_id=1, source_target_pairs={{0,4},{1,5},{2,6},{3,7},{4,0},{5,1},{6,2},{7,3},{8,12},{9,13},{10,... | collective-permute-start | bytes 786440 | tf_op jit(solution)/shard_map/ppermute | solution.py:278
  148.9 3.7 %copy-start.5 = (f32[256,256]{1,0:T(8,128)S(1)}, f32[256,256]{1,0:T(8,128)}, u32[]{:S(2)}) copy-start(f32[256,256]{1,0:T(8,128)} %get-tuple-element.34) | copy-start | bytes 786436
  148.9 20.8 %all-to-all-start.1 = ((f32[8,128,256]{2,1,0:T(8,128)}), f32[8,128,256]{2,1,0:T(8,128)S(1)}, u32[]{:S(2)}, u32[]{:S(2)}) async-start(f32[8,128,256]{2,1,0:T(8,128)} %bitcast.73), calls=%async_computation.1 | async-start | bytes 2097152 | tf_op jit(solution)/shard_map/all_to_all | solution.py:616
  169.7 1.0 copy-start.2

commit v8 on v7

--- a/solution.py
+++ b/solution.py
@@ -20,6 +20,7 @@
 GROUP = 64
 PARTS = 4
 STEP = 8
+CHUNK = 2
 TOLERANCE = 3e-4
 AXES = ("rows", "cols")
 SHIFTS = (1, -1, 2)
@@ -342,26 +343,33 @@
 
 
 def fetch(table, count, rest, pieces, buf, rest_buf, sem, rest_sem, step, slot):
-    n = buf.shape[1]
-    for p in range(n):
-        array = table[step * n + p]
-        index = table[64 + step * n + p]
-        for a, ref in enumerate(pieces):
-
-            @pl.when(array == a)
-            def _(ref=ref, p=p):
-                pltpu.make_async_copy(ref.at[index], buf.at[slot, p], sem.at[slot]).start()
+    n = buf.shape[2]
+    for j in range(CHUNK):
+        at = step * CHUNK + j
+        for p in range(n):
+            array = table[at * n + p]
+            index = table[64 + at * n + p]
+            for a, ref in enumerate(pieces):
+
+                @pl.when(array == a)
+                def _(ref=ref, p=p, j=j):
+                    pltpu.make_async_copy(
+                        ref.at[index], buf.at[slot, j, p], sem.at[slot, j]
+                    ).start()
 
     @pl.when(count > 0)
     def _():
-        rest_copy(table, rest, rest_buf, rest_sem, step, slot, 0).start()
-
-
-def rest_copy(table, rest, rest_buf, rest_sem, step, slot, group):
-    first = pl.multiple_of((2 * step + table[128]) * STEP, STEP)
+        for j in range(CHUNK):
+            rest_copy(table, rest, rest_buf, rest_sem, step, slot, j, 0).start()
+
+
+def rest_copy(table, rest, rest_buf, rest_sem, step, slot, j, group):
+    first = pl.multiple_of((2 * (step * CHUNK + j) + table[128]) * STEP, STEP)
     at = pl.multiple_of(group * GROUP, GROUP)
     return pltpu.make_async_copy(
-        rest.at[pl.ds(first, STEP), pl.ds(at, GROUP), :], rest_buf.at[slot], rest_sem.at[slot]
+        rest.at[pl.ds(first, STEP), pl.ds(at, GROUP), :],
+        rest_buf.at[slot, j],
+        rest_sem.at[slot, j],
     )
 
 
@@ -371,6 +379,7 @@
     step = pl.program_id(0)
     slot = lax.rem(step, 2)
     count = count_ref[0]
+    parts = [(j, i) for j in range(CHUNK) for i in range(STEP)]
 
     @pl.when(step == 0)
     def _():
@@ -385,28 +394,36 @@
     def _():
         fetch(table, count, rest, pieces, *bufs, step + 1, 1 - slot)
 
-    pltpu.make_async_copy(pieces[0].at[pl.ds(0, buf.shape[1])], buf.at[slot], sem.at[slot]).wait()
+    for j in range(CHUNK):
+        pltpu.make_async_copy(
+            pieces[0].at[pl.ds(0, buf.shape[2])], buf.at[slot, j], sem.at[slot, j]
+        ).wait()
 
     @pl.when(count > 0)
     def _():
-        rest_copy(table, rest, rest_buf, rest_sem, step, slot, 0).wait()
-
-    def listed(at):
-        return jnp.concatenate([rest_buf[at, i] for i in range(STEP)], 1)
-
-    t = buf[slot].reshape(256, STEP * LO)
-    head = jnp.concatenate([head_ref[i] for i in range(STEP)], 1)
+        for j in range(CHUNK):
+            rest_copy(table, rest, rest_buf, rest_sem, step, slot, j, 0).wait()
+
+    def tile():
+        return jnp.concatenate([buf[slot, j].reshape(256, STEP * LO) for j in range(CHUNK)], 1)
+
+    def listed():
+        return jnp.concatenate([rest_buf[slot, j, i] for j, i in parts], 1)
+
+    t = tile()
+    head = jnp.concatenate([head_ref[j, 0, i] for j, i in parts], 1)
     fold_ref[...] += dot(head, t, NT)
-    both = dot(jnp.concatenate([t, listed(slot)], 0), t, NT)
+    both = dot(jnp.concatenate([t, listed()], 0), t, NT)
     gram_ref[...] += both[:256]
     extra_ref[:GROUP] += both[256:]
 
     def more(group, carry):
-        copy = rest_copy(table, rest, rest_buf, rest_sem, step, slot, group)
-        copy.start()
-        copy.wait()
+        for j in range(CHUNK):
+            copy = rest_copy(table, rest, rest_buf, rest_sem, step, slot, j, group)
+            copy.start()
+            copy.wait()
         at = pl.multiple_of(group * GROUP, GROUP)
-        extra_ref[pl.ds(at, GROUP), :] += dot(listed(slot), buf[slot].reshape(256, STEP * LO), NT)
+        extra_ref[pl.ds(at, GROUP), :] += dot(listed(), tile(), NT)
         return carry
 
     lax.fori_loop(1, groups_of(count), more, 0)
@@ -453,16 +470,17 @@
 
 def product(table, count, head, rest, pieces, more, slab):
     n = head.shape[1]
-    steps = HI // STEP // 2
+    by_range = head.reshape(HI // STEP // 2, 2, STEP, n, LO)
+    ranges = HI // STEP // 2
     any_spec = pl.BlockSpec(memory_space=pl.ANY)
     whole = lambda x: pl.BlockSpec(x.shape, lambda i, *scalars: (0, 0))
     sums = [jax.ShapeDtypeStruct((rows, 256), F32) for rows in (n, 256, n)]
     out = [jax.ShapeDtypeStruct((slab, 256), F32), sums[1]] if more else sums
     scratch = [
-        pltpu.VMEM((2, 8, *pieces[0].shape[1:]), BF),
-        pltpu.VMEM((2, STEP, GROUP, LO), BF),
-        pltpu.SemaphoreType.DMA((2,)),
-        pltpu.SemaphoreType.DMA((2,)),
+        pltpu.VMEM((2, CHUNK, 8, *pieces[0].shape[1:]), BF),
+        pltpu.VMEM((2, CHUNK, STEP, GROUP, LO), BF),
+        pltpu.SemaphoreType.DMA((2, CHUNK)),
+        pltpu.SemaphoreType.DMA((2, CHUNK)),
     ]
     if more:
         scratch = [pltpu.VMEM((n, 256), F32)] * 2 + scratch
@@ -470,9 +488,11 @@
         second_kernel if more else first_kernel,
         grid_spec=pltpu.PrefetchScalarGridSpec(
             num_scalar_prefetch=2,
-            grid=(steps,),
+            grid=(ranges // CHUNK,),
             in_specs=[
-                pl.BlockSpec((STEP, n, LO), lambda i, table, count: (2 * i + table[128], 0, 0))
+                pl.BlockSpec(
+                    (CHUNK, 1, STEP, n, LO), lambda i, table, count: (i, table[128], 0, 0, 0)
+                )
             ]
             + [any_spec] * 6
             + [whole(x) for x in more],
@@ -483,7 +503,7 @@
         cost_estimate=pl.CostEstimate(
             flops=15_000_000_000, bytes_accessed=30_000_000, transcendentals=0
         ),
-    )(table, count, head, rest, *pieces, *more)
+    )(table, count, by_range, rest, *pieces, *more)
 
 
 def exact(a, b, dims):

time: 197 us -> 195 us (0.990)
  Pallas kernels: 91.5 us -> 89.4 us
    pallas_call x2, Pallas kernels: 36.2 us -> 34.1 us  [product(): pl.pallas_call(second_kernel if more else first_kernel, grid_spec=pltpu.P...]
  transfers between devices with their start and end apart: 21 -> 21, of which waited for: 7 -> 7; matrix products, arithmetic and copies ran while one was open for 7% -> 7% of each run, Pallas kernels for 46% -> 45%
where the time goes in v8:
time: 195 us; the launch traced here: 193 us
  Pallas kernels  89.4 us (46%)
  starting transfers between devices  34.8 us (18%)
  waiting for transfers between devices  29.2 us (15%)
  blocking collectives  21.2 us (11%)
  local copies, waits for them, and re-layouts  10.7 us (5%)
  other arithmetic  5.74 us (3%)
    pallas_call x2, Pallas kernels, product(): pl.pallas_call(second_kernel if more else first_kernel, grid_spec=pltpu.P...  34.1 us
    pallas_call x4, Pallas kernels, build(): made = (call(hi, lo, v, *made),)  28.5 us
    ppermute x16, starting transfers between devices, shifted(): return lax.ppermute(value, AXES, pairs)  18.8 us
    all_to_all x1, blocking collectives, per_device(): moved = lax.all_to_all(solved, 'rows', 0, 0, tiled=True)  12.4 us
    ppermute x3, waiting for transfers between devices, summed_over_cols(): other = lax.ppermute(value, AXES, pairs)  12 us
    ppermute x16, waiting for transfers between devices, shifted(): return lax.ppermute(value, AXES, pairs)  10.8 us
    pallas_call x1, Pallas kernels, inverse(): pl.pallas_call(inverse_kernel, out_shape=[jax.ShapeDtypeStruct((n, n), F3...  9.79 us
    all_to_all x1, blocking collectives, per_device(): moved = lax.all_to_all(moved, 'cols', 0, 0, tiled=True)  8.79 us
  transfers between devices with their start and end apart: 21, of which 7 were waited for; matrix products, arithmetic and copies ran while one was open for 7% of the time, Pallas kernels for 45%

profile of v8, /device:TPU:0, one launch (start us, length us, event | category | flops | bytes accessed | tf_op | source)
XLA Modules:
  0.0 192.8 jit_solution(11372457287037762088)
XLA Ops:
  0.0 0.9 dynamic-slice_bitcast_fusion.1
  1.0 2.0 %broadcast_in_dim.68 = bf16[16,16,2048]{2,1,0:T(8,128)(2,1)} broadcast(bf16[16,2048]{1,0:T(8,128)(2,1)} %bitcast.80), dimensions={1,2} | broadcast | bytes 1114112 | tf_op jit(solution)/shard_map/broadcast_in_dim | solution.py:610
  3.0 8.0 %all-to-all-start = ((bf16[16,16,2048]{2,1,0:T(8,128)(2,1)}), bf16[16,16,2048]{2,1,0:T(8,128)(2,1)}, u32[]{:S(2)}, u32[]{:S(2)}) async-start(bf16[16,16,2048]{2,1,0:T(8,128)(2,1)} %broadcast_in_dim.68), calls=%async_computation | async-start | bytes 2097152 | tf_op jit(solution)/shard_map/all_to_all | solution.py:611
  11.6 5.3 %shard_map.83 = (f32[512,128]{1,0:T(8,128)}, f32[512,128]{1,0:T(8,128)}, f32[512,128]{1,0:T(8,128)}, s32[1,512]{1,0:T(1,128)}, s32[1]{0:T(128)}) custom-call(s32[1]{0:T(128)S(6)} %copy.35.live_ref, s32[512,128]{1,0:T(8,128)} %third_ref.1, bf16[512,128]{1,0:T(8,128)(2,1)} %value_ref.1, s32[1,512]{1,0:T(1,128)} %bitcast.83), custom_call_target="tpu_custom_call" | custom-call | flops 3000000000 | bytes 1000000 | tf_op jit(solution)/shard_map/pallas_call | solution.py:85
  16.9 7.1 %shard_map.84.refs_0_ = bf16[128,512,256]{2,1,0:T(8,128)(2,1)} custom-call(f32[512,128]{1,0:T(8,128)} %get-tuple-element.26.hi_ref, f32[512,128]{1,0:T(8,128)} %get-tuple-element.27.lo_ref, f32[512,128]{1,0:T(8,128)} %get-tuple-element.28.v_ref), custom_call_target="tpu_custom_call" | custom-call | flops 7500000256 | bytes 8388608 | tf_op jit(solution)/shard_map/pallas_call | solution.py:184
  24.1 1.9 %collective-permute-start.4 = (bf16[1,2,16,2048]{3,2,1,0:T(8,128)(2,1)S(1)}, bf16[1,2,16,2048]{3,2,1,0:T(8,128)(2,1)S(1)}, u32[]{:S(2)}, u32[]{:S(2)}) collective-permute-start(bf16[1,2,16,2048]{3,2,1,0:T(8,128)(2,1)S(1)} %maximum_select_fusion), channel_id=1, source_target_pairs={{0,16},{1,17},{2,18},{3,19},{4,20},{5,21},{6,22},{7,23},{8,10},{9,... | collective-permute-start | bytes 393224 | tf_op jit(solution)/shard_map/ppermute | solution.py:258
  26.0 1.4 collective-permute-start.5
  27.4 2.2 %collective-permute-start.6 = (bf16[1,2,16,2048]{3,2,1,0:T(8,128)(2,1)S(1)}, bf16[1,2,16,2048]{3,2,1,0:T(8,128)(2,1)S(1)}, u32[]{:S(2)}, u32[]{:S(2)}) collective-permute-start(bf16[1,2,16,2048]{3,2,1,0:T(8,128)(2,1)S(1)} %maximum_select_fusion), channel_id=1, source_target_pairs={{0,32},{1,33},{2,34},{3,35},{4,36},{5,37},{6,38},{7,39},{8,12},{9,... | collective-permute-start | bytes 393224 | tf_op jit(solution)/shard_map/ppermute | solution.py:258
  29.6 0.8 collective-permute-done.4
  30.3 0.7 collective-permute-done.5
  31.0 2.9 %collective-permute-done.6 = bf16[1,2,16,2048]{3,2,1,0:T(8,128)(2,1)S(1)} collective-permute-done((bf16[1,2,16,2048]{3,2,1,0:T(8,128)(2,1)S(1)}, bf16[1,2,16,2048]{3,2,1,0:T(8,128)(2,1)S(1)}, u32[]{:S(2)}, u32[]{:S(2)}) %collective-permute-start.6) | collective-permute-done | bytes 131104 | tf_op jit(solution)/shard_map/ppermute | solution.py:258
  33.9 1.6 collective-permute-start.7
  35.6 1.7 collective-permute-start.8
  37.2 2.0 %collective-permute-start.9 = (bf16[1,4,2,16,2048]{4,3,2,1,0:T(8,128)(2,1)S(1)}, bf16[1,4,2,16,2048]{4,3,2,1,0:T(8,128)(2,1)}, u32[]{:S(2)}, u32[]{:S(2)}) collective-permute-start(bf16[1,4,2,16,2048]{4,3,2,1,0:T(8,128)(2,1)S(1)} %maximum_bitcast_fusion), channel_id=1, source_target_pairs={{0,4},{1,5},{2,6},{3,7},{4,0},{5,1},{6,2},{7,3},{8,72},{9,73},{10,... | collective-permute-start | bytes 1572872 | tf_op jit(solution)/shard_map/ppermute | solution.py:258
  39.2 7.1 %shard_map.85.refs_0_ = bf16[128,512,256]{2,1,0:T(8,128)(2,1)} custom-call(f32[512,128]{1,0:T(8,128)} %get-tuple-element.26.hi_ref, f32[512,128]{1,0:T(8,128)} %get-tuple-element.27.lo_ref, f32[512,128]{1,0:T(8,128)} %get-tuple-element.28.v_ref, bf16[128,512,256]{2,1,0:T(8,128)(2,1)} %shard_map.84.refs_0_), custom_call_target="tpu_custom_call", output_to_operand_aliasing={{}: (3, {})} | custom-call | flops 7500000256 | bytes 8388608 | tf_op jit(solution)/shard_map/pallas_call | solution.py:184
  46.4 0.8 copy-done.4
  47.2 4.2 %collective-permute-done.9 = bf16[1,4,2,16,2048]{4,3,2,1,0:T(8,128)(2,1)} collective-permute-done((bf16[1,4,2,16,2048]{4,3,2,1,0:T(8,128)(2,1)S(1)}, bf16[1,4,2,16,2048]{4,3,2,1,0:T(8,128)(2,1)}, u32[]{:S(2)}, u32[]{:S(2)}) %collective-permute-start.9) | collective-permute-done | bytes 524320 | tf_op jit(solution)/shard_map/ppermute | solution.py:258
  51.3 1.5 pad_maximum_fusion.1
  52.8 1.1 collective-permute-start.11
  53.9 2.6 %collective-permute-start.13 = (bf16[4,4,2,16,2048]{4,3,2,1,0:T(8,128)(2,1)S(1)}, bf16[4,4,2,16,2048]{4,3,2,1,0:T(8,128)(2,1)}, u32[]{:S(2)}, u32[]{:S(2)}) collective-permute-start(bf16[4,4,2,16,2048]{4,3,2,1,0:T(8,128)(2,1)S(1)} %pad_maximum_fusion.1), channel_id=1, source_target_pairs={{0,65},{1,0},{2,67},{3,2},{4,69},{5,4},{6,71},{7,6},{8,56},{9,57},... | collective-permute-start | bytes 6291464 | tf_op jit(solution)/shard_map/ppermute | solution.py:258
  56.5 6.4 %shard_map.88.rest = bf16[128,512,256]{2,1,0:T(8,128)(2,1)} custom-call(s32[1]{0:T(128)} %get-tuple-element.25.count_ref, s32[1,512]{1,0:T(1,128)} %get-tuple-element.29.list_ref, f32[512,128]{1,0:T(8,128)} %get-tuple-element.26.hi_ref, f32[512,128]{1,0:T(8,128)} %get-tuple-element.27.lo_ref, f32[512,128]{1,0:T(8,128)} %get-tuple-element.28.v_ref), custom_call_target="tpu_custom_call" | custom-call | flops 6000000000 | bytes 6000000 | tf_op jit(solution)/shard_map/pallas_call | solution.py:224
  63.0 7.1 %shard_map.86.refs_0_ = bf16[128,512,256]{2,1,0:T(8,128)(2,1)} custom-call(f32[512,128]{1,0:T(8,128)} %get-tuple-element.26.hi_ref, f32[512,128]{1,0:T(8,128)} %get-tuple-element.27.lo_ref, f32[512,128]{1,0:T(8,128)} %get-tuple-element.28.v_ref, bf16[128,512,256]{2,1,0:T(8,128)(2,1)} %shard_map.85.refs_0_), custom_call_target="tpu_custom_call", output_to_operand_aliasing={{}: (3, {})} | custom-call | flops 7500000256 | bytes 8388608 | tf_op jit(solution)/shard_map/pallas_call | solution.py:184
  70.1 3.0 %shard_map.82 = (bf16[512,256]{1,0:T(8,128)(2,1)}, f32[256,256]{1,0:T(8,128)}) custom-call(s32[1]{0:T(128)} %bitcast.5.first_ref, bf16[16,16,2048]{2,1,0:T(8,128)(2,1)} %all-to-all-done.range_ref, s32[1,512]{1,0:T(1,128)} %bitcast.84), custom_call_target="tpu_custom_call" | custom-call | flops 2000000000 | bytes 2000000 | tf_op jit(solution)/shard_map/pallas_call | solution.py:316
  73.9 12.0 %collective-permute-done = f32[256,256]{1,0:T(8,128)S(1)} collective-permute-done((f32[256,256]{1,0:T(8,128)}, f32[256,256]{1,0:T(8,128)S(1)}, u32[]{:S(2)}, u32[]{:S(2)}) %collective-permute-start) | collective-permute-done | bytes 262176 | tf_op jit(solution)/shard_map/ppermute | solution.py:279
  85.9 1.0 add.101
  86.8 1.5 collective-permute-start.1
  88.3 2.4 %slice.82 = bf16[2,4,2,16,2048]{4,3,2,1,0:T(8,128)(2,1)} slice(bf16[4,4,2,16,2048]{4,3,2,1,0:T(8,128)(2,1)} %collective-permute-done.11), slice={[0:2], [0:4], [0:2], [0:16], [0:2048]} | slice | bytes 2097152 | tf_op jit(solution)/shard_map/slice | solution.py:295
  90.7 2.3 %slice.83 = bf16[2,4,2,16,2048]{4,3,2,1,0:T(8,128)(2,1)} slice(bf16[4,4,2,16,2048]{4,3,2,1,0:T(8,128)(2,1)} %collective-permute-done.13), slice={[2:4], [0:4], [0:2], [0:16], [0:2048]} | slice | bytes 2097152 | tf_op jit(solution)/shard_map/slice | solution.py:296
  93.0 3.2 %collective-permute-start.17 = (bf16[2,4,2,16,2048]{4,3,2,1,0:T(8,128)(2,1)}, bf16[2,4,2,16,2048]{4,3,2,1,0:T(8,128)(2,1)}, u32[]{:S(2)}, u32[]{:S(2)}) collective-permute-start(bf16[2,4,2,16,2048]{4,3,2,1,0:T(8,128)(2,1)} %slice.83), channel_id=1, source_target_pairs={{0,65},{1,0},{2,67},{3,2},{4,69},{5,4},{6,71},{7,6},{8,56},{9,57},... | collective-permute-start | bytes 3145736 | tf_op jit(solution)/shard_map/ppermute | solution.py:258
  96.3 0.7 pad_add_fusion.table
  96.9 0.6 pad_add_fusion.1.table
  97.6 0.5 collective-permute-start.12
  98.1 7.1 %shard_map.87 = bf16[128,512,256]{2,1,0:T(8,128)(2,1)} custom-call(f32[512,128]{1,0:T(8,128)} %get-tuple-element.26.hi_ref, f32[512,128]{1,0:T(8,128)} %get-tuple-element.27.lo_ref, f32[512,128]{1,0:T(8,128)} %get-tuple-element.28.v_ref, bf16[128,512,256]{2,1,0:T(8,128)(2,1)} %shard_map.86.refs_0_), custom_call_target="tpu_custom_call", output_to_operand_aliasing={{}: (3, {})} | custom-call | flops 7500000256 | bytes 8388608 | tf_op jit(solution)/shard_map/pallas_call | solution.py:184
  105.2 1.7 add.102
  107.0 0.5 collective-permute-start.16
  107.5 2.3 %collective-permute-done.17 = bf16[2,4,2,16,2048]{4,3,2,1,0:T(8,128)(2,1)} collective-permute-done((bf16[2,4,2,16,2048]{4,3,2,1,0:T(8,128)(2,1)}, bf16[2,4,2,16,2048]{4,3,2,1,0:T(8,128)(2,1)}, u32[]{:S(2)}, u32[]{:S(2)}) %collective-permute-start.17) | collective-permute-done | bytes 1048608 | tf_op jit(solution)/shard_map/ppermute | solution.py:258
  109.8 16.0 %shard_map.89 = (f32[512,256]{1,0:T(8,128)}, f32[256,256]{1,0:T(8,128)}, f32[512,256]{1,0:T(8,128)}) custom-call(s32[130]{0:T(256)} %pad_add_fusion.table, s32[1]{0:T(128)} %get-tuple-element.25.count_ref, bf16[8,2,8,512,256]{4,3,2,1,0:T(8,128)(2,1)} %bitcast.70, bf16[128,512,256]{2,1,0:T(8,128)(2,1)} %shard_map.88.rest, bf16[16,2,16,2048]{3,2,1,0:T(8,128)(2,1)} %bitcast.73, ...), custom_call_target="tpu_custom_call" | custom-call | flops 15000000512 | bytes 30000000 | tf_op jit(solution)/shard_map/pallas_call | solution.py:487
  125.8 2.8 %collective-permute-start.2 = (f32[256,256]{1,0:T(8,128)S(1)}, f32[256,256]{1,0:T(8,128)S(1)}, u32[]{:S(2)}, u32[]{:S(2)}) collective-permute-start(f32[256,256]{1,0:T(8,128)S(1)} %copy-done.3), channel_id=1, source_target_pairs={{0,4},{1,5},{2,6},{3,7},{4,0},{5,1},{6,2},{7,3},{8,12},{9,13},{10,... | collective-permute-start | bytes 786440 | tf_op jit(solution)/shard_map/ppermute | solution.py:279
  128.6 18.1 %shard_map.90 = (f32[1024,256]{1,0:T(8,128)}, f32[256,256]{1,0:T(8,128)}) custom-call(s32[130]{0:T(256)} %pad_add_fusion.1.table, s32[1]{0:T(128)} %get-tuple-element.25.count_ref, bf16[8,2,8,512,256]{4,3,2,1,0:T(8,128)(2,1)} %bitcast.71, bf16[128,512,256]{2,1,0:T(8,128)(2,1)} %shard_map.88.rest, bf16[16,2,16,2048]{3,2,1,0:T(8,128)(2,1)} %collective-permute-done.10.p0, ...), custom_call_target="tpu_custom_call" | custom-call | flops 15000000512 | bytes 30000000 | tf_op jit(solution)/shard_map/pallas_call | solution.py:487
  146.7 3.7 %all-to-all-start.1 = ((f32[8,128,256]{2,1,0:T(8,128)}), f32[8,128,256]{2,1,0:T(8,128)S(1)}, u32[]{:S(2)}, u32[]{:S(2)}) async-start(f32[8,128,256]{2,1,0:T(8,128)} %bitcast.76), calls=%async_computation.1 | async-start | bytes 2097152 | tf_op jit(solution)/shard_map/all_to_all | solution.py:636
  150.5 9.8 %shard_map.91 = (f32[256,256]{1,0:T(8,128)S(1)}, s32[1]{0:T(128)}) custom-call(f32[256,256]{1,0:T(8,128)S(1)} %multiply_multiply_fusion.gram_ref), custom_call_target="tpu_custom_call" | custom-call | flops 5000000000 | bytes 600000 | tf_op jit(solution)/shard_map/pallas_call | solution.py:553
  161.0 0.3 conditional.1
  161.3 6.4 %all-to-all-done.1.spread_ref = f32[8,128,256]{2,1,0:T(8,128)S(1)} async-done(((f32[8,128,256]{2,1,0:T(8,128)}), f32[8,128,256]{2,1,0:T(8,128)S(1)}, u32[]{:S(2)}, u32[]{:S(2)}) %all-to-all-start.1) | async-done | bytes 1048608 | tf_op jit(solution)/shard_map/all_to_all | solution.py:636
  167.7 1.0 copy-done.2
  168.6 2.3 %shard_map.92 = f32[16,16,128]{2,1,0:T(8,128)} custom-call(f32[256,256]{1,0:T(8,128)S(1)} %get-tuple-element.127.inverse_ref, f32[8,128,256]{2,1,0:T(8,128)} %copy-done.2), custom_call_target="tpu_custom_call" | custom-call | flops 500000000 | bytes 1500000 | tf_op jit(solution)/shard_map/pallas_call | solution.py:582
  170.9 12.4 %all_to_all.20 = f32[16,16,128]{2,1,0:T(8,128)S(1)} all-to-all(f32[16,16,128]{2,1,0:T(8,128)} %shard_map.92), channel_id=1, replica_groups=mesh['rows'=16,'cols'=8] {'rows'}, dimensions={0} | all-to-all | bytes 262144 | tf_op jit(solution)/shard_map/all_to_all | solution.py:638
  183.3 8.8 %all_to_all.21 = f32[8,2,16,128]{3,2,1,0:T(8,128)S(1)} all-to-all(f32[8,2,16,128]{3,2,1,0:T(8,128)S(1)} %bitcast.77), channel_id=1, replica_groups=mesh['rows'=16,'cols'=8] {'cols'}, dimensions={0} | all-to-all | bytes 262144 | tf_op jit(solution)/shard_map/all_to_all | solution.py:641
  192.1 0.7 copy.18
  (49 shorter events, 1.1 us)
Async XLA Ops:
  0.9 23.2 %collective-permute-start.3 = (bf16[16,2048]{1,0:T(8,128)(2,1)S(1)}, bf16[16,2048]{1,0:T(8,128)(2,1)S(1)}, u32[]{:S(2)}, u32[]{:S(2)}) collective-permute-start(bf16[16,2048]{1,0:T(8,128)(2,1)S(1)} %get-tuple-element.66), channel_id=1, source_target_pairs={{0,8},{1,9},{2,10},{3,11},{4,12},{5,13},{6,14},{7,15},{8,0},{9,1},... | collective-permute-start | bytes 196616 | tf_op jit(solution)/shard_map/ppermute | solution.py:258
  3.0 67.1 %all-to-all-start = ((bf16[16,16,2048]{2,1,0:T(8,128)(2,1)}), bf16[16,16,2048]{2,1,0:T(8,128)(2,1)}, u32[]{:S(2)}, u32[]{:S(2)}) async-start(bf16[16,16,2048]{2,1,0:T(8,128)(2,1)} %broadcast_in_dim.68), calls=%async_computation | async-start | bytes 2097152 | tf_op jit(solution)/shard_map/all_to_all | solution.py:611
  24.1 6.2 %collective-permute-start.4 = (bf16[1,2,16,2048]{3,2,1,0:T(8,128)(2,1)S(1)}, bf16[1,2,16,2048]{3,2,1,0:T(8,128)(2,1)S(1)}, u32[]{:S(2)}, u32[]{:S(2)}) collective-permute-start(bf16[1,2,16,2048]{3,2,1,0:T(8,128)(2,1)S(1)} %maximum_select_fusion), channel_id=1, source_target_pairs={{0,16},{1,17},{2,18},{3,19},{4,20},{5,21},{6,22},{7,23},{8,10},{9,... | collective-permute-start | bytes 393224 | tf_op jit(solution)/shard_map/ppermute | solution.py:258
  26.0 5.0 %collective-permute-start.5 = (bf16[1,2,16,2048]{3,2,1,0:T(8,128)(2,1)S(1)}, bf16[1,2,16,2048]{3,2,1,0:T(8,128)(2,1)S(1)}, u32[]{:S(2)}, u32[]{:S(2)}) collective-permute-start(bf16[1,2,16,2048]{3,2,1,0:T(8,128)(2,1)S(1)} %maximum_select_fusion), channel_id=1, source_target_pairs={{0,48},{1,49},{2,50},{3,51},{4,52},{5,53},{6,54},{7,55},{8,14},{9,... | collective-permute-start | bytes 393224 | tf_op jit(solution)/shard_map/ppermute | solution.py:258
  27.4 6.5 %collective-permute-start.6 = (bf16[1,2,16,2048]{3,2,1,0:T(8,128)(2,1)S(1)}, bf16[1,2,16,2048]{3,2,1,0:T(8,128)(2,1)S(1)}, u32[]{:S(2)}, u32[]{:S(2)}) collective-permute-start(bf16[1,2,16,2048]{3,2,1,0:T(8,128)(2,1)S(1)} %maximum_select_fusion), channel_id=1, source_target_pairs={{0,32},{1,33},{2,34},{3,35},{4,36},{5,37},{6,38},{7,39},{8,12},{9,... | collective-permute-start | bytes 393224 | tf_op jit(solution)/shard_map/ppermute | solution.py:258
  33.9 12.4 %collective-permute-start.7 = (bf16[1,4,2,16,2048]{4,3,2,1,0:T(8,128)(2,1)S(1)}, bf16[1,4,2,16,2048]{4,3,2,1,0:T(8,128)(2,1)S(1)}, u32[]{:S(2)}, u32[]{:S(2)}) collective-permute-start(bf16[1,4,2,16,2048]{4,3,2,1,0:T(8,128)(2,1)S(1)} %maximum_bitcast_fusion), channel_id=1, source_target_pairs={{0,2},{1,3},{2,4},{3,5},{4,6},{5,7},{6,0},{7,1},{8,9},{9,72},{10,1... | collective-permute-start | bytes 1572872 | tf_op jit(solution)/shard_map/ppermute | solution.py:258
  35.6 10.8 %collective-permute-start.8 = (bf16[1,4,2,16,2048]{4,3,2,1,0:T(8,128)(2,1)S(1)}, bf16[1,4,2,16,2048]{4,3,2,1,0:T(8,128)(2,1)S(1)}, u32[]{:S(2)}, u32[]{:S(2)}) collective-permute-start(bf16[1,4,2,16,2048]{4,3,2,1,0:T(8,128)(2,1)S(1)} %maximum_bitcast_fusion), channel_id=1, source_target_pairs={{0,6},{1,7},{2,0},{3,1},{4,2},{5,3},{6,4},{7,5},{8,73},{9,8},{10,7... | collective-permute-start | bytes 1572872 | tf_op jit(solution)/shard_map/ppermute | solution.py:258
  37.2 14.1 %collective-permute-start.9 = (bf16[1,4,2,16,2048]{4,3,2,1,0:T(8,128)(2,1)S(1)}, bf16[1,4,2,16,2048]{4,3,2,1,0:T(8,128)(2,1)}, u32[]{:S(2)}, u32[]{:S(2)}) collective-permute-start(bf16[1,4,2,16,2048]{4,3,2,1,0:T(8,128)(2,1)S(1)} %maximum_bitcast_fusion), channel_id=1, source_target_pairs={{0,4},{1,5},{2,6},{3,7},{4,0},{5,1},{6,2},{7,3},{8,72},{9,73},{10,... | collective-permute-start | bytes 1572872 | tf_op jit(solution)/shard_map/ppermute | solution.py:258
  46.4 0.8 copy-start.4
  52.8 44.8 %copy-start = (bf16[4,4,2,16,2048]{4,3,2,1,0:T(8,128)(2,1)}, bf16[4,4,2,16,2048]{4,3,2,1,0:T(8,128)(2,1)S(1)}, u32[]{:S(2)}) copy-start(bf16[4,4,2,16,2048]{4,3,2,1,0:T(8,128)(2,1)S(1)} %pad_maximum_fusion.1) | copy-start | bytes 6291460
  52.8 35.5 %collective-permute-start.11 = (bf16[4,4,2,16,2048]{4,3,2,1,0:T(8,128)(2,1)S(1)}, bf16[4,4,2,16,2048]{4,3,2,1,0:T(8,128)(2,1)}, u32[]{:S(2)}, u32[]{:S(2)}) collective-permute-start(bf16[4,4,2,16,2048]{4,3,2,1,0:T(8,128)(2,1)S(1)} %pad_maximum_fusion.1), channel_id=1, source_target_pairs={{0,1},{1,64},{2,3},{3,66},{4,5},{5,68},{6,7},{7,70},{8,24},{9,25},... | collective-permute-start | bytes 6291464 | tf_op jit(solution)/shard_map/ppermute | solution.py:258
  53.9 36.8 %collective-permute-start.13 = (bf16[4,4,2,16,2048]{4,3,2,1,0:T(8,128)(2,1)S(1)}, bf16[4,4,2,16,2048]{4,3,2,1,0:T(8,128)(2,1)}, u32[]{:S(2)}, u32[]{:S(2)}) collective-permute-start(bf16[4,4,2,16,2048]{4,3,2,1,0:T(8,128)(2,1)S(1)} %pad_maximum_fusion.1), channel_id=1, source_target_pairs={{0,65},{1,0},{2,67},{3,2},{4,69},{5,4},{6,71},{7,6},{8,56},{9,57},... | collective-permute-start | bytes 6291464 | tf_op jit(solution)/shard_map/ppermute | solution.py:258
  73.2 12.7 %collective-permute-start = (f32[256,256]{1,0:T(8,128)}, f32[256,256]{1,0:T(8,128)S(1)}, u32[]{:S(2)}, u32[]{:S(2)}) collective-permute-start(f32[256,256]{1,0:T(8,128)} %get-tuple-element.24), channel_id=1, source_target_pairs={{0,1},{1,0},{2,3},{3,2},{4,5},{5,4},{6,7},{7,6},{8,9},{9,8},{10,11... | collective-permute-start | bytes 786440 | tf_op jit(solution)/shard_map/ppermute | solution.py:279
  86.8 11.3 %collective-permute-start.1 = (f32[256,256]{1,0:T(8,128)S(1)}, f32[256,256]{1,0:T(8,128)}, u32[]{:S(2)}, u32[]{:S(2)}) collective-permute-start(f32[256,256]{1,0:T(8,128)S(1)} %add.101), channel_id=1, source_target_pairs={{0,2},{1,3},{2,0},{3,1},{4,6},{5,7},{6,4},{7,5},{8,10},{9,11},{10,... | collective-permute-start | bytes 786440 | tf_op jit(solution)/shard_map/ppermute | solution.py:279
  90.7 16.2 %collective-permute-start.15 = (bf16[2,4,2,16,2048]{4,3,2,1,0:T(8,128)(2,1)}, bf16[2,4,2,16,2048]{4,3,2,1,0:T(8,128)(2,1)S(1)}, u32[]{:S(2)}, u32[]{:S(2)}) collective-permute-start(bf16[2,4,2,16,2048]{4,3,2,1,0:T(8,128)(2,1)} %slice.82), channel_id=1, source_target_pairs={{0,1},{1,64},{2,3},{3,66},{4,5},{5,68},{6,7},{7,70},{8,24},{9,25},... | collective-permute-start | bytes 3145736 | tf_op jit(solution)/shard_map/ppermute | solution.py:258
  93.0 16.7 %collective-permute-start.17 = (bf16[2,4,2,16,2048]{4,3,2,1,0:T(8,128)(2,1)}, bf16[2,4,2,16,2048]{4,3,2,1,0:T(8,128)(2,1)}, u32[]{:S(2)}, u32[]{:S(2)}) collective-permute-start(bf16[2,4,2,16,2048]{4,3,2,1,0:T(8,128)(2,1)} %slice.83), channel_id=1, source_target_pairs={{0,65},{1,0},{2,67},{3,2},{4,69},{5,4},{6,71},{7,6},{8,56},{9,57},... | collective-permute-start | bytes 3145736 | tf_op jit(solution)/shard_map/ppermute | solution.py:258
  97.6 28.1 %collective-permute-start.10 = (bf16[16,2,16,2048]{3,2,1,0:T(8,128)(2,1)S(1)}, bf16[16,2,16,2048]{3,2,1,0:T(8,128)(2,1)}, u32[]{:S(2)}, u32[]{:S(2)}) collective-permute-start(bf16[16,2,16,2048]{3,2,1,0:T(8,128)(2,1)S(1)} %bitcast.72), channel_id=1, source_target_pairs={{0,8},{1,9},{2,10},{3,11},{4,12},{5,13},{6,14},{7,15},{8,0},{9,1},... | collective-permute-start | bytes 6291464 | tf_op jit(solution)/shard_map/ppermute | solution.py:258
  97.6 31.0 %collective-permute-start.12 = (bf16[16,2,16,2048]{3,2,1,0:T(8,128)(2,1)}, bf16[16,2,16,2048]{3,2,1,0:T(8,128)(2,1)}, u32[]{:S(2)}, u32[]{:S(2)}) collective-permute-start(bf16[16,2,16,2048]{3,2,1,0:T(8,128)(2,1)} %bitcast.19.p1), channel_id=1, source_target_pairs={{0,8},{1,9},{2,10},{3,11},{4,12},{5,13},{6,14},{7,15},{8,0},{9,1},... | collective-permute-start | bytes 6291464 | tf_op jit(solution)/shard_map/ppermute | solution.py:258
  98.1 30.5 %collective-permute-start.14 = (bf16[16,2,16,2048]{3,2,1,0:T(8,128)(2,1)}, bf16[16,2,16,2048]{3,2,1,0:T(8,128)(2,1)}, u32[]{:S(2)}, u32[]{:S(2)}) collective-permute-start(bf16[16,2,16,2048]{3,2,1,0:T(8,128)(2,1)} %bitcast.20.p2), channel_id=1, source_target_pairs={{0,8},{1,9},{2,10},{3,11},{4,12},{5,13},{6,14},{7,15},{8,0},{9,1},... | collective-permute-start | bytes 6291464 | tf_op jit(solution)/shard_map/ppermute | solution.py:258
  106.9 2.8 %copy-start.1 = (bf16[2,4,2,16,2048]{4,3,2,1,0:T(8,128)(2,1)}, bf16[2,4,2,16,2048]{4,3,2,1,0:T(8,128)(2,1)S(1)}, u32[]{:S(2)}) copy-start(bf16[2,4,2,16,2048]{4,3,2,1,0:T(8,128)(2,1)S(1)} %collective-permute-done.15) | copy-start | bytes 3145732
  107.0 21.6 %collective-permute-start.16 = (bf16[8,2,16,2048]{3,2,1,0:T(8,128)(2,1)S(1)}, bf16[8,2,16,2048]{3,2,1,0:T(8,128)(2,1)}, u32[]{:S(2)}, u32[]{:S(2)}) collective-permute-start(bf16[8,2,16,2048]{3,2,1,0:T(8,128)(2,1)S(1)} %bitcast.74), channel_id=1, source_target_pairs={{0,8},{1,9},{2,10},{3,11},{4,12},{5,13},{6,14},{7,15},{8,0},{9,1},... | collective-permute-start | bytes 3145736 | tf_op jit(solution)/shard_map/ppermute | solution.py:258
  109.8 18.8 %collective-permute-start.18 = (bf16[8,2,16,2048]{3,2,1,0:T(8,128)(2,1)}, bf16[8,2,16,2048]{3,2,1,0:T(8,128)(2,1)}, u32[]{:S(2)}, u32[]{:S(2)}) collective-permute-start(bf16[8,2,16,2048]{3,2,1,0:T(8,128)(2,1)} %bitcast.22.p4), channel_id=1, source_target_pairs={{0,8},{1,9},{2,10},{3,11},{4,12},{5,13},{6,14},{7,15},{8,0},{9,1},... | collective-permute-start | bytes 3145736 | tf_op jit(solution)/shard_map/ppermute | solution.py:258
  109.8 16.0 %copy-start.3 = (f32[256,256]{1,0:T(8,128)S(1)}, f32[256,256]{1,0:T(8,128)}, u32[]{:S(2)}) copy-start(f32[256,256]{1,0:T(8,128)} %add.102) | copy-start | bytes 786436
  125.8 24.7 %collective-permute-start.2 = (f32[256,256]{1,0:T(8,128)S(1)}, f32[256,256]{1,0:T(8,128)S(1)}, u32[]{:S(2)}, u32[]{:S(2)}) collective-permute-start(f32[256,256]{1,0:T(8,128)S(1)} %copy-done.3), channel_id=1, source_target_pairs={{0,4},{1,5},{2,6},{3,7},{4,0},{5,1},{6,2},{7,3},{8,12},{9,13},{10,... | collective-permute-start | bytes 786440 | tf_op jit(solution)/shard_map/ppermute | solution.py:279
  146.7 3.7 %copy-start.5 = (f32[256,256]{1,0:T(8,128)S(1)}, f32[256,256]{1,0:T(8,128)}, u32[]{:S(2)}) copy-start(f32[256,256]{1,0:T(8,128)} %get-tuple-element.34) | copy-start | bytes 786436
  146.7 20.9 %all-to-all-start.1 = ((f32[8,128,256]{2,1,0:T(8,128)}), f32[8,128,256]{2,1,0:T(8,128)S(1)}, u32[]{:S(2)}, u32[]{:S(2)}) async-start(f32[8,128,256]{2,1,0:T(8,128)} %bitcast.76), calls=%async_computation.1 | async-start | bytes 2097152 | tf_op jit(solution)/shard_map/all_to_all | solution.py:636
  167.6 1.0 copy-start.2

commit v9 on v8

--- a/solution.py
+++ b/solution.py
@@ -18,7 +18,7 @@
 NB = 16
 PITCH = 140
 GROUP = 64
-PARTS = 4
+PARTS = (8, 16, 8)
 STEP = 8
 CHUNK = 2
 TOLERANCE = 3e-4
@@ -161,10 +161,10 @@
 
 def build(hi, lo, v):
     n = hi.shape[0]
-    steps = n // NB // PARTS
+    assert n == NB * sum(PARTS)
     made = ()
-    for part in range(PARTS):
-        first = part * steps
+    first = 0
+    for steps in PARTS:
         spec = pl.BlockSpec((NB, 128), lambda i, first=first: (first + i, 0))
         call = pl.pallas_call(
             functools.partial(build_kernel, first),
@@ -176,12 +176,13 @@
             + [pltpu.VMEM((2, HI, NB, LO), BF), pltpu.SemaphoreType.DMA((2,))],
             input_output_aliases={3: 0} if made else {},
             cost_estimate=pl.CostEstimate(
-                flops=30_000_000_000 // PARTS,
-                bytes_accessed=n * HI * LO * 2 // PARTS,
+                flops=940_000_000 * steps,
+                bytes_accessed=steps * NB * HI * LO * 2,
                 transcendentals=0,
             ),
         )
         made = (call(hi, lo, v, *made),)
+        first += steps
     return made[0]
 
 

time: 195 us -> 190 us (0.974)
  waiting for transfers between devices: 29.2 us -> 26.3 us
    ppermute x3, waiting for transfers between devices: 12 us -> 6.28 us  [summed_over_cols(): other = lax.ppermute(value, AXES, pairs)]
    ppermute x16, waiting for transfers between devices: 10.8 us -> 13.6 us  [shifted(): return lax.ppermute(value, AXES, pairs)]
    pallas_call x4 -> x3, Pallas kernels: 28.5 us -> 27.1 us  [build(): made = (call(hi, lo, v, *made),)]
  transfers between devices with their start and end apart: 21 -> 21, of which waited for: 7 -> 6; matrix products, arithmetic and copies ran while one was open for 7% -> 7% of each run, Pallas kernels for 45% -> 46%
where the time goes in v9:
time: 190 us; the launch traced here: 188 us
  Pallas kernels  88 us (46%)
  starting transfers between devices  34.4 us (18%)
  waiting for transfers between devices  26.3 us (14%)
  blocking collectives  20.5 us (11%)
  local copies, waits for them, and re-layouts  10.7 us (6%)
  other arithmetic  5.74 us (3%)
    pallas_call x2, Pallas kernels, product(): pl.pallas_call(second_kernel if more else first_kernel, grid_spec=pltpu.P...  34.1 us
    pallas_call x3, Pallas kernels, build(): made = (call(hi, lo, v, *made),)  27.1 us
    ppermute x16, starting transfers between devices, shifted(): return lax.ppermute(value, AXES, pairs)  18.4 us
    ppermute x16, waiting for transfers between devices, shifted(): return lax.ppermute(value, AXES, pairs)  13.6 us
    all_to_all x1, blocking collectives, per_device(): moved = lax.all_to_all(solved, 'rows', 0, 0, tiled=True)  11.8 us
    pallas_call x1, Pallas kernels, inverse(): pl.pallas_call(inverse_kernel, out_shape=[jax.ShapeDtypeStruct((n, n), F3...  9.79 us
    all_to_all x1, blocking collectives, per_device(): moved = lax.all_to_all(moved, 'cols', 0, 0, tiled=True)  8.79 us
    all_to_all x1, starting transfers between devices, per_device(): second_range = lax.all_to_all(second, 'rows', 0, 0, tiled=True)  7.98 us
  transfers between devices with their start and end apart: 21, of which 6 were waited for; matrix products, arithmetic and copies ran while one was open for 7% of the time, Pallas kernels for 46%

profile of v9, /device:TPU:0, one launch (start us, length us, event | category | flops | bytes accessed | tf_op | source)
XLA Modules:
  0.0 187.5 jit_solution(12086919409629507147)
XLA Ops:
  0.0 0.9 dynamic-slice_bitcast_fusion.1
  1.0 2.0 %broadcast_in_dim.68 = bf16[16,16,2048]{2,1,0:T(8,128)(2,1)} broadcast(bf16[16,2048]{1,0:T(8,128)(2,1)} %bitcast.80), dimensions={1,2} | broadcast | bytes 1114112 | tf_op jit(solution)/shard_map/broadcast_in_dim | solution.py:611
  3.0 8.0 %all-to-all-start = ((bf16[16,16,2048]{2,1,0:T(8,128)(2,1)}), bf16[16,16,2048]{2,1,0:T(8,128)(2,1)}, u32[]{:S(2)}, u32[]{:S(2)}) async-start(bf16[16,16,2048]{2,1,0:T(8,128)(2,1)} %broadcast_in_dim.68), calls=%async_computation | async-start | bytes 2097152 | tf_op jit(solution)/shard_map/all_to_all | solution.py:612
  11.6 1.9 %collective-permute-start.4 = (bf16[1,2,16,2048]{3,2,1,0:T(8,128)(2,1)S(1)}, bf16[1,2,16,2048]{3,2,1,0:T(8,128)(2,1)S(1)}, u32[]{:S(2)}, u32[]{:S(2)}) collective-permute-start(bf16[1,2,16,2048]{3,2,1,0:T(8,128)(2,1)S(1)} %maximum_select_fusion), channel_id=1, source_target_pairs={{0,16},{1,17},{2,18},{3,19},{4,20},{5,21},{6,22},{7,23},{8,10},{9,... | collective-permute-start | bytes 393224 | tf_op jit(solution)/shard_map/ppermute | solution.py:259
  13.6 1.4 collective-permute-start.5
  15.0 2.2 %collective-permute-start.6 = (bf16[1,2,16,2048]{3,2,1,0:T(8,128)(2,1)S(1)}, bf16[1,2,16,2048]{3,2,1,0:T(8,128)(2,1)S(1)}, u32[]{:S(2)}, u32[]{:S(2)}) collective-permute-start(bf16[1,2,16,2048]{3,2,1,0:T(8,128)(2,1)S(1)} %maximum_select_fusion), channel_id=1, source_target_pairs={{0,32},{1,33},{2,34},{3,35},{4,36},{5,37},{6,38},{7,39},{8,12},{9,... | collective-permute-start | bytes 393224 | tf_op jit(solution)/shard_map/ppermute | solution.py:259
  17.1 5.3 %shard_map.83 = (f32[512,128]{1,0:T(8,128)}, f32[512,128]{1,0:T(8,128)}, f32[512,128]{1,0:T(8,128)}, s32[1,512]{1,0:T(1,128)}, s32[1]{0:T(128)}) custom-call(s32[1]{0:T(128)S(6)} %copy.33.live_ref, s32[512,128]{1,0:T(8,128)} %third_ref.1, bf16[512,128]{1,0:T(8,128)(2,1)} %value_ref.1, s32[1,512]{1,0:T(1,128)} %bitcast.83), custom_call_target="tpu_custom_call" | custom-call | flops 3000000000 | bytes 1000000 | tf_op jit(solution)/shard_map/pallas_call | solution.py:85
  22.4 5.4 %collective-permute-done.4 = bf16[1,2,16,2048]{3,2,1,0:T(8,128)(2,1)S(1)} collective-permute-done((bf16[1,2,16,2048]{3,2,1,0:T(8,128)(2,1)S(1)}, bf16[1,2,16,2048]{3,2,1,0:T(8,128)(2,1)S(1)}, u32[]{:S(2)}, u32[]{:S(2)}) %collective-permute-start.4) | collective-permute-done | bytes 131104 | tf_op jit(solution)/shard_map/ppermute | solution.py:259
  27.9 1.7 collective-permute-done.6
  29.6 1.6 collective-permute-start.7
  31.3 1.7 collective-permute-start.8
  32.9 2.0 %collective-permute-start.9 = (bf16[1,4,2,16,2048]{4,3,2,1,0:T(8,128)(2,1)S(1)}, bf16[1,4,2,16,2048]{4,3,2,1,0:T(8,128)(2,1)}, u32[]{:S(2)}, u32[]{:S(2)}) collective-permute-start(bf16[1,4,2,16,2048]{4,3,2,1,0:T(8,128)(2,1)S(1)} %maximum_bitcast_fusion), channel_id=1, source_target_pairs={{0,4},{1,5},{2,6},{3,7},{4,0},{5,1},{6,2},{7,3},{8,72},{9,73},{10,... | collective-permute-start | bytes 1572872 | tf_op jit(solution)/shard_map/ppermute | solution.py:259
  34.9 7.1 %shard_map.84.refs_0_ = bf16[128,512,256]{2,1,0:T(8,128)(2,1)} custom-call(f32[512,128]{1,0:T(8,128)} %get-tuple-element.26.hi_ref, f32[512,128]{1,0:T(8,128)} %get-tuple-element.27.lo_ref, f32[512,128]{1,0:T(8,128)} %get-tuple-element.28.v_ref), custom_call_target="tpu_custom_call" | custom-call | flops 7520000000 | bytes 8388608 | tf_op jit(solution)/shard_map/pallas_call | solution.py:184
  42.0 0.8 copy-done.4
  42.8 4.2 %collective-permute-done.9 = bf16[1,4,2,16,2048]{4,3,2,1,0:T(8,128)(2,1)} collective-permute-done((bf16[1,4,2,16,2048]{4,3,2,1,0:T(8,128)(2,1)S(1)}, bf16[1,4,2,16,2048]{4,3,2,1,0:T(8,128)(2,1)}, u32[]{:S(2)}, u32[]{:S(2)}) %collective-permute-start.9) | collective-permute-done | bytes 524320 | tf_op jit(solution)/shard_map/ppermute | solution.py:259
  47.0 1.5 pad_maximum_fusion.1
  48.5 1.1 collective-permute-start.11
  49.6 2.2 %collective-permute-start.13 = (bf16[4,4,2,16,2048]{4,3,2,1,0:T(8,128)(2,1)S(1)}, bf16[4,4,2,16,2048]{4,3,2,1,0:T(8,128)(2,1)}, u32[]{:S(2)}, u32[]{:S(2)}) collective-permute-start(bf16[4,4,2,16,2048]{4,3,2,1,0:T(8,128)(2,1)S(1)} %pad_maximum_fusion.1), channel_id=1, source_target_pairs={{0,65},{1,0},{2,67},{3,2},{4,69},{5,4},{6,71},{7,6},{8,56},{9,57},... | collective-permute-start | bytes 6291464 | tf_op jit(solution)/shard_map/ppermute | solution.py:259
  51.8 12.9 %shard_map.85.refs_0_ = bf16[128,512,256]{2,1,0:T(8,128)(2,1)} custom-call(f32[512,128]{1,0:T(8,128)} %get-tuple-element.26.hi_ref, f32[512,128]{1,0:T(8,128)} %get-tuple-element.27.lo_ref, f32[512,128]{1,0:T(8,128)} %get-tuple-element.28.v_ref, bf16[128,512,256]{2,1,0:T(8,128)(2,1)} %shard_map.84.refs_0_), custom_call_target="tpu_custom_call", output_to_operand_aliasing={{}: (3, {})} | custom-call | flops 15040000000 | bytes 16777216 | tf_op jit(solution)/shard_map/pallas_call | solution.py:184
  64.8 6.5 %shard_map.87.rest = bf16[128,512,256]{2,1,0:T(8,128)(2,1)} custom-call(s32[1]{0:T(128)} %get-tuple-element.25.count_ref, s32[1,512]{1,0:T(1,128)} %get-tuple-element.29.list_ref, f32[512,128]{1,0:T(8,128)} %get-tuple-element.26.hi_ref, f32[512,128]{1,0:T(8,128)} %get-tuple-element.27.lo_ref, f32[512,128]{1,0:T(8,128)} %get-tuple-element.28.v_ref), custom_call_target="tpu_custom_call" | custom-call | flops 6000000000 | bytes 6000000 | tf_op jit(solution)/shard_map/pallas_call | solution.py:225
  71.3 3.0 %shard_map.82 = (bf16[512,256]{1,0:T(8,128)(2,1)}, f32[256,256]{1,0:T(8,128)}) custom-call(s32[1]{0:T(128)} %bitcast.5.first_ref, bf16[16,16,2048]{2,1,0:T(8,128)(2,1)} %all-to-all-done.range_ref, s32[1,512]{1,0:T(1,128)} %bitcast.84), custom_call_target="tpu_custom_call" | custom-call | flops 2000000000 | bytes 2000000 | tf_op jit(solution)/shard_map/pallas_call | solution.py:317
  74.5 0.1 reshape.208
  74.6 0.1 reshape.210
  75.0 6.3 %collective-permute-done = f32[256,256]{1,0:T(8,128)S(1)} collective-permute-done((f32[256,256]{1,0:T(8,128)}, f32[256,256]{1,0:T(8,128)S(1)}, u32[]{:S(2)}, u32[]{:S(2)}) %collective-permute-start) | collective-permute-done | bytes 262176 | tf_op jit(solution)/shard_map/ppermute | solution.py:280
  81.3 1.0 add.101
  82.2 1.5 collective-permute-start.1
  83.8 2.4 %slice.82 = bf16[2,4,2,16,2048]{4,3,2,1,0:T(8,128)(2,1)} slice(bf16[4,4,2,16,2048]{4,3,2,1,0:T(8,128)(2,1)} %collective-permute-done.11), slice={[0:2], [0:4], [0:2], [0:16], [0:2048]} | slice | bytes 2097152 | tf_op jit(solution)/shard_map/slice | solution.py:296
  86.1 2.3 %slice.83 = bf16[2,4,2,16,2048]{4,3,2,1,0:T(8,128)(2,1)} slice(bf16[4,4,2,16,2048]{4,3,2,1,0:T(8,128)(2,1)} %collective-permute-done.13), slice={[2:4], [0:4], [0:2], [0:16], [0:2048]} | slice | bytes 2097152 | tf_op jit(solution)/shard_map/slice | solution.py:297
  88.4 3.2 %collective-permute-start.17 = (bf16[2,4,2,16,2048]{4,3,2,1,0:T(8,128)(2,1)}, bf16[2,4,2,16,2048]{4,3,2,1,0:T(8,128)(2,1)}, u32[]{:S(2)}, u32[]{:S(2)}) collective-permute-start(bf16[2,4,2,16,2048]{4,3,2,1,0:T(8,128)(2,1)} %slice.83), channel_id=1, source_target_pairs={{0,65},{1,0},{2,67},{3,2},{4,69},{5,4},{6,71},{7,6},{8,56},{9,57},... | collective-permute-start | bytes 3145736 | tf_op jit(solution)/shard_map/ppermute | solution.py:259
  91.7 0.7 pad_add_fusion.table
  92.3 0.6 pad_add_fusion.1.table
  93.0 0.5 collective-permute-start.12
  93.5 7.1 %shard_map.86 = bf16[128,512,256]{2,1,0:T(8,128)(2,1)} custom-call(f32[512,128]{1,0:T(8,128)} %get-tuple-element.26.hi_ref, f32[512,128]{1,0:T(8,128)} %get-tuple-element.27.lo_ref, f32[512,128]{1,0:T(8,128)} %get-tuple-element.28.v_ref, bf16[128,512,256]{2,1,0:T(8,128)(2,1)} %shard_map.85.refs_0_), custom_call_target="tpu_custom_call", output_to_operand_aliasing={{}: (3, {})} | custom-call | flops 7520000000 | bytes 8388608 | tf_op jit(solution)/shard_map/pallas_call | solution.py:184
  100.6 1.7 add.102
  102.4 0.5 collective-permute-start.16
  102.9 2.2 %collective-permute-done.17 = bf16[2,4,2,16,2048]{4,3,2,1,0:T(8,128)(2,1)} collective-permute-done((bf16[2,4,2,16,2048]{4,3,2,1,0:T(8,128)(2,1)}, bf16[2,4,2,16,2048]{4,3,2,1,0:T(8,128)(2,1)}, u32[]{:S(2)}, u32[]{:S(2)}) %collective-permute-start.17) | collective-permute-done | bytes 1048608 | tf_op jit(solution)/shard_map/ppermute | solution.py:259
  105.1 16.0 %shard_map.88 = (f32[512,256]{1,0:T(8,128)}, f32[256,256]{1,0:T(8,128)}, f32[512,256]{1,0:T(8,128)}) custom-call(s32[130]{0:T(256)} %pad_add_fusion.table, s32[1]{0:T(128)} %get-tuple-element.25.count_ref, bf16[8,2,8,512,256]{4,3,2,1,0:T(8,128)(2,1)} %bitcast.70, bf16[128,512,256]{2,1,0:T(8,128)(2,1)} %shard_map.87.rest, bf16[16,2,16,2048]{3,2,1,0:T(8,128)(2,1)} %bitcast.73, ...), custom_call_target="tpu_custom_call" | custom-call | flops 15000000512 | bytes 30000000 | tf_op jit(solution)/shard_map/pallas_call | solution.py:488
  121.1 2.8 %collective-permute-start.2 = (f32[256,256]{1,0:T(8,128)S(1)}, f32[256,256]{1,0:T(8,128)S(1)}, u32[]{:S(2)}, u32[]{:S(2)}) collective-permute-start(f32[256,256]{1,0:T(8,128)S(1)} %copy-done.3), channel_id=1, source_target_pairs={{0,4},{1,5},{2,6},{3,7},{4,0},{5,1},{6,2},{7,3},{8,12},{9,13},{10,... | collective-permute-start | bytes 786440 | tf_op jit(solution)/shard_map/ppermute | solution.py:280
  123.9 18.1 %shard_map.89 = (f32[1024,256]{1,0:T(8,128)}, f32[256,256]{1,0:T(8,128)}) custom-call(s32[130]{0:T(256)} %pad_add_fusion.1.table, s32[1]{0:T(128)} %get-tuple-element.25.count_ref, bf16[8,2,8,512,256]{4,3,2,1,0:T(8,128)(2,1)} %bitcast.71, bf16[128,512,256]{2,1,0:T(8,128)(2,1)} %shard_map.87.rest, bf16[16,2,16,2048]{3,2,1,0:T(8,128)(2,1)} %collective-permute-done.10.p0, ...), custom_call_target="tpu_custom_call" | custom-call | flops 15000000512 | bytes 30000000 | tf_op jit(solution)/shard_map/pallas_call | solution.py:488
  142.0 3.7 %all-to-all-start.1 = ((f32[8,128,256]{2,1,0:T(8,128)}), f32[8,128,256]{2,1,0:T(8,128)S(1)}, u32[]{:S(2)}, u32[]{:S(2)}) async-start(f32[8,128,256]{2,1,0:T(8,128)} %bitcast.76), calls=%async_computation.1 | async-start | bytes 2097152 | tf_op jit(solution)/shard_map/all_to_all | solution.py:637
  145.8 9.8 %shard_map.90 = (f32[256,256]{1,0:T(8,128)S(1)}, s32[1]{0:T(128)}) custom-call(f32[256,256]{1,0:T(8,128)S(1)} %multiply_multiply_fusion.gram_ref), custom_call_target="tpu_custom_call" | custom-call | flops 5000000000 | bytes 600000 | tf_op jit(solution)/shard_map/pallas_call | solution.py:554
  156.3 0.3 conditional.1
  156.5 6.4 %all-to-all-done.1.spread_ref = f32[8,128,256]{2,1,0:T(8,128)S(1)} async-done(((f32[8,128,256]{2,1,0:T(8,128)}), f32[8,128,256]{2,1,0:T(8,128)S(1)}, u32[]{:S(2)}, u32[]{:S(2)}) %all-to-all-start.1) | async-done | bytes 1048608 | tf_op jit(solution)/shard_map/all_to_all | solution.py:637
  163.0 1.0 copy-done.2
  163.9 2.3 %shard_map.91 = f32[16,16,128]{2,1,0:T(8,128)} custom-call(f32[256,256]{1,0:T(8,128)S(1)} %get-tuple-element.127.inverse_ref, f32[8,128,256]{2,1,0:T(8,128)} %copy-done.2), custom_call_target="tpu_custom_call" | custom-call | flops 500000000 | bytes 1500000 | tf_op jit(solution)/shard_map/pallas_call | solution.py:583
  166.2 11.8 %all_to_all.20 = f32[16,16,128]{2,1,0:T(8,128)S(1)} all-to-all(f32[16,16,128]{2,1,0:T(8,128)} %shard_map.91), channel_id=1, replica_groups=mesh['rows'=16,'cols'=8] {'rows'}, dimensions={0} | all-to-all | bytes 262144 | tf_op jit(solution)/shard_map/all_to_all | solution.py:639
  178.0 8.8 %all_to_all.21 = f32[8,2,16,128]{3,2,1,0:T(8,128)S(1)} all-to-all(f32[8,2,16,128]{3,2,1,0:T(8,128)S(1)} %bitcast.77), channel_id=1, replica_groups=mesh['rows'=16,'cols'=8] {'cols'}, dimensions={0} | all-to-all | bytes 262144 | tf_op jit(solution)/shard_map/all_to_all | solution.py:642
  186.8 0.7 copy.17
  (48 shorter events, 0.9 us)
Async XLA Ops:
  0.9 10.7 %collective-permute-start.3 = (bf16[16,2048]{1,0:T(8,128)(2,1)S(1)}, bf16[16,2048]{1,0:T(8,128)(2,1)S(1)}, u32[]{:S(2)}, u32[]{:S(2)}) collective-permute-start(bf16[16,2048]{1,0:T(8,128)(2,1)S(1)} %get-tuple-element.66), channel_id=1, source_target_pairs={{0,8},{1,9},{2,10},{3,11},{4,12},{5,13},{6,14},{7,15},{8,0},{9,1},... | collective-permute-start | bytes 196616 | tf_op jit(solution)/shard_map/ppermute | solution.py:259
  3.0 68.3 %all-to-all-start = ((bf16[16,16,2048]{2,1,0:T(8,128)(2,1)}), bf16[16,16,2048]{2,1,0:T(8,128)(2,1)}, u32[]{:S(2)}, u32[]{:S(2)}) async-start(bf16[16,16,2048]{2,1,0:T(8,128)(2,1)} %broadcast_in_dim.68), calls=%async_computation | async-start | bytes 2097152 | tf_op jit(solution)/shard_map/all_to_all | solution.py:612
  11.6 16.2 %collective-permute-start.4 = (bf16[1,2,16,2048]{3,2,1,0:T(8,128)(2,1)S(1)}, bf16[1,2,16,2048]{3,2,1,0:T(8,128)(2,1)S(1)}, u32[]{:S(2)}, u32[]{:S(2)}) collective-permute-start(bf16[1,2,16,2048]{3,2,1,0:T(8,128)(2,1)S(1)} %maximum_select_fusion), channel_id=1, source_target_pairs={{0,16},{1,17},{2,18},{3,19},{4,20},{5,21},{6,22},{7,23},{8,10},{9,... | collective-permute-start | bytes 393224 | tf_op jit(solution)/shard_map/ppermute | solution.py:259
  13.6 14.3 %collective-permute-start.5 = (bf16[1,2,16,2048]{3,2,1,0:T(8,128)(2,1)S(1)}, bf16[1,2,16,2048]{3,2,1,0:T(8,128)(2,1)S(1)}, u32[]{:S(2)}, u32[]{:S(2)}) collective-permute-start(bf16[1,2,16,2048]{3,2,1,0:T(8,128)(2,1)S(1)} %maximum_select_fusion), channel_id=1, source_target_pairs={{0,48},{1,49},{2,50},{3,51},{4,52},{5,53},{6,54},{7,55},{8,14},{9,... | collective-permute-start | bytes 393224 | tf_op jit(solution)/shard_map/ppermute | solution.py:259
  15.0 14.6 %collective-permute-start.6 = (bf16[1,2,16,2048]{3,2,1,0:T(8,128)(2,1)S(1)}, bf16[1,2,16,2048]{3,2,1,0:T(8,128)(2,1)S(1)}, u32[]{:S(2)}, u32[]{:S(2)}) collective-permute-start(bf16[1,2,16,2048]{3,2,1,0:T(8,128)(2,1)S(1)} %maximum_select_fusion), channel_id=1, source_target_pairs={{0,32},{1,33},{2,34},{3,35},{4,36},{5,37},{6,38},{7,39},{8,12},{9,... | collective-permute-start | bytes 393224 | tf_op jit(solution)/shard_map/ppermute | solution.py:259
  29.6 12.4 %collective-permute-start.7 = (bf16[1,4,2,16,2048]{4,3,2,1,0:T(8,128)(2,1)S(1)}, bf16[1,4,2,16,2048]{4,3,2,1,0:T(8,128)(2,1)S(1)}, u32[]{:S(2)}, u32[]{:S(2)}) collective-permute-start(bf16[1,4,2,16,2048]{4,3,2,1,0:T(8,128)(2,1)S(1)} %maximum_bitcast_fusion), channel_id=1, source_target_pairs={{0,2},{1,3},{2,4},{3,5},{4,6},{5,7},{6,0},{7,1},{8,9},{9,72},{10,1... | collective-permute-start | bytes 1572872 | tf_op jit(solution)/shard_map/ppermute | solution.py:259
  31.3 10.7 %collective-permute-start.8 = (bf16[1,4,2,16,2048]{4,3,2,1,0:T(8,128)(2,1)S(1)}, bf16[1,4,2,16,2048]{4,3,2,1,0:T(8,128)(2,1)S(1)}, u32[]{:S(2)}, u32[]{:S(2)}) collective-permute-start(bf16[1,4,2,16,2048]{4,3,2,1,0:T(8,128)(2,1)S(1)} %maximum_bitcast_fusion), channel_id=1, source_target_pairs={{0,6},{1,7},{2,0},{3,1},{4,2},{5,3},{6,4},{7,5},{8,73},{9,8},{10,7... | collective-permute-start | bytes 1572872 | tf_op jit(solution)/shard_map/ppermute | solution.py:259
  32.9 14.1 %collective-permute-start.9 = (bf16[1,4,2,16,2048]{4,3,2,1,0:T(8,128)(2,1)S(1)}, bf16[1,4,2,16,2048]{4,3,2,1,0:T(8,128)(2,1)}, u32[]{:S(2)}, u32[]{:S(2)}) collective-permute-start(bf16[1,4,2,16,2048]{4,3,2,1,0:T(8,128)(2,1)S(1)} %maximum_bitcast_fusion), channel_id=1, source_target_pairs={{0,4},{1,5},{2,6},{3,7},{4,0},{5,1},{6,2},{7,3},{8,72},{9,73},{10,... | collective-permute-start | bytes 1572872 | tf_op jit(solution)/shard_map/ppermute | solution.py:259
  42.0 0.8 copy-start.4
  48.5 44.5 %copy-start = (bf16[4,4,2,16,2048]{4,3,2,1,0:T(8,128)(2,1)}, bf16[4,4,2,16,2048]{4,3,2,1,0:T(8,128)(2,1)S(1)}, u32[]{:S(2)}) copy-start(bf16[4,4,2,16,2048]{4,3,2,1,0:T(8,128)(2,1)S(1)} %pad_maximum_fusion.1) | copy-start | bytes 6291460
  48.5 35.2 %collective-permute-start.11 = (bf16[4,4,2,16,2048]{4,3,2,1,0:T(8,128)(2,1)S(1)}, bf16[4,4,2,16,2048]{4,3,2,1,0:T(8,128)(2,1)}, u32[]{:S(2)}, u32[]{:S(2)}) collective-permute-start(bf16[4,4,2,16,2048]{4,3,2,1,0:T(8,128)(2,1)S(1)} %pad_maximum_fusion.1), channel_id=1, source_target_pairs={{0,1},{1,64},{2,3},{3,66},{4,5},{5,68},{6,7},{7,70},{8,24},{9,25},... | collective-permute-start | bytes 6291464 | tf_op jit(solution)/shard_map/ppermute | solution.py:259
  49.6 36.5 %collective-permute-start.13 = (bf16[4,4,2,16,2048]{4,3,2,1,0:T(8,128)(2,1)S(1)}, bf16[4,4,2,16,2048]{4,3,2,1,0:T(8,128)(2,1)}, u32[]{:S(2)}, u32[]{:S(2)}) collective-permute-start(bf16[4,4,2,16,2048]{4,3,2,1,0:T(8,128)(2,1)S(1)} %pad_maximum_fusion.1), channel_id=1, source_target_pairs={{0,65},{1,0},{2,67},{3,2},{4,69},{5,4},{6,71},{7,6},{8,56},{9,57},... | collective-permute-start | bytes 6291464 | tf_op jit(solution)/shard_map/ppermute | solution.py:259
  74.3 7.0 %collective-permute-start = (f32[256,256]{1,0:T(8,128)}, f32[256,256]{1,0:T(8,128)S(1)}, u32[]{:S(2)}, u32[]{:S(2)}) collective-permute-start(f32[256,256]{1,0:T(8,128)} %get-tuple-element.24), channel_id=1, source_target_pairs={{0,1},{1,0},{2,3},{3,2},{4,5},{5,4},{6,7},{7,6},{8,9},{9,8},{10,11... | collective-permute-start | bytes 786440 | tf_op jit(solution)/shard_map/ppermute | solution.py:280
  82.2 11.3 %collective-permute-start.1 = (f32[256,256]{1,0:T(8,128)S(1)}, f32[256,256]{1,0:T(8,128)}, u32[]{:S(2)}, u32[]{:S(2)}) collective-permute-start(f32[256,256]{1,0:T(8,128)S(1)} %add.101), channel_id=1, source_target_pairs={{0,2},{1,3},{2,0},{3,1},{4,6},{5,7},{6,4},{7,5},{8,10},{9,11},{10,... | collective-permute-start | bytes 786440 | tf_op jit(solution)/shard_map/ppermute | solution.py:280
  86.1 16.2 %collective-permute-start.15 = (bf16[2,4,2,16,2048]{4,3,2,1,0:T(8,128)(2,1)}, bf16[2,4,2,16,2048]{4,3,2,1,0:T(8,128)(2,1)S(1)}, u32[]{:S(2)}, u32[]{:S(2)}) collective-permute-start(bf16[2,4,2,16,2048]{4,3,2,1,0:T(8,128)(2,1)} %slice.82), channel_id=1, source_target_pairs={{0,1},{1,64},{2,3},{3,66},{4,5},{5,68},{6,7},{7,70},{8,24},{9,25},... | collective-permute-start | bytes 3145736 | tf_op jit(solution)/shard_map/ppermute | solution.py:259
  88.4 16.6 %collective-permute-start.17 = (bf16[2,4,2,16,2048]{4,3,2,1,0:T(8,128)(2,1)}, bf16[2,4,2,16,2048]{4,3,2,1,0:T(8,128)(2,1)}, u32[]{:S(2)}, u32[]{:S(2)}) collective-permute-start(bf16[2,4,2,16,2048]{4,3,2,1,0:T(8,128)(2,1)} %slice.83), channel_id=1, source_target_pairs={{0,65},{1,0},{2,67},{3,2},{4,69},{5,4},{6,71},{7,6},{8,56},{9,57},... | collective-permute-start | bytes 3145736 | tf_op jit(solution)/shard_map/ppermute | solution.py:259
  93.0 28.0 %collective-permute-start.10 = (bf16[16,2,16,2048]{3,2,1,0:T(8,128)(2,1)S(1)}, bf16[16,2,16,2048]{3,2,1,0:T(8,128)(2,1)}, u32[]{:S(2)}, u32[]{:S(2)}) collective-permute-start(bf16[16,2,16,2048]{3,2,1,0:T(8,128)(2,1)S(1)} %bitcast.72), channel_id=1, source_target_pairs={{0,8},{1,9},{2,10},{3,11},{4,12},{5,13},{6,14},{7,15},{8,0},{9,1},... | collective-permute-start | bytes 6291464 | tf_op jit(solution)/shard_map/ppermute | solution.py:259
  93.0 30.9 %collective-permute-start.12 = (bf16[16,2,16,2048]{3,2,1,0:T(8,128)(2,1)}, bf16[16,2,16,2048]{3,2,1,0:T(8,128)(2,1)}, u32[]{:S(2)}, u32[]{:S(2)}) collective-permute-start(bf16[16,2,16,2048]{3,2,1,0:T(8,128)(2,1)} %bitcast.19.p1), channel_id=1, source_target_pairs={{0,8},{1,9},{2,10},{3,11},{4,12},{5,13},{6,14},{7,15},{8,0},{9,1},... | collective-permute-start | bytes 6291464 | tf_op jit(solution)/shard_map/ppermute | solution.py:259
  93.5 30.4 %collective-permute-start.14 = (bf16[16,2,16,2048]{3,2,1,0:T(8,128)(2,1)}, bf16[16,2,16,2048]{3,2,1,0:T(8,128)(2,1)}, u32[]{:S(2)}, u32[]{:S(2)}) collective-permute-start(bf16[16,2,16,2048]{3,2,1,0:T(8,128)(2,1)} %bitcast.20.p2), channel_id=1, source_target_pairs={{0,8},{1,9},{2,10},{3,11},{4,12},{5,13},{6,14},{7,15},{8,0},{9,1},... | collective-permute-start | bytes 6291464 | tf_op jit(solution)/shard_map/ppermute | solution.py:259
  102.4 2.7 %copy-start.1 = (bf16[2,4,2,16,2048]{4,3,2,1,0:T(8,128)(2,1)}, bf16[2,4,2,16,2048]{4,3,2,1,0:T(8,128)(2,1)S(1)}, u32[]{:S(2)}) copy-start(bf16[2,4,2,16,2048]{4,3,2,1,0:T(8,128)(2,1)S(1)} %collective-permute-done.15) | copy-start | bytes 3145732
  102.4 21.5 %collective-permute-start.16 = (bf16[8,2,16,2048]{3,2,1,0:T(8,128)(2,1)S(1)}, bf16[8,2,16,2048]{3,2,1,0:T(8,128)(2,1)}, u32[]{:S(2)}, u32[]{:S(2)}) collective-permute-start(bf16[8,2,16,2048]{3,2,1,0:T(8,128)(2,1)S(1)} %bitcast.74), channel_id=1, source_target_pairs={{0,8},{1,9},{2,10},{3,11},{4,12},{5,13},{6,14},{7,15},{8,0},{9,1},... | collective-permute-start | bytes 3145736 | tf_op jit(solution)/shard_map/ppermute | solution.py:259
  105.0 18.8 %collective-permute-start.18 = (bf16[8,2,16,2048]{3,2,1,0:T(8,128)(2,1)}, bf16[8,2,16,2048]{3,2,1,0:T(8,128)(2,1)}, u32[]{:S(2)}, u32[]{:S(2)}) collective-permute-start(bf16[8,2,16,2048]{3,2,1,0:T(8,128)(2,1)} %bitcast.22.p4), channel_id=1, source_target_pairs={{0,8},{1,9},{2,10},{3,11},{4,12},{5,13},{6,14},{7,15},{8,0},{9,1},... | collective-permute-start | bytes 3145736 | tf_op jit(solution)/shard_map/ppermute | solution.py:259
  105.1 16.0 %copy-start.3 = (f32[256,256]{1,0:T(8,128)S(1)}, f32[256,256]{1,0:T(8,128)}, u32[]{:S(2)}) copy-start(f32[256,256]{1,0:T(8,128)} %add.102) | copy-start | bytes 786436
  121.1 24.7 %collective-permute-start.2 = (f32[256,256]{1,0:T(8,128)S(1)}, f32[256,256]{1,0:T(8,128)S(1)}, u32[]{:S(2)}, u32[]{:S(2)}) collective-permute-start(f32[256,256]{1,0:T(8,128)S(1)} %copy-done.3), channel_id=1, source_target_pairs={{0,4},{1,5},{2,6},{3,7},{4,0},{5,1},{6,2},{7,3},{8,12},{9,13},{10,... | collective-permute-start | bytes 786440 | tf_op jit(solution)/shard_map/ppermute | solution.py:280
  142.0 3.7 %copy-start.5 = (f32[256,256]{1,0:T(8,128)S(1)}, f32[256,256]{1,0:T(8,128)}, u32[]{:S(2)}) copy-start(f32[256,256]{1,0:T(8,128)} %get-tuple-element.34) | copy-start | bytes 786436
  142.0 20.9 %all-to-all-start.1 = ((f32[8,128,256]{2,1,0:T(8,128)}), f32[8,128,256]{2,1,0:T(8,128)S(1)}, u32[]{:S(2)}, u32[]{:S(2)}) async-start(f32[8,128,256]{2,1,0:T(8,128)} %bitcast.76), calls=%async_computation.1 | async-start | bytes 2097152 | tf_op jit(solution)/shard_map/all_to_all | solution.py:637
  163.0 1.0 copy-start.2
